TPU v7x, 128 devices: a whole 4x4x4 slice. The times are simulated.
128 devices in a mesh: rep: 4 (over z), ep: 4 (over y), dp: 8 (over x, core).
Axes of the slice: x: 4, y: 4, z: 4, core: 2. Of those that a mesh axis runs over, the one named last changes fastest.
Arguments:
- tok_in: bfloat16 [131072, 384], P(('rep', 'ep', 'dp'))
- tok_grad: bfloat16 [131072, 384], P(('rep', 'ep', 'dp'))
- route_ids: int32 [2, 131072, 2], P(None, ('rep', 'ep', 'dp'))
- gate_vals: float32 [2, 131072, 2], P(None, ('rep', 'ep', 'dp'))
- w_dense: bfloat16 [2, 384, 384], replicated
- w_gate: bfloat16 [2, 8, 384, 1024], P(None, 'ep')
- w_up: bfloat16 [2, 8, 384, 1024], P(None, 'ep')
- w_down: bfloat16 [2, 8, 1024, 384], P(None, 'ep')
Outputs:
- output 1: bfloat16 [131072, 384], P(('rep', 'ep', 'dp'))
- output 2: bfloat16 [131072, 384], P(('rep', 'ep', 'dp'))
- output 3: bfloat16 [2, 384, 384], replicated
- output 4: bfloat16 [2, 8, 384, 1024], P(None, 'ep')
- output 5: bfloat16 [2, 8, 384, 1024], P(None, 'ep')
- output 6: bfloat16 [2, 8, 1024, 384], P(None, 'ep')
All inputs are finite; a program needn't handle non-finite values.
Results may differ from a plain program's by a relative error of at most 0.02.
Values are sent between devices in bfloat16 or wider.
A program may use at most 1 GiB of HBM per device.

v0:
```python
import jax
import jax.numpy as jnp
from jax import lax
from jax.sharding import PartitionSpec as P

TOK_AXES = ("rep", "ep", "dp")


def slot_tables(route_loc, experts):
    tokens, top_k = route_loc.shape
    capacity = 2 * tokens * top_k // experts
    flat_ids = route_loc.reshape(tokens * top_k)
    expert_hits = (flat_ids[:, None] == jnp.arange(experts, dtype=jnp.int32)[None, :]).astype(jnp.int32)
    slot_rank = jnp.sum((jnp.cumsum(expert_hits, axis=0) - 1) * expert_hits, axis=1)
    slot_of = flat_ids * capacity + slot_rank
    copy_of = jnp.full((experts * capacity,), tokens * top_k, jnp.int32)
    copy_of = copy_of.at[slot_of].set(jnp.arange(tokens * top_k, dtype=jnp.int32))
    return slot_of, copy_of


def layer_forward(tok_loc, route_loc, gate_loc, dense_w, gate_w, up_w, down_w, ep_size):
    tokens, top_k = route_loc.shape
    model_width = tok_loc.shape[1]
    experts = gate_w.shape[0] * ep_size
    capacity = 2 * tokens * top_k // experts
    mixed_val = (tok_loc.astype(jnp.float32) + jnp.dot(tok_loc, dense_w, preferred_element_type=jnp.float32)).astype(jnp.bfloat16)
    slot_of, copy_of = slot_tables(route_loc, experts)
    padded = jnp.concatenate([mixed_val, jnp.zeros((1, model_width), jnp.bfloat16)], axis=0)
    send_buf = jnp.take(padded, copy_of // top_k, axis=0).reshape(experts, capacity, model_width)
    expert_in = lax.all_to_all(send_buf, "ep", 0, 1, tiled=True)
    act_gate = jnp.einsum("end,edf->enf", expert_in, gate_w, preferred_element_type=jnp.float32).astype(jnp.bfloat16)
    act_up = jnp.einsum("end,edf->enf", expert_in, up_w, preferred_element_type=jnp.float32).astype(jnp.bfloat16)
    hidden = (jax.nn.silu(act_gate.astype(jnp.float32)) * act_up.astype(jnp.float32)).astype(jnp.bfloat16)
    expert_out = jnp.einsum("enf,efd->end", hidden, down_w, preferred_element_type=jnp.float32).astype(jnp.bfloat16)
    returned = lax.all_to_all(expert_out, "ep", 1, 0, tiled=True).reshape(experts * capacity, model_width)
    per_copy = jnp.take(returned, slot_of, axis=0).reshape(tokens, top_k, model_width)
    mix_sum = jnp.sum(gate_loc[:, :, None] * per_copy, axis=1)
    tok_out = (mixed_val.astype(jnp.float32) + mix_sum).astype(jnp.bfloat16)
    return tok_out, (tok_loc, slot_of, copy_of, expert_in, act_gate, act_up, hidden)


def layer_backward(grad_out, gate_loc, dense_w, gate_w, up_w, down_w, layer_saved, ep_size):
    tok_loc, slot_of, copy_of, expert_in, act_gate, act_up, hidden = layer_saved
    tokens, top_k = gate_loc.shape
    model_width = grad_out.shape[1]
    experts = gate_w.shape[0] * ep_size
    capacity = copy_of.shape[0] // experts
    gate_pad = jnp.concatenate([gate_loc.reshape(tokens * top_k), jnp.zeros((1,), jnp.float32)])
    grad_pad = jnp.concatenate([grad_out, jnp.zeros((1, model_width), jnp.bfloat16)], axis=0)
    slot_gate = jnp.take(gate_pad, copy_of)
    send_grad = (slot_gate[:, None] * jnp.take(grad_pad, copy_of // top_k, axis=0)).astype(jnp.bfloat16).reshape(experts, capacity, model_width)
    grad_exp_out = lax.all_to_all(send_grad, "ep", 0, 1, tiled=True)
    grad_hidden = jnp.einsum("end,efd->enf", grad_exp_out, down_w, preferred_element_type=jnp.float32)
    grad_down = jnp.einsum("enf,end->efd", hidden, grad_exp_out, preferred_element_type=jnp.float32)
    gate_f = act_gate.astype(jnp.float32)
    sig_gate = jax.nn.sigmoid(gate_f)
    grad_up_act = (grad_hidden * gate_f * sig_gate).astype(jnp.bfloat16)
    grad_gate_act = (grad_hidden * act_up.astype(jnp.float32) * sig_gate * (1.0 + gate_f * (1.0 - sig_gate))).astype(jnp.bfloat16)
    grad_gate = jnp.einsum("end,enf->edf", expert_in, grad_gate_act, preferred_element_type=jnp.float32)
    grad_up = jnp.einsum("end,enf->edf", expert_in, grad_up_act, preferred_element_type=jnp.float32)
    grad_exp_in = (jnp.einsum("enf,edf->end", grad_gate_act, gate_w, preferred_element_type=jnp.float32) + jnp.einsum("enf,edf->end", grad_up_act, up_w, preferred_element_type=jnp.float32)).astype(jnp.bfloat16)
    grad_back = lax.all_to_all(grad_exp_in, "ep", 1, 0, tiled=True).reshape(experts * capacity, model_width)
    grad_mixed = grad_out.astype(jnp.float32) + jnp.sum(jnp.take(grad_back, slot_of, axis=0).reshape(tokens, top_k, model_width), axis=1, dtype=jnp.float32)
    grad_mixed_bf = grad_mixed.astype(jnp.bfloat16)
    grad_dense = lax.dot_general(tok_loc, grad_mixed_bf, (((0,), (0,)), ((), ())), preferred_element_type=jnp.float32)
    grad_tok = (grad_mixed + lax.dot_general(grad_mixed_bf, dense_w, (((1,), (1,)), ((), ())), preferred_element_type=jnp.float32)).astype(jnp.bfloat16)
    return grad_tok, grad_dense, grad_gate, grad_up, grad_down


def solution(mesh):
    ep_size = mesh.shape["ep"]
    tok_spec = P(TOK_AXES, None)
    route_spec = P(None, TOK_AXES, None)
    expert_spec = P(None, "ep", None, None)
    whole_spec = P(None, None, None)

    def device_step(tok_in, tok_grad, route_ids, gate_vals, w_dense, w_gate, w_up, w_down):
        layers = w_dense.shape[0]
        current = tok_in
        saved_all = []
        for layer_idx in range(layers):
            current, layer_saved = layer_forward(current, route_ids[layer_idx], gate_vals[layer_idx], w_dense[layer_idx], w_gate[layer_idx], w_up[layer_idx], w_down[layer_idx], ep_size)
            saved_all.append(layer_saved)
        grad_cur = tok_grad
        dense_sums = []
        gate_sums = []
        up_sums = []
        down_sums = []
        for layer_idx in reversed(range(layers)):
            grad_cur, grad_dense, grad_gate, grad_up, grad_down = layer_backward(grad_cur, gate_vals[layer_idx], w_dense[layer_idx], w_gate[layer_idx], w_up[layer_idx], w_down[layer_idx], saved_all[layer_idx], ep_size)
            dense_sums.insert(0, lax.psum(grad_dense.astype(jnp.bfloat16), TOK_AXES))
            gate_sums.insert(0, lax.psum(lax.psum(grad_gate.astype(jnp.bfloat16), "rep"), "dp"))
            up_sums.insert(0, lax.psum(lax.psum(grad_up.astype(jnp.bfloat16), "rep"), "dp"))
            down_sums.insert(0, lax.psum(lax.psum(grad_down.astype(jnp.bfloat16), "rep"), "dp"))
        return current, grad_cur, jnp.stack(dense_sums), jnp.stack(gate_sums), jnp.stack(up_sums), jnp.stack(down_sums)

    return jax.shard_map(device_step, mesh=mesh, in_specs=(tok_spec, tok_spec, route_spec, route_spec, whole_spec, expert_spec, expert_spec, expert_spec), out_specs=(tok_spec, tok_spec, whole_spec, expert_spec, expert_spec, expert_spec), check_vma=False)
```

profile of v0, /device:TPU:1, one launch (start us, length us, event | category | flops | bytes accessed | tf_op | source)
XLA Modules:
  0.0 1078.6 jit_solution(2029944057224555122)
XLA Ops:
  22.6 17.1 %gather_fusion = bf16[4096,384]{1,0:T(8,128)(2,1)} fusion(bf16[1025,384]{1,0:T(8,128)(2,1)S(1)} %concatenate.18, s32[4096]{0:T(1024)S(1)} %get-tuple-element.47), kind=kCustom, calls=%fused_computation.clone | custom fusion | bytes 6307840 | tf_op jit(solution)/shard_map/jit(_take)/gather | solution.py:29
  57.3 27.5 %all-to-all-done = bf16[8,512,384]{2,1,0:T(8,128)(2,1)S(1)} async-done(((bf16[8,512,384]{2,1,0:T(8,128)(2,1)}), bf16[8,512,384]{2,1,0:T(8,128)(2,1)S(1)}, u32[]{:S(2)}, u32[]{:S(2)}) %all-to-all-start) | async-done | bytes 3145760 | tf_op jit(solution)/shard_map/all_to_all | solution.py:30
  94.5 12.9 %fusion = (bf16[2,2048,1024]{2,1,0:T(8,128)(2,1)}, bf16[2,2048,1024]{2,1,0:T(8,128)(2,1)}) fusion(bf16[2,2048,1024]{2,1,0:T(8,128)(2,1)} %convolution_convert_fusion.3, bf16[2,2048,384]{2,1,0:T(8,128)(2,1)S(1)} %bitcast.173, bf16[2,2,384,1024]{3,2,1,0:T(8,128)(2,1)S(1)} %copy-done.49), kind=kOutput, calls=%fused_computation.24 | convolution fusion | flops 3258974208 | bytes 29884416 | tf_op jit(solution)/shard_map/end,edf->enf/dot_general | solution.py:32
  115.7 28.6 %copy.59 = bf16[2,2048,384]{2,0,1:T(2,128)(2,1)} copy(bf16[2,2048,384]{2,1,0:T(8,128)(2,1)S(1)} %convolution_convert_fusion.5) | data formatting | bytes 6291456 | tf_op jit(solution)/shard_map/convert_element_type | solution.py:34
  160.0 23.0 %gather_fusion.4 = f32[4096]{0:T(1024)S(1)} fusion(f32[2049]{0:T(1024)S(1)} %get-tuple-element.63, s32[4096]{0:T(1024)S(1)} %get-tuple-element.52), kind=kCustom, calls=%fused_computation.2.clone | custom fusion | bytes 49152 | tf_op jit(solution)/shard_map/jit(_take)/gather | solution.py:50
  183.1 17.1 %gather_fusion.5 = bf16[4096,384]{1,0:T(8,128)(2,1)} fusion(bf16[1025,384]{1,0:T(8,128)(2,1)S(1)} %concatenate.21, s32[4096]{0:T(1024)S(1)} %get-tuple-element.53), kind=kCustom, calls=%fused_computation.4.clone | custom fusion | bytes 6307840 | tf_op jit(solution)/shard_map/jit(_take)/gather | solution.py:51
  229.1 17.4 %multiply_reduce_fusion.1 = f32[1024,384]{1,0:T(8,128)S(1)} fusion(f32[1024,2,384]{2,1,0:T(2,128)S(1)} %reshape.175, f32[1024,2]{1,0:T(8,128)} %copy.54), kind=kLoop, calls=%fused_computation.58 | loop fusion | flops 1179648 | bytes 4726784 | tf_op jit(solution)/shard_map/reduce_sum | solution.py:37
  249.2 17.1 %gather_fusion.2 = bf16[4096,384]{1,0:T(8,128)(2,1)} fusion(bf16[1025,384]{1,0:T(8,128)(2,1)S(1)} %concatenate.19, s32[4096]{0:T(1024)S(1)} %get-tuple-element.53), kind=kCustom, calls=%fused_computation.3.clone | custom fusion | bytes 6307840 | tf_op jit(solution)/shard_map/jit(_take)/gather | solution.py:29
  278.0 30.9 %all-to-all-done.2 = bf16[8,512,384]{2,1,0:T(8,128)(2,1)S(1)} async-done(((bf16[8,512,384]{2,1,0:T(8,128)(2,1)}), bf16[8,512,384]{2,1,0:T(8,128)(2,1)S(1)}, u32[]{:S(2)}, u32[]{:S(2)}) %all-to-all-start.2) | async-done | bytes 3145760 | tf_op jit(solution)/shard_map/all_to_all | solution.py:30
  325.5 19.6 %fusion.19 = (bf16[2,2048,1024]{2,1,0:T(8,128)(2,1)}, bf16[2,2048,1024]{2,1,0:T(8,128)(2,1)}, bf16[2,2048,1024]{2,1,0:T(8,128)(2,1)}) fusion(bf16[2,2048,1024]{2,1,0:T(8,128)(2,1)} %convolution_convert_fusion.1, bf16[2,2048,1024]{2,1,0:T(8,128)(2,1)} %convolution_convert_fusion, bf16[2,2048,384]{2,1,0:T(8,128)(2,1)S(1)} %bitcast.177, ...), kind=kOutput, calls=%fused_computation.43 | convolution fusion | flops 3296722944 | bytes 46661632 | tf_op jit(solution)/shard_map/end,efd->enf/dot_general | solution.py:53
  361.4 28.6 %copy.70 = bf16[2,2048,384]{2,0,1:T(2,128)(2,1)} copy(bf16[2,2048,384]{2,1,0:T(8,128)(2,1)S(1)} %add_convert_fusion.1) | data formatting | bytes 6291456 | tf_op jit(solution)/shard_map/convert_element_type | solution.py:61
  402.0 28.4 %copy.66 = bf16[2,2048,384]{2,0,1:T(2,128)(2,1)} copy(bf16[2,2048,384]{2,1,0:T(8,128)(2,1)S(1)} %convolution_convert_fusion.4) | data formatting | bytes 6291456 | tf_op jit(solution)/shard_map/convert_element_type | solution.py:34
  437.2 23.0 %gather_fusion.7 = f32[4096]{0:T(1024)S(1)} fusion(f32[2049]{0:T(1024)S(1)} %get-tuple-element.62, s32[4096]{0:T(1024)S(1)} %copy-done.38), kind=kCustom, calls=%fused_computation.9.clone | custom fusion | bytes 49152 | tf_op jit(solution)/shard_map/jit(_take)/gather | solution.py:50
  483.8 11.1 %gather_fusion.3 = bf16[2048,384]{1,0:T(8,128)(2,1)} fusion(bf16[4096,384]{1,0:T(8,128)(2,1)} %bitcast.161, s32[2048]{0:T(1024)S(1)} %broadcast_clamp_fusion.2), kind=kCustom, calls=%fused_computation.6.clone | custom fusion | bytes 3153920 | tf_op jit(solution)/shard_map/jit(_take)/gather | solution.py:36
  509.8 17.1 %gather_fusion.8 = bf16[4096,384]{1,0:T(8,128)(2,1)} fusion(bf16[1025,384]{1,0:T(8,128)(2,1)S(1)} %concatenate.23, s32[4096]{0:T(1024)S(1)} %copy-done.31), kind=kCustom, calls=%fused_computation.5.clone | custom fusion | bytes 6307840 | tf_op jit(solution)/shard_map/jit(_take)/gather | solution.py:51
  536.4 10.2 convolution_convert_fusion.6
  569.0 10.6 convolution_convert_fusion.7
  579.7 18.9 %fusion.13 = (bf16[2,2048,1024]{2,1,0:T(8,128)(2,1)}, bf16[2,2048,1024]{2,1,0:T(8,128)(2,1)}) fusion(bf16[2,2048,1024]{2,1,0:T(8,128)(2,1)} %convolution_convert_fusion.3, bf16[2,2048,1024]{2,1,0:T(8,128)(2,1)} %get-tuple-element.61, bf16[2,2048,384]{2,1,0:T(8,128)(2,1)} %bitcast.183, bf16[2,2,1024,384]{3,2,1,0:T(8,128)(2,1)} %param.21), kind=kOutput, calls=%fused_computation.37 | convolution fusion | flops 3284140032 | bytes 38273024 | tf_op jit(solution)/shard_map/end,efd->enf/dot_general | solution.py:53
  629.5 28.4 %copy.74 = bf16[2,2048,384]{2,0,1:T(2,128)(2,1)} copy(bf16[2,2048,384]{2,1,0:T(8,128)(2,1)S(1)} %add_convert_fusion) | data formatting | bytes 6291456 | tf_op jit(solution)/shard_map/convert_element_type | solution.py:61
  665.3 27.7 %all-to-all-done.7 = bf16[2,2048,384]{2,0,1:T(2,128)(2,1)S(1)} async-done(((bf16[2,2048,384]{2,0,1:T(2,128)(2,1)}), bf16[2,2048,384]{2,0,1:T(2,128)(2,1)S(1)}, u32[]{:S(2)}, u32[]{:S(2)}) %all-to-all-start.7) | async-done | bytes 3145760 | tf_op jit(solution)/shard_map/all_to_all | solution.py:62
  718.2 76.1 %all-reduce.15.cloned.1.call-done = (bf16[2,384,1024]{2,1,0:T(8,128)(2,1)}, bf16[2,384,1024]{2,1,0:T(8,128)(2,1)}, bf16[2,384,1024]{2,1,0:T(8,128)(2,1)}, bf16[2...) async-done(((bf16[2,384,1024]{2,1,0:T(8,128)(2,1)}, bf16[2,384,1024]{2,1,0:T(8,128)(2,1)}, bf16[2,384,1024]{2,1,0:T(8,128)(2,1)}, ...) | async-done | bytes 9437200 | tf_op jit(solution)/shard_map/psum | solution.py:92
  799.6 17.8 %multiply_reduce_fusion = f32[1024,384]{1,0:T(8,128)S(1)} fusion(f32[1024,2,384]{2,1,0:T(2,128)} %reshape.176, f32[1024,2]{1,0:T(8,128)} %copy.61), kind=kLoop, calls=%fused_computation.57 | loop fusion | flops 1179648 | bytes 4726784 | tf_op jit(solution)/shard_map/reduce_sum | solution.py:37
  820.0 128.1 %all-reduce.11.cloned.1.call-done = (bf16[1,384,384]{1,2,0:T(8,128)(2,1)}, bf16[1,384,384]{1,2,0:T(8,128)(2,1)}) async-done(((bf16[1,384,384]{1,2,0:T(8,128)(2,1)}, bf16[1,384,384]{1,2,0:T(8,128)(2,1)}), (bf16[1,384,384]{1,2,0:T(8,128)(2,1)}, bf16[1,384,384]{1,2,0:T(8,128)(2,1)})) %all-reduce.11.cloned.1.call-update) | async-done | bytes 589840 | tf_op jit(solution)/shard_map/psum | solution.py:91
  950.2 112.6 %all-reduce.13.cloned.1.call-done = (bf16[1,2,384,1024]{3,2,1,0:T(8,128)(2,1)}, bf16[1,2,384,1024]{3,2,1,0:T(8,128)(2,1)}, bf16[1,2,384,1024]{3,2,1,0:T(8,128)(2...) async-done(((bf16[1,2,384,1024]{3,2,1,0:T(8,128)(2,1)}, bf16[1,2,384,1024]{3,2,1,0:T(8,128)(2,1)}, ...) | async-done | bytes 9437200 | tf_op jit(solution)/shard_map/psum | solution.py:92
  (235 shorter events, 314.0 us)
Async XLA Ops:
  20.4 19.3 %copy-start.39 = (pred[4096]{0:T(1024)(128)(4,1)}, pred[4096]{0:T(1024)(128)(4,1)S(1)}, u32[]{:S(2)}) copy-start(pred[4096]{0:T(1024)(128)(4,1)S(1)} %compare_and_fusion.1) | copy-start | bytes 12292
  21.0 18.7 %copy-start.30 = (s32[4096]{0:T(1024)}, s32[4096]{0:T(1024)S(1)}, u32[]{:S(2)}) copy-start(s32[4096]{0:T(1024)S(1)} %get-tuple-element.47) | copy-start | bytes 49156
  43.2 41.7 %all-to-all-start = ((bf16[8,512,384]{2,1,0:T(8,128)(2,1)}), bf16[8,512,384]{2,1,0:T(8,128)(2,1)S(1)}, u32[]{:S(2)}, u32[]{:S(2)}) async-start(bf16[8,512,384]{2,1,0:T(8,128)(2,1)} %bitcast.169), calls=%async_computation | async-start | bytes 6291456 | tf_op jit(solution)/shard_map/all_to_all | solution.py:30
  50.7 34.5 %copy-start.32 = (s32[2048]{0:T(1024)}, s32[2048]{0:T(1024)S(1)}, u32[]{:S(2)}) copy-start(s32[2048]{0:T(1024)S(1)} %eq.58) | copy-start | bytes 24580
  57.3 27.9 %copy-start.34 = (s32[2048]{0:T(1024)}, s32[2048]{0:T(1024)S(1)}, u32[]{:S(2)}) copy-start(s32[2048]{0:T(1024)S(1)} %fusion.65) | copy-start | bytes 24580
  144.4 61.4 %all-to-all-start.1 = ((bf16[2,2048,384]{2,0,1:T(2,128)(2,1)}), bf16[2,2048,384]{2,0,1:T(2,128)(2,1)}, u32[]{:S(2)}, u32[]{:S(2)}) async-start(bf16[2,2048,384]{2,0,1:T(2,128)(2,1)} %copy.59), calls=%async_computation.1 | async-start | bytes 6291456 | tf_op jit(solution)/shard_map/all_to_all | solution.py:35
  200.2 22.1 %copy-start.42 = (pred[2048]{0:T(1024)(128)(4,1)}, pred[2048]{0:T(1024)(128)(4,1)S(1)}, u32[]{:S(2)}) copy-start(pred[2048]{0:T(1024)(128)(4,1)S(1)} %compare_and_fusion.3) | copy-start | bytes 6148
  205.8 64.0 %all-to-all-start.4 = ((bf16[8,512,384]{2,1,0:T(8,128)(2,1)}), bf16[8,512,384]{2,1,0:T(8,128)(2,1)}, u32[]{:S(2)}, u32[]{:S(2)}) async-start(bf16[8,512,384]{2,1,0:T(8,128)(2,1)} %bitcast.30), calls=%async_computation.4 | async-start | bytes 6291456 | tf_op jit(solution)/shard_map/all_to_all | solution.py:52
  269.8 39.1 %all-to-all-start.2 = ((bf16[8,512,384]{2,1,0:T(8,128)(2,1)}), bf16[8,512,384]{2,1,0:T(8,128)(2,1)S(1)}, u32[]{:S(2)}, u32[]{:S(2)}) async-start(bf16[8,512,384]{2,1,0:T(8,128)(2,1)} %bitcast.171), calls=%async_computation.2 | async-start | bytes 6291456 | tf_op jit(solution)/shard_map/all_to_all | solution.py:30
  390.0 40.4 %all-to-all-start.5 = ((bf16[2,2048,384]{2,0,1:T(2,128)(2,1)}), bf16[2,2048,384]{2,0,1:T(2,128)(2,1)S(1)}, u32[]{:S(2)}, u32[]{:S(2)}) async-start(bf16[2,2048,384]{2,0,1:T(2,128)(2,1)} %copy.70), calls=%async_computation.5 | async-start | bytes 6291456 | tf_op jit(solution)/shard_map/all_to_all | solution.py:62
  432.1 38.6 %all-to-all-start.3 = ((bf16[2,2048,384]{2,0,1:T(2,128)(2,1)}), bf16[2,2048,384]{2,0,1:T(2,128)(2,1)}, u32[]{:S(2)}, u32[]{:S(2)}) async-start(bf16[2,2048,384]{2,0,1:T(2,128)(2,1)} %copy.66), calls=%async_computation.3 | async-start | bytes 6291456 | tf_op jit(solution)/shard_map/all_to_all | solution.py:35
  437.1 23.1 %copy-start.33 = (s32[2048]{0:T(1024)S(1)}, s32[2048]{0:T(1024)}, u32[]{:S(2)}) copy-start(s32[2048]{0:T(1024)} %copy-done.32) | copy-start | bytes 24580
  437.1 23.1 %copy-start.35 = (s32[2048]{0:T(1024)S(1)}, s32[2048]{0:T(1024)}, u32[]{:S(2)}) copy-start(s32[2048]{0:T(1024)} %copy-done.34) | copy-start | bytes 24580
  437.2 23.1 %copy-start.29 = (s32[4096]{0:T(1024)S(1)}, s32[4096]{0:T(1024)}, u32[]{:S(2)}) copy-start(s32[4096]{0:T(1024)} %copy-done.28) | copy-start | bytes 49156
  532.5 36.2 %all-to-all-start.6 = ((bf16[8,512,384]{2,1,0:T(8,128)(2,1)}), bf16[8,512,384]{2,1,0:T(8,128)(2,1)S(1)}, u32[]{:S(2)}, u32[]{:S(2)}) async-start(bf16[8,512,384]{2,1,0:T(8,128)(2,1)} %bitcast.170), calls=%async_computation.6 | async-start | bytes 6291456 | tf_op jit(solution)/shard_map/all_to_all | solution.py:52
  536.2 258.2 %all-reduce.15.cloned.1.call-start = ((), (), s32[]{:S(2)}) async-start(), calls=%async_computation.10 | async-start | bytes 18874368 | tf_op jit(solution)/shard_map/psum | solution.py:92
  579.7 18.9 %copy-start.12 = (bf16[2,4,512,384]{3,2,1,0:T(8,128)(2,1)S(1)}, bf16[2,4,512,384]{3,2,1,0:T(8,128)(2,1)}, u32[]{:S(2)}) copy-start(bf16[2,4,512,384]{3,2,1,0:T(8,128)(2,1)} %copy-done.11) | copy-start | bytes 9437188
  657.9 35.2 %all-to-all-start.7 = ((bf16[2,2048,384]{2,0,1:T(2,128)(2,1)}), bf16[2,2048,384]{2,0,1:T(2,128)(2,1)S(1)}, u32[]{:S(2)}, u32[]{:S(2)}) async-start(bf16[2,2048,384]{2,0,1:T(2,128)(2,1)} %copy.74), calls=%async_computation.7 | async-start | bytes 6291456 | tf_op jit(solution)/shard_map/all_to_all | solution.py:62
  661.6 286.5 %all-reduce.11.cloned.1.call-start = ((), (), s32[]{:S(2)}) async-start(), calls=%async_computation.8 | async-start | bytes 1179648 | tf_op jit(solution)/shard_map/psum | solution.py:91
  716.8 77.6 %copy-start.5 = (f32[1024,384]{1,0:T(8,128)}, f32[1024,384]{1,0:T(8,128)S(1)}, u32[]{:S(2)}) copy-start(f32[1024,384]{1,0:T(8,128)S(1)} %reduce_sum.65) | copy-start | bytes 4718596
  718.2 344.7 %all-reduce.13.cloned.1.call-start = ((), (), s32[]{:S(2)}) async-start(), calls=%async_computation.9 | async-start | bytes 18874368 | tf_op jit(solution)/shard_map/psum | solution.py:92
  799.6 18.9 %copy-start.6 = (f32[1024,384]{1,0:T(8,128)S(1)}, f32[1024,384]{1,0:T(8,128)}, u32[]{:S(2)}) copy-start(f32[1024,384]{1,0:T(8,128)} %copy-done.5) | copy-start | bytes 4718596
  799.6 18.9 %copy-start.21 = (bf16[1024,384]{1,0:T(8,128)(2,1)S(1)}, bf16[1024,384]{1,0:T(8,128)(2,1)}, u32[]{:S(2)}) copy-start(bf16[1024,384]{1,0:T(8,128)(2,1)} %copy-done.19) | copy-start | bytes 2359300
  799.6 18.9 %copy-start.56 = (bf16[2,384,384]{2,1,0:T(8,128)(2,1)S(1)}, bf16[2,384,384]{2,1,0:T(8,128)(2,1)}, u32[]{:S(2)}) copy-start(bf16[2,384,384]{2,1,0:T(8,128)(2,1)} %param.18) | copy-start | bytes 1769476
  (45 other events, 298.4 us)
Sparse Core Ops, SparseCore 0:
  611.6 182.6 all-reduce.14
  799.1 148.8 all-reduce.10
  950.8 111.9 all-reduce.12
where the time goes:
time: 1080 us
  waiting for transfers between devices  417 us (39%)
  local copies, waits for them, and re-layouts  343 us (32%)
  matrix products  179 us (17%)
  other arithmetic  89.3 us (8%)
  starting transfers between devices  35.9 us (3%)
  between operations  14.9 us (1%)
    psum x1, waiting for transfers between devices, device_step(): dense_sums.insert(0, lax.psum(grad_dense.astype(jnp.bfloat16), TOK_AXES))  128 us
    psum x1, waiting for transfers between devices, device_step(): lax.psum(lax.psum(grad_gate.astype(jnp.bfloat16), 'rep'), 'dp')  113 us
    psum x1, waiting for transfers between devices, device_step(): lax.psum(grad_gate.astype(jnp.bfloat16), 'rep')  76.1 us
    all_to_all x2, waiting for transfers between devices, layer_forward(): expert_in = lax.all_to_all(send_buf, 'ep', 0, 1, tiled=True)  58.4 us
    convert_element_type x2, local copies, waits for them, and re-layouts, layer_backward(): (jnp.einsum('enf,edf->end', grad_gate_act, gate_w, preferred_element_type...  57 us
    convert_element_type x2, local copies, waits for them, and re-layouts, layer_forward(): jnp.einsum('enf,efd->end', hidden, down_w, preferred_element_type=jnp.flo...  57 us
    gather x2, local copies, waits for them, and re-layouts, layer_backward(): slot_gate = jnp.take(gate_pad, copy_of)  46.1 us
    dot_general x2, matrix products, layer_backward(): jnp.einsum('end,efd->enf', grad_exp_out, down_w, preferred_element_type=j...  38.5 us
  transfers between devices with their start and end apart: 11, of which 8 were waited for; matrix products, arithmetic and copies ran while one was open for 29% of the time, Pallas kernels for 0%

commit v1 on v0

v1 whole, which is shorter than its diff:
```python
import functools

import jax
import jax.numpy as jnp
from jax import lax
from jax.experimental import pallas as pl
from jax.experimental.pallas import tpu as pltpu
from jax.sharding import PartitionSpec as P

TOK_AXES = ("rep", "ep", "dp")
F32 = jnp.float32
BF16 = jnp.bfloat16
LANES = 128
SIDE = 4
WAYS = (1, -1)
BUFS = (0, 1)
LAYERS = (1, 0)
ARRAYS = range(3)
SLOTS = 8
MESH = pl.DeviceIdType.MESH
VMEM_LIMIT = 63 << 20


def dot(a, b):
    return jnp.dot(a, b, preferred_element_type=F32)


def dot_nt(a, b):
    return lax.dot_general(a, b, (((1,), (1,)), ((), ())), preferred_element_type=F32)


def dot_tn(a, b):
    return lax.dot_general(a, b, (((0,), (0,)), ((), ())), preferred_element_type=F32)


class Place:
    def __init__(self):
        self.z, self.y, dp = lax.axis_index("rep"), lax.axis_index("ep"), lax.axis_index("dp")
        self.x, self.c = dp // 2, dp % 2

    def at(self, axis, step):
        z, y, x, c = self.z, self.y, self.x, self.c
        if axis == "z":
            z = (z + step + SIDE) % SIDE
        elif axis == "y":
            y = (y + step + SIDE) % SIDE
        elif axis == "x":
            x = (x + step + SIDE) % SIDE
        else:
            c = 1 - c
        return (z, y, x * 2 + c)


class Copies:
    def __init__(self, place, send, recv):
        self.place, self.send, self.recv, self.made, self.number, self.count = place, send, recv, {}, {}, 0

    def add(self, key, src, dst, axis, step, like=None):
        if like is None:
            n, self.count = self.count, self.count + 1
        else:
            n = self.number[like]
        self.number[key] = n
        self.made[key] = pltpu.make_async_remote_copy(src_ref=src, dst_ref=dst, send_sem=self.send.at[n], recv_sem=self.recv.at[n], device_id=self.place.at(axis, step), device_id_type=MESH)

    def start(self, *keys):
        for key in keys:
            self.made[key].start()

    def arrive(self, *keys):
        for key in keys:
            self.made[key].wait_recv()

    def sent(self, *keys):
        for key in keys:
            self.made[key].wait_send()

    def drain(self):
        for copy in self.made.values():
            copy.wait_send()


def greet(place):
    barrier = pltpu.get_barrier_semaphore()
    peers = [(axis, step) for axis in "xyz" for step in WAYS] + [("c", 0)]
    for axis, step in peers:
        pl.semaphore_signal(barrier, inc=1, device_id=place.at(axis, step), device_id_type=MESH)
    pl.semaphore_wait(barrier, len(peers))


class Gather:
    FROM = {2: -1, 3: 1, 6: 2}
    PASS = {2: 4, 3: 5, 6: 7}

    def __init__(self, layer, copies, place, own, whole):
        self.layer, self.copies, self.place, self.own, self.whole = layer, copies, place, own, whole
        rows, ff = own[0].shape[2], own[2].shape[2]
        self.cut = {"x": ((0, 0, rows // SIDE), (2, 0, ff // 2 // SIDE)), "z": ((1, 0, rows // SIDE), (2, ff // 2, ff // 2 // SIDE))}
        mine = {"x": place.x, "z": place.z}
        for color in ("x", "z"):
            for part in BUFS:
                self._add(("y", 2, color, part), color, part, None, 2, mine[color], None, "y", 1)
                self._add(("y", 3, color, part), color, part, None, 3, mine[color], None, "y", -1)
                if color == "x":
                    self._add(("y", 6, color, part), color, part, 2, 6, mine[color], None, "y", 1)
                else:
                    self._add(("y", 6, color, part), color, part, 3, 6, mine[color], None, "y", -1)
                for slot in (2, 3, 6):
                    for step in WAYS:
                        self._add(("near", slot, color, part, step), color, part, slot, slot, mine[color], None, color, step)
                        behind = (mine[color] - step + SIDE) % SIDE
                        self._add(("far", slot, color, part, step), color, part, slot, slot, behind, (1 - step) // 2, color, step)
        for slot, to in self.PASS.items():
            for array in ARRAYS:
                copies.add((layer, "pass", slot, array), whole[array].at[layer, slot], whole[array].at[layer, to], "c", 0)

    def _view(self, refs, index, color, part, quarter, half):
        array, base, size = self.cut[color][part]
        start = base + quarter * size
        if half is not None:
            size = size // 2
            start = start + half * size
        return refs[array].at[self.layer, index, pl.ds(pl.multiple_of(start, 16), size)]

    def _add(self, key, color, part, src_slot, dst_slot, quarter, half, axis, step):
        src = self._view(self.own, self.place.c, color, part, quarter, half) if src_slot is None else self._view(self.whole, src_slot, color, part, quarter, half)
        self.copies.add((self.layer,) + key, src, self._view(self.whole, dst_slot, color, part, quarter, half), axis, step)

    def _keys(self, *key, extra=()):
        return [(self.layer,) + key + (part,) + extra for part in BUFS]

    def lead(self):
        self.spread(2, "x")
        self.spread(3, "z")

    def lead_onward(self):
        self.onward(2, "x")
        self.onward(3, "z")

    def follow(self):
        self.spread(2, "z")
        self.spread(3, "x")

    def follow_onward(self):
        self.onward(2, "z")
        self.onward(3, "x")

    def last(self):
        self.spread(6, "x")
        self.spread(6, "z")

    def last_onward(self):
        self.onward(6, "x")
        self.onward(6, "z")

    def complete_y(self):
        self.complete(2)
        self.complete(3)

    def complete_last(self):
        self.complete(6)

    def passed_left(self):
        self.passed(2)

    def passed_right(self):
        self.passed(3)

    def passed_last(self):
        self.passed(6)

    def begin(self):
        for slot, color in ((2, "x"), (3, "z"), (2, "z"), (3, "x")):
            self.copies.start(*self._keys("y", slot, color))

    def spread(self, slot, color):
        self.copies.arrive(*self._keys("y", slot, color))
        if (slot, color) in ((2, "x"), (3, "z")):
            self.copies.start(*self._keys("y", 6, color))
        for step in WAYS:
            self.copies.start(*self._keys("near", slot, color, extra=(step,)))

    def onward(self, slot, color):
        for step in WAYS:
            self.copies.arrive(*self._keys("near", slot, color, extra=(step,)))
            self.copies.start(*self._keys("far", slot, color, extra=(step,)))

    def complete(self, slot):
        for color in ("x", "z"):
            for step in WAYS:
                self.copies.arrive(*self._keys("far", slot, color, extra=(step,)))
        self.copies.start(*[(self.layer, "pass", slot, array) for array in ARRAYS])

    def passed(self, slot):
        self.copies.arrive(*[(self.layer, "pass", slot, array) for array in ARRAYS])


GATHER_COPIES = 2 * (2 * 2 * (3 + 3 * 4) + 9)


def route(layer, ids_ref, gate_ref, rank_ref, rank_t_ref, gmat_ref, place):
    tokens = ids_ref.shape[1]
    ids, gates = ids_ref[layer], gate_ref[layer]
    off = ((ids >> 1) - place.y) & (SIDE - 1)
    odd = (ids + place.c) & 1
    slot = jnp.where(off == 0, odd, jnp.where(off == SIDE - 1, 2 + 2 * odd, jnp.where(off == 1, 3 + 2 * odd, 6 + odd)))
    lane = lax.broadcasted_iota(jnp.int32, (tokens, LANES), 1)
    hit0 = slot[:, 0:1] == lane
    hit1 = slot[:, 1:2] == lane
    hit = hit0 | hit1
    gmat_ref[layer] = jnp.where(hit0, gates[:, 0:1], 0.0) + jnp.where(hit1, gates[:, 1:2], 0.0)
    row = lax.broadcasted_iota(jnp.int32, (tokens, tokens), 0)
    col = lax.broadcasted_iota(jnp.int32, (tokens, tokens), 1)
    below = jnp.where(col < row, 1.0, 0.0).astype(BF16)
    rank = jnp.where(hit, dot(below, jnp.where(hit, 1.0, 0.0).astype(BF16)), -1.0)
    rank_ref[layer] = rank.astype(jnp.int32)
    rank_t_ref[layer] = jnp.transpose(rank)[:SLOTS].astype(jnp.int32)


def one_hot(rank_t_ref, layer, slot, rows):
    tokens = rank_t_ref.shape[2]
    place = lax.broadcasted_iota(jnp.int32, (rows, tokens), 0)
    return jnp.where(rank_t_ref[layer, pl.ds(slot, 1), :] == place, 1.0, 0.0).astype(BF16)


def column(ref, layer, slot, zero):
    tokens = ref.shape[1]
    lane = lax.broadcasted_iota(jnp.int32, (tokens, LANES), 1)
    return jnp.sum(jnp.where(lane == slot, ref[layer], zero), axis=1, keepdims=True)


def one_hot_t(rank_ref, layer, slot, rows):
    tokens = rank_ref.shape[1]
    place = lax.broadcasted_iota(jnp.int32, (tokens, rows), 1)
    return jnp.where(column(rank_ref, layer, slot, jnp.int32(0)) == place, 1.0, 0.0).astype(BF16)


def fwd_kernel(cap, x_ref, ids_ref, gate_ref, wd_ref, o1_ref, o3_ref, o2_ref, y_ref, x1_ref, rank_ref, rank_t_ref, gmat_ref, g1_ref, g3_ref, g2_ref, z_ref, a_ref, b_ref, u_ref, acc_ref, b1_ref, b3_ref, b2_ref, load_sem, keep_sem, send_sem, recv_sem):
    s = pl.program_id(0)
    steps = pl.num_programs(0)
    layer, slot = s // SLOTS, s % SLOTS
    place = Place()
    copies = Copies(place, send_sem, recv_sem)
    own, whole, bufs = (o1_ref, o3_ref, o2_ref), (g1_ref, g3_ref, g2_ref), (b1_ref, b3_ref, b2_ref)
    g0, g1 = (Gather(l, copies, place, own, whole) for l in BUFS)

    def at(step, body):
        pl.when(s == step)(body)

    def loads(step, mine):
        l, k = step // SLOTS, step % SLOTS
        for n in ARRAYS:
            src = own[n].at[l, (place.c + k) % 2] if mine else whole[n].at[l, k]
            yield pltpu.make_async_copy(src, bufs[n].at[step % 2], load_sem.at[step % 2, n])

    def keeps(step):
        for n in ARRAYS:
            yield pltpu.make_async_copy(bufs[n].at[step % 2], whole[n].at[step // SLOTS, step % SLOTS], keep_sem.at[step % 2, n])

    def load(step):
        k = step % SLOTS

        @pl.when(k < 2)
        def _():
            for copy in loads(step, True):
                copy.start()

        @pl.when(k >= 2)
        def _():
            for copy in loads(step, False):
                copy.start()

    @pl.when(s == 0)
    def _():
        load(0)
        greet(place)
        g0.begin()
        for l in BUFS:
            route(l, ids_ref, gate_ref, rank_ref, rank_t_ref, gmat_ref, place)
        g0.lead()
        load(1)

    plan = [
        [],
        [g0.follow],
        [g0.lead_onward, g0.last, g1.begin, g0.follow_onward, g0.complete_y, lambda: load(s), g0.last_onward],
        [g0.passed_left],
        [g1.lead, g0.complete_last, g0.passed_right],
        [g1.follow],
        [g1.lead_onward, g0.passed_last],
        [g1.last],
        [g1.follow_onward],
        [g1.complete_y, g1.last_onward],
        [],
        [g1.passed_left],
        [g1.complete_last, g1.passed_right],
        [],
        [g1.passed_last],
    ]
    for step, parts in enumerate(plan):

        @pl.when(s == step)
        def _(parts=parts):
            for part in parts:
                part()

    for copy in loads(s, False):
        copy.wait()

    @pl.when((s > 0) & (s != 1) & (s < steps - 1))
    def _():
        load(s + 1)

    @pl.when(slot < 2)
    def _():
        for copy in keeps(s):
            copy.start()

    def enter(x):
        u_ref[...] = (x.astype(F32) + dot(x, wd_ref[layer])).astype(BF16)
        acc_ref[...] = jnp.zeros_like(acc_ref)

    at(0, lambda: enter(x_ref[...]))
    at(SLOTS, lambda: enter(x1_ref[...]))

    buf = s % 2
    z = dot(one_hot(rank_t_ref, layer, slot, cap), u_ref[...]).astype(BF16)
    z_ref[0, 0] = z
    a = dot(z, b1_ref[buf]).astype(BF16)
    b = dot(z, b3_ref[buf]).astype(BF16)
    a_ref[0, 0] = a
    b_ref[0, 0] = b
    h = (jax.nn.silu(a.astype(F32)) * b.astype(F32)).astype(BF16)
    o = dot(h, b2_ref[buf]).astype(BF16)
    acc_ref[...] += column(gmat_ref, layer, slot, 0.0) * dot(one_hot_t(rank_ref, layer, slot, cap), o)

    def leave(out_ref):
        out_ref[...] = (u_ref[...].astype(F32) + acc_ref[...]).astype(BF16)

    @pl.when(slot < 2)
    def _():
        for copy in keeps(s):
            copy.wait()

    at(SLOTS - 1, lambda: leave(x1_ref))

    @pl.when(s == steps - 1)
    def _():
        leave(y_ref)
        copies.drain()


def forward(cap, x, ids, gates, wd, w1, w3, w2):
    tokens, width = x.shape
    layers, _, ff = ids.shape[0], None, w1.shape[3]
    vmem = pl.BlockSpec(memory_space=pltpu.VMEM)
    hbm = pl.BlockSpec(memory_space=pl.ANY)

    def saved(n):
        return pl.BlockSpec((1, 1, cap, n), lambda s: (s // SLOTS, s % SLOTS, 0, 0))

    shape = jax.ShapeDtypeStruct
    return pl.pallas_call(
        functools.partial(fwd_kernel, cap),
        grid=(layers * SLOTS,),
        in_specs=[vmem] * 4 + [hbm] * 3,
        out_specs=[vmem] * 5 + [hbm] * 3 + [saved(width), saved(ff), saved(ff)],
        out_shape=[
            shape((tokens, width), BF16),
            shape((tokens, width), BF16),
            shape((layers, tokens, LANES), jnp.int32),
            shape((layers, SLOTS, tokens), jnp.int32),
            shape((layers, tokens, LANES), F32),
            shape((layers, SLOTS, width, ff), BF16),
            shape((layers, SLOTS, width, ff), BF16),
            shape((layers, SLOTS, ff, width), BF16),
            shape((layers, SLOTS, cap, width), BF16),
            shape((layers, SLOTS, cap, ff), BF16),
            shape((layers, SLOTS, cap, ff), BF16),
        ],
        scratch_shapes=[
            pltpu.VMEM((tokens, width), BF16),
            pltpu.VMEM((tokens, width), F32),
            pltpu.VMEM((2, width, ff), BF16),
            pltpu.VMEM((2, width, ff), BF16),
            pltpu.VMEM((2, ff, width), BF16),
            pltpu.SemaphoreType.DMA((2, 3)),
            pltpu.SemaphoreType.DMA((2, 3)),
            pltpu.SemaphoreType.DMA((GATHER_COPIES,)),
            pltpu.SemaphoreType.DMA((GATHER_COPIES,)),
        ],
        compiler_params=pltpu.CompilerParams(vmem_limit_bytes=VMEM_LIMIT, collective_id=0, has_side_effects=True),
        name="forward",
    )(x, ids, gates, wd, w1, w3, w2)


def add_to(dst, src):
    dst[...] = (dst[...].astype(F32) + src[...].astype(F32)).astype(BF16)


class RingSum:
    def __init__(self, copies, name, axis, block, first, second):
        self.copies, self.name, self.block, self.first, self.second = copies, name, block, first, second
        self.early, self.later = ([(name, when, step) for step in WAYS] for when in ("early", "later"))
        for half, step in enumerate(WAYS):
            copies.add(self.early[half], block(2, half), first.at[half], axis, step)
            copies.add(self.later[half], block(step, None), second.at[half], axis, step)

    def start(self):
        self.copies.start(*self.early)

    def onward(self):
        self.copies.arrive(*self.early)
        for half, step in enumerate(WAYS):
            add_to(self.block(step, half), self.first.at[half])
        self.copies.start(*self.later)

    def finish(self, out):
        self.copies.arrive(*self.later)
        out[...] = (self.block(0, None)[...].astype(F32) + self.second[0].astype(F32) + self.second[1].astype(F32)).astype(BF16)
        self.copies.sent(*self.early, *self.later)


class RingSpread:
    def __init__(self, copies, name, axis, me, block, source=None, like=None):
        self.copies = copies
        self.near, self.far = ([(name, when, step) for step in WAYS] for when in ("near", "far"))
        for half, step in enumerate(WAYS):
            behind = (me - step + SIDE) % SIDE
            near, far = (None, None) if like is None else (like.near[half], like.far[half])
            copies.add(self.near[half], block(me, None) if source is None else source, block(me, None), axis, step, near)
            copies.add(self.far[half], block(behind, half), block(behind, half), axis, step, far)

    def start(self):
        self.copies.start(*self.near)

    def onward(self):
        for near, far in zip(self.near, self.far):
            self.copies.arrive(near)
            self.copies.start(far)

    def finish(self):
        self.copies.arrive(*self.far)
        self.copies.sent(*self.near, *self.far)


def slices(ref, lead, base, size):
    def block(index, half):
        start, rows = base + index * size, size
        if half is not None:
            rows = size // 2
            start = start + half * rows
        return ref.at[(*lead, pl.ds(pl.multiple_of(start, 16), rows))]

    return block


def slabs(ref):
    def block(index, half):
        if half is None:
            return ref.at[index]
        rows = ref.shape[1] // 2
        return ref.at[index, pl.ds(half * rows, rows)]

    return block


def total(ref):
    return (ref[0].astype(F32) + ref[1].astype(F32) + ref[2].astype(F32) + ref[3].astype(F32)).astype(BF16)


OWN_STEPS = {1: 0, 4: 1, 5: 2, 7: 3}
REDUCE_COPIES = 107


def bwd_kernel(cap, dy_ref, x0_ref, x1_ref, wd_ref, rank_ref, rank_t_ref, gmat_ref, w1_ref, w3_ref, w2_ref, z_ref, a_ref, b_ref, dx_ref, gd_ref, g1_ref, g3_ref, g2_ref, acc_ref, cur_ref, m1_ref, m3_ref, m2_ref, d1_ref, d3_ref, d2_ref, s1_ref, s3_ref, s2_ref, r11_ref, r12_ref, r31_ref, r32_ref, t1_ref, t3_ref, y11_ref, y12_ref, y31_ref, y32_ref, y21_ref, y22_ref, u1_ref, u2_ref, l1_ref, l2_ref, c1_ref, c3_ref, cu_ref, cl_ref, f1_ref, f3_ref, fu_ref, fl_ref, dp_ref, dr_ref, dcx_ref, dcy_ref, dcz_ref, ds_ref, de_ref, put_sem, send_sem, recv_sem, credit):
    s = pl.program_id(0)
    steps = pl.num_programs(0)
    layer, slot, t = 1 - s // SLOTS, SLOTS - 1 - s % SLOTS, s % SLOTS
    group = t // 4 + t // 5 + t // 7
    into = (t // 2 + t // 3) % 2
    place = Place()
    copies = Copies(place, send_sem, recv_sem)
    rows, ff = s1_ref.shape[1], s2_ref.shape[1]
    quarter, part = rows // SIDE, ff // 2 // SIDE
    half_d = rows // 2

    stage, mate, own = (m1_ref, m3_ref, m2_ref), (d1_ref, d3_ref, d2_ref), (s1_ref, s3_ref, s2_ref)
    outs = (g1_ref, g3_ref, g2_ref)
    for buf in BUFS:
        for n in ARRAYS:
            copies.add(("pair", buf, n), stage[n], mate[n].at[buf], "c", 0)

    def ring_blocks(ref, q, me, base, size):
        block = slices(ref, (q,), base, size)
        return lambda offset, half: block((me + offset + SIDE) % SIDE, half)

    def group_blocks(ref):
        block = slabs(ref)
        return lambda offset, half: block({2: 0, 1: 1, -1: 2, 0: 3}[offset], half)

    first = {
        "x": [RingSum(copies, ("x", q), "x", ring_blocks(s1_ref, q, place.x, 0, quarter), r11_ref.at[q], r12_ref.at[q]) for q in range(SIDE)],
        "z": [RingSum(copies, ("z", q), "z", ring_blocks(s3_ref, q, place.z, 0, quarter), r31_ref.at[q], r32_ref.at[q]) for q in range(SIDE)],
    }
    mid = {"x": t1_ref, "z": t3_ref}
    on_y = {
        "x": RingSum(copies, "yx", "y", group_blocks(t1_ref), y11_ref, y12_ref),
        "z": RingSum(copies, "yz", "y", group_blocks(t3_ref), y31_ref, y32_ref),
        "w": RingSum(copies, "yw", "y", group_blocks(s2_ref), y21_ref, y22_ref),
    }
    inner = {
        "u": RingSum(copies, "u", "x", ring_blocks(s2_ref, 3, place.x, 0, part), u1_ref, u2_ref),
        "l": RingSum(copies, "l", "z", ring_blocks(s2_ref, 3, place.z, ff // 2, part), l1_ref, l2_ref),
    }
    ring_of = {"x": ("x", place.x), "u": ("x", place.x), "z": ("z", place.z), "l": ("z", place.z)}
    other_of = {"x": ("z", place.z), "u": ("z", place.z), "z": ("x", place.x), "l": ("x", place.x)}
    cross_ref = {"x": c1_ref, "z": c3_ref, "u": cu_ref, "l": cl_ref}
    done_ref = {"x": f1_ref, "z": f3_ref, "u": fu_ref, "l": fl_ref}
    out_of = {"x": (g1_ref, 0, quarter), "z": (g3_ref, 0, quarter), "u": (g2_ref, 0, part), "l": (g2_ref, ff // 2, part)}
    cross, final, puts = {}, {}, {}
    for i, k in enumerate(out_of):
        cross[k] = RingSpread(copies, ("cross", k), *other_of[k], slabs(cross_ref[k]))
        ref, base, size = out_of[k]
        for late in LAYERS:
            block = slices(ref, (late, place.c), base, size)
            final[k, late] = RingSpread(copies, ("final", k, late), *ring_of[k], block, source=done_ref[k], like=final.get((k, 1)))
            puts[k, late] = pltpu.make_async_copy(done_ref[k], block(ring_of[k][1], None), put_sem.at[i])
    mine, theirs = (pl.ds(pl.multiple_of(c * half_d, 16), half_d) for c in (place.c, 1 - place.c))
    for late in LAYERS:
        for n, out in enumerate(outs):
            copies.add(("pass", n, late), out.at[late, place.c], out.at[late, place.c], "c", 0, None if late else ("pass", n, 1))
    copies.add("dense pair", dp_ref.at[theirs], dr_ref, "c", 0)
    copies.add("dense pass", ds_ref, de_ref, "c", 0)
    dense_refs = {"y": dcy_ref, "x": dcx_ref, "z": dcz_ref}
    index_of = {"y": place.y, "x": place.x, "z": place.z}
    dense = {k: RingSpread(copies, ("dense", k), k, index_of[k], slabs(ref)) for k, ref in dense_refs.items()}

    def reduce_start(q):
        for k in ("x", "z"):
            first[k][q].start()

    def reduce_onward(q):
        for k in ("x", "z"):
            first[k][q].onward()

    def reduce_finish(q):
        for k in ("x", "z"):
            first[k][q].finish(mid[k].at[q])

    def y_start():
        for k in ("x", "z"):
            on_y[k].start()

    def y_onward():
        for k in ("x", "z"):
            on_y[k].onward()

    def y_finish():
        for k in ("x", "z"):
            on_y[k].finish(cross_ref[k].at[other_of[k][1]])
            cross[k].start()

    def w_finish():
        on_y["w"].finish(s2_ref.at[3])
        for k in ("u", "l"):
            inner[k].start()

    def inner_onward():
        for k in ("u", "l"):
            inner[k].onward()

    def inner_finish():
        for k in ("u", "l"):
            inner[k].finish(cross_ref[k].at[other_of[k][1]])
            cross[k].start()

    def cross_onward(*keys):
        for k in keys:
            cross[k].onward()

    def cross_finish(late, *keys):
        for k in keys:
            cross[k].finish()
            done_ref[k][...] = total(cross_ref[k])
            puts[k, late].start()
            final[k, late].start()

    def final_onward(late, *keys):
        for k in keys:
            final[k, late].onward()

    def final_finish(late, *keys):
        for k in keys:
            final[k, late].finish()
            puts[k, late].wait()
        copies.start(*[("pass", n, late) for n in ((0, 1) if "x" in keys else (2,))])

    def pass_finish(late):
        keys = [("pass", n, late) for n in ARRAYS]
        copies.arrive(*keys)
        copies.sent(*keys)

    def dense_sum():
        copies.arrive("dense pair")
        dcy_ref[place.y] = (dp_ref[mine].astype(F32) + dr_ref[...].astype(F32)).astype(BF16)
        copies.sent("dense pair")
        dense["y"].start()

    def dense_next(k, follow):
        dense[k].finish()
        dense_refs[follow][index_of[follow]] = total(dense_refs[k])
        dense[follow].start()

    def dense_pass(late):
        dense["z"].finish()
        ds_ref[...] = total(dcz_ref)
        gd_ref[late, mine] = ds_ref[...]
        copies.start("dense pass")

    def dense_finish(late):
        copies.arrive("dense pass")
        gd_ref[late, theirs] = de_ref[...]
        copies.sent("dense pass")

    spread = [
        lambda: (copies.start("dense pair"), reduce_onward(3), w_finish()),
        lambda: (dense_sum(), reduce_finish(3), y_finish(), inner_onward()),
        lambda: (inner_finish(), cross_onward("x", "z"), dense["y"].onward()),
        lambda: (cross_finish(1, "x", "z"), cross_onward("u", "l"), dense_next("y", "x")),
        lambda: (final_onward(1, "x", "z"), cross_finish(1, "u", "l"), dense["x"].onward()),
        lambda: (final_finish(1, "x", "z"), final_onward(1, "u", "l"), dense_next("x", "z")),
        lambda: (final_finish(1, "u", "l"), dense["z"].onward()),
        lambda: (pass_finish(1), dense_pass(1)),
    ]

    def ending():
        dense_finish(1)
        copies.start("dense pair")
        w_finish()
        reduce_onward(3)
        dense_sum()
        inner_onward()
        reduce_finish(3)
        y_finish()
        dense["y"].onward()
        inner_finish()
        cross_onward("x", "z")
        dense_next("y", "x")
        cross_onward("u", "l")
        cross_finish(0, "x", "z")
        dense["x"].onward()
        cross_finish(0, "u", "l")
        final_onward(0, "x", "z")
        dense_next("x", "z")
        final_onward(0, "u", "l")
        final_finish(0, "x", "z")
        dense["z"].onward()
        final_finish(0, "u", "l")
        dense_pass(0)
        pass_finish(0)
        dense_finish(0)

    def at(step, body):
        pl.when(s == step)(lambda: body() and None)

    def each(step, body):
        pl.when(t == step)(lambda: body() and None)

    def load_grad(x):
        acc_ref[...] = x.astype(F32)
        cur_ref[...] = x

    @pl.when(s == 0)
    def _():
        greet(place)
        load_grad(dy_ref[...])

    for step, body in enumerate(spread):
        at(step + SLOTS, body)
    each(2, lambda: reduce_onward(0))
    each(3, lambda: (reduce_finish(0), y_start()))
    each(5, lambda: reduce_onward(1))
    each(6, lambda: (reduce_onward(2), reduce_finish(1), on_y["w"].onward()))
    each(7, lambda: (reduce_finish(2), y_onward()))

    grad_gated = (column(gmat_ref, layer, slot, 0.0) * cur_ref[...].astype(F32)).astype(BF16)
    do = dot(one_hot(rank_t_ref, layer, slot, cap), grad_gated).astype(BF16)
    dh = dot_nt(do, w2_ref[0, 0])
    a = a_ref[0, 0].astype(F32)
    b = b_ref[0, 0].astype(F32)
    sig = jax.nn.sigmoid(a)
    act = a * sig
    h = (act * b).astype(BF16)
    db = (dh * act).astype(BF16)
    da = (dh * b * sig * (1.0 + a * (1.0 - sig))).astype(BF16)
    z = z_ref[0, 0]
    dz = (dot_nt(da, w1_ref[0, 0]) + dot_nt(db, w3_ref[0, 0])).astype(BF16)
    acc_ref[...] += dot(one_hot_t(rank_ref, layer, slot, cap), dz)

    def weight_grads():
        return dot_tn(z, da), dot_tn(z, db), dot_tn(h, do)

    is_own = functools.reduce(jnp.logical_or, [t == step for step in OWN_STEPS])

    @pl.when(jnp.logical_not(is_own))
    def _():
        for buf in BUFS:
            pl.when((s > 0) & (into == 1 - buf))(lambda buf=buf: copies.sent(*[("pair", buf, n) for n in ARRAYS]))

        for ref, grad in zip(stage, weight_grads()):
            ref[...] = grad.astype(BF16)

        pl.when(s >= 3)(lambda: pl.semaphore_wait(credit.at[into], 1))
        for buf in BUFS:
            pl.when(into == buf)(lambda buf=buf: copies.start(*[("pair", buf, n) for n in ARRAYS]))

    @pl.when(is_own)
    def _():
        for buf in BUFS:
            pl.when(group % 2 == buf)(lambda buf=buf: copies.arrive(*[("pair", buf, n) for n in ARRAYS]))

        for ref, add, grad in zip(own, mate, weight_grads()):
            ref[group] = (grad + add[group % 2].astype(F32)).astype(BF16)

        @pl.when(s < 13)
        def _():
            pl.semaphore_signal(credit.at[group % 2], inc=1, device_id=place.at("c", 0), device_id_type=MESH)

    def leave(x, out_ref):
        grad = acc_ref[...]
        grad_b = grad.astype(BF16)
        dp_ref[...] = dot_tn(x, grad_b).astype(BF16)
        out_ref[...] = (grad + dot_nt(grad_b, wd_ref[layer])).astype(BF16)

    for step, q in OWN_STEPS.items():
        each(step, lambda q=q: reduce_start(q))
    each(1, lambda: on_y["w"].start())

    @pl.when(s == SLOTS - 1)
    def _():
        leave(x1_ref[...], cur_ref)
        acc_ref[...] = cur_ref[...].astype(F32)

    @pl.when(s == steps - 1)
    def _():
        leave(x0_ref[...], dx_ref)
        ending()
        copies.sent(*[("pair", 1, n) for n in ARRAYS])


def backward(cap, dy, x0, x1, wd, rank, rank_t, gmat, w1, w3, w2, z, a, b):
    tokens, width = dy.shape
    layers, ff = w1.shape[0], w1.shape[3]
    local, quarter, part = SLOTS // SIDE, width // SIDE, ff // 2 // SIDE
    hbm = pl.BlockSpec(memory_space=pl.ANY)

    def fixed(shape):
        return pl.BlockSpec(shape, lambda s: (0,) * len(shape), pipeline_mode=pl.Buffered(1))

    def stream(*shape):
        return pl.BlockSpec((1, 1, *shape), lambda s: (1 - s // SLOTS, SLOTS - 1 - s % SLOTS, 0, 0))

    def buf(*shape):
        return pltpu.VMEM(shape, BF16)

    shape = jax.ShapeDtypeStruct
    ups, downs = [(width, ff), (width, ff), (ff, width)], [(quarter, ff), (part, width)]
    scratch = [pltpu.VMEM((tokens, width), F32), buf(tokens, width)]
    scratch += [buf(*u) for u in ups] + [buf(2, *u) for u in ups] + [buf(SIDE, *u) for u in ups]
    scratch += [buf(SIDE, 2, quarter // 2, ff), buf(SIDE, 2, quarter, ff)] * 2
    scratch += [buf(SIDE, quarter, ff)] * 2
    scratch += [buf(2, quarter // 2, ff), buf(2, quarter, ff)] * 2 + [buf(2, ff // 2, width), buf(2, ff, width)]
    scratch += [buf(2, part // 2, width), buf(2, part, width)] * 2
    scratch += [buf(SIDE, quarter, ff)] * 2 + [buf(SIDE, part, width)] * 2
    scratch += [buf(quarter, ff)] * 2 + [buf(part, width)] * 2
    scratch += [buf(width, width), buf(width // 2, width)] + [buf(SIDE, width // 2, width)] * 3 + [buf(width // 2, width)] * 2
    scratch += [pltpu.SemaphoreType.DMA((4,)), pltpu.SemaphoreType.DMA((REDUCE_COPIES,)), pltpu.SemaphoreType.DMA((REDUCE_COPIES,)), pltpu.SemaphoreType.REGULAR((2,))]
    return pl.pallas_call(
        functools.partial(bwd_kernel, cap),
        grid=(layers * SLOTS,),
        in_specs=[fixed(v.shape) for v in (dy, x0, x1, wd, rank, rank_t, gmat)] + [stream(*u) for u in ups] + [stream(cap, width), stream(cap, ff), stream(cap, ff)],
        out_specs=[fixed((tokens, width)), fixed((layers, width, width))] + [hbm] * 3,
        out_shape=[shape((tokens, width), BF16), shape((layers, width, width), BF16)] + [shape((layers, local, *u), BF16) for u in ups],
        scratch_shapes=scratch,
        compiler_params=pltpu.CompilerParams(vmem_limit_bytes=VMEM_LIMIT, collective_id=1, has_side_effects=True),
        name="backward",
    )(dy, x0, x1, wd, rank, rank_t, gmat, w1, w3, w2, z, a, b)


def solution(mesh):
    tok_spec = P(TOK_AXES, None)
    route_spec = P(None, TOK_AXES, None)
    expert_spec = P(None, "ep", None, None)
    whole_spec = P(None, None, None)

    def device_step(tok_in, tok_grad, route_ids, gate_vals, w_dense, w_gate, w_up, w_down):
        tokens, top_k = route_ids.shape[1:]
        cap = 2 * tokens * top_k // SLOTS
        y, x1, *kept = forward(cap, tok_in, route_ids, gate_vals, w_dense, w_gate, w_up, w_down)
        return (y, *backward(cap, tok_grad, tok_in, x1, w_dense, *kept))

    return jax.shard_map(device_step, mesh=mesh, in_specs=(tok_spec, tok_spec, route_spec, route_spec, whole_spec, expert_spec, expert_spec, expert_spec), out_specs=(tok_spec, tok_spec, whole_spec, expert_spec, expert_spec, expert_spec), check_vma=False)
```

time: 1080 us -> 316 us (0.29)
  waiting for transfers between devices: 417 us -> 0 us
  local copies, waits for them, and re-layouts: 343 us -> 17.1 us
  Pallas kernels: 0 us -> 298 us
  matrix products: 179 us -> 0 us
  other arithmetic: 89.3 us -> 0 us
  starting transfers between devices: 35.9 us -> 0 us
  between operations: 14.9 us -> 0.68 us
    psum x3 -> x0, waiting for transfers between devices: 317 us -> none  [the longest x1 128 us: device_step(): dense_sums.insert(0, lax.psum(grad_dense.astype(jnp.bfloat16), TOK_AXES))]
    pallas_call x0 -> x2, Pallas kernels: none -> 298 us  [the longest x1 191 us: backward(): pl.pallas_call(functools.partial(bwd_kernel, cap), grid=(layers * SLOTS,)...]
    dot_general x24 -> x0, matrix products: 179 us -> none  [the longest x2 38.5 us: layer_backward(): jnp.einsum('end,efd->enf', grad_exp_out, down_w, preferred_element_type=j...]
    gather x10 -> x0, local copies, waits for them, and re-layouts: 153 us -> none  [the longest x2 46.1 us: layer_backward(): slot_gate = jnp.take(gate_pad, copy_of)]
    convert_element_type x8 -> x0, local copies, waits for them, and re-layouts: 127 us -> none  [the longest x2 57 us: layer_backward(): (jnp.einsum('enf,edf->end', grad_gate_act, gate_w, preferred_element_type...]
    all_to_all x8 -> x0, waiting for transfers between devices: 100 us -> none  [the longest x2 58.4 us: layer_forward(): expert_in = lax.all_to_all(send_buf, 'ep', 0, 1, tiled=True)]
    reduce_sum x6 -> x0, other arithmetic: 46.7 us -> none  [the longest x2 35.1 us: layer_forward(): mix_sum = jnp.sum(gate_loc[:, :, None] * per_copy, axis=1)]
    all_to_all x8 -> x0, starting transfers between devices: 35.6 us -> none  [the longest x2 9.82 us: layer_forward(): lax.all_to_all(expert_out, 'ep', 1, 0, tiled=True)]
  transfers between devices with their start and end apart: 11 -> 0, of which waited for: 8 -> 0; matrix products, arithmetic and copies ran while one was open for 29% -> 0% of each run, Pallas kernels for 0% -> 0%
where the time goes in v1:
time: 316 us
  Pallas kernels  298 us (94%)
  local copies, waits for them, and re-layouts  17.1 us (5%)
    pallas_call x1, Pallas kernels, backward(): pl.pallas_call(functools.partial(bwd_kernel, cap), grid=(layers * SLOTS,)...  191 us
    pallas_call x1, Pallas kernels, forward(): pl.pallas_call(functools.partial(fwd_kernel, cap), grid=(layers * SLOTS,)...  107 us
    unnamed x16, local copies, waits for them, and re-layouts  17.1 us

profile of v1, /device:TPU:1, one launch (start us, length us, event | category | flops | bytes accessed | tf_op | source)
XLA Modules:
  0.0 315.8 jit_solution(13414384010884924630)
XLA Ops:
  0.6 2.1 copy.14.ids_ref
  2.7 2.1 copy.15.gate_ref
  4.7 107.5 %forward.1 = (bf16[1024,384]{1,0:T(8,128)(2,1)}, bf16[1024,384]{1,0:T(8,128)(2,1)}, s32[2,1024,128]{2,1,0:T(8,128)}, s32[2,8,1024]{2,1,0:T(8,128)}, f32[2,1024,1...) custom-call(bf16[1024,384]{1,0:T(8,128)(2,1)} %x0_ref.1, ...), custom_call_target="tpu_custom_call" | custom-call | tf_op jit(solution)/shard_map/forward/pallas_call | solution.py:363
  112.2 0.0 copy-start.3
  112.2 190.6 %backward.1 = (bf16[1024,384]{1,0:T(8,128)(2,1)}, bf16[2,384,384]{2,1,0:T(8,128)(2,1)}, bf16[2,2,384,1024]{3,2,1,0:T(8,128)(2,1)}, bf16[2,2,384,1024]{3,2,1,0:T(8,128)(2,1)}, bf16[2,2,1024,384]{3,2,1,0:T(8,128)(2,1)}) custom-call(bf16[1024,384]{1,0:T(8,128)(2,1)} %dy_ref.1, bf16[1024,384]{1,0:T(8,128)(2,1)} %x0_ref.1, ...), custom_call_target="tpu_custom_call" | custom-call | tf_op jit(solution)/shard_map/backward/pallas_call | solution.py:779
  302.8 0.0 copy-start.2
  302.8 0.0 copy-done.3
  302.8 0.9 copy.22
  303.7 2.4 copy.23
  306.1 1.9 copy.24
  308.0 0.0 copy-done.2
  308.0 0.0 copy-start.1
  308.0 1.7 copy.25
  309.7 1.4 copy-done.1
  311.1 0.0 copy-start
  311.1 1.7 copy.26
  312.7 1.4 copy-done
  314.1 1.7 copy.27
Async XLA Ops:
  112.2 190.6 %copy-start.3 = (bf16[1024,384]{1,0:T(8,128)(2,1)S(1)}, bf16[1024,384]{1,0:T(8,128)(2,1)}, u32[]{:S(2)}) copy-start(bf16[1024,384]{1,0:T(8,128)(2,1)} %get-tuple-element.44) | copy-start | bytes 2359300
  302.8 5.3 %copy-start.2 = (bf16[2,2,384,1024]{3,2,1,0:T(8,128)(2,1)S(1)}, bf16[2,2,384,1024]{3,2,1,0:T(8,128)(2,1)}, u32[]{:S(2)}) copy-start(bf16[2,2,384,1024]{3,2,1,0:T(8,128)(2,1)} %get-tuple-element.47) | copy-start | bytes 9437188
  308.0 3.0 copy-start.1
  311.1 3.0 copy-start

commit v2 on v1

--- a/solution.py
+++ b/solution.py
@@ -198,23 +198,24 @@
 GATHER_COPIES = 2 * (2 * 2 * (3 + 3 * 4) + 9)
 
 
-def route(layer, ids_ref, gate_ref, rank_ref, rank_t_ref, gmat_ref, place):
-    tokens = ids_ref.shape[1]
-    ids, gates = ids_ref[layer], gate_ref[layer]
-    off = ((ids >> 1) - place.y) & (SIDE - 1)
-    odd = (ids + place.c) & 1
-    slot = jnp.where(off == 0, odd, jnp.where(off == SIDE - 1, 2 + 2 * odd, jnp.where(off == 1, 3 + 2 * odd, 6 + odd)))
-    lane = lax.broadcasted_iota(jnp.int32, (tokens, LANES), 1)
-    hit0 = slot[:, 0:1] == lane
-    hit1 = slot[:, 1:2] == lane
-    hit = hit0 | hit1
-    gmat_ref[layer] = jnp.where(hit0, gates[:, 0:1], 0.0) + jnp.where(hit1, gates[:, 1:2], 0.0)
-    row = lax.broadcasted_iota(jnp.int32, (tokens, tokens), 0)
-    col = lax.broadcasted_iota(jnp.int32, (tokens, tokens), 1)
-    below = jnp.where(col < row, 1.0, 0.0).astype(BF16)
-    rank = jnp.where(hit, dot(below, jnp.where(hit, 1.0, 0.0).astype(BF16)), -1.0)
-    rank_ref[layer] = rank.astype(jnp.int32)
-    rank_t_ref[layer] = jnp.transpose(rank)[:SLOTS].astype(jnp.int32)
+def route(ids_ref, gate_ref, rank_ref, rank_t_ref, gmat_ref, place):
+    layers, _, tokens = ids_ref.shape
+    below = lax.broadcasted_iota(jnp.int32, (tokens, tokens), 0) < lax.broadcasted_iota(jnp.int32, (tokens, tokens), 1)
+    below = jnp.where(below, 1.0, 0.0).astype(BF16)
+    lead = lax.broadcasted_iota(jnp.int32, (LANES, tokens), 0)
+    for layer in range(layers):
+        ids, gates = ids_ref[layer], gate_ref[layer]
+        off = ((ids >> 1) - place.y) & (SIDE - 1)
+        odd = (ids + place.c) & 1
+        slot = jnp.where(off == 0, odd, jnp.where(off == SIDE - 1, 2 + 2 * odd, jnp.where(off == 1, 3 + 2 * odd, 6 + odd)))
+        hits = [slot[n : n + 1] == lead for n in BUFS]
+        hit = hits[0] | hits[1]
+        weight = jnp.where(hits[0], gates[0:1], 0.0) + jnp.where(hits[1], gates[1:2], 0.0)
+        count = dot(jnp.where(hit, 1.0, 0.0)[: 2 * SLOTS].astype(BF16), below)
+        rank = jnp.where(hit, jnp.concatenate([count, jnp.zeros((LANES - 2 * SLOTS, tokens), F32)], axis=0), -1.0)
+        rank_t_ref[layer] = rank[:SLOTS].astype(jnp.int32)
+        rank_ref[layer] = jnp.transpose(rank).astype(jnp.int32)
+        gmat_ref[layer] = jnp.transpose(weight)
 
 
 def one_hot(rank_t_ref, layer, slot, rows):
@@ -275,26 +276,24 @@
         load(0)
         greet(place)
         g0.begin()
-        for l in BUFS:
-            route(l, ids_ref, gate_ref, rank_ref, rank_t_ref, gmat_ref, place)
-        g0.lead()
         load(1)
+        route(ids_ref, gate_ref, rank_ref, rank_t_ref, gmat_ref, place)
 
     plan = [
         [],
-        [g0.follow],
-        [g0.lead_onward, g0.last, g1.begin, g0.follow_onward, g0.complete_y, lambda: load(s), g0.last_onward],
+        [g0.lead],
+        [g0.follow, g0.lead_onward, g0.follow_onward, g0.last, g0.complete_y, lambda: load(s), g1.begin],
         [g0.passed_left],
-        [g1.lead, g0.complete_last, g0.passed_right],
-        [g1.follow],
-        [g1.lead_onward, g0.passed_last],
-        [g1.last],
-        [g1.follow_onward],
-        [g1.complete_y, g1.last_onward],
+        [g0.last_onward, g1.lead, g0.passed_right],
+        [g1.follow, g0.complete_last],
+        [g0.passed_last],
+        [g1.lead_onward],
+        [g1.follow_onward, g1.last],
+        [g1.complete_y],
         [],
-        [g1.passed_left],
-        [g1.complete_last, g1.passed_right],
-        [],
+        [g1.last_onward, g1.passed_left],
+        [g1.passed_right],
+        [g1.complete_last],
         [g1.passed_last],
     ]
     for step, parts in enumerate(plan):
@@ -409,11 +408,12 @@
     def start(self):
         self.copies.start(*self.early)
 
-    def onward(self):
-        self.copies.arrive(*self.early)
-        for half, step in enumerate(WAYS):
-            add_to(self.block(step, half), self.first.at[half])
-        self.copies.start(*self.later)
+    def onward(self, *ways):
+        for half in ways or BUFS:
+            self.copies.arrive(self.early[half])
+        for half in ways or BUFS:
+            add_to(self.block(WAYS[half], half), self.first.at[half])
+            self.copies.start(self.later[half])
 
     def finish(self, out):
         self.copies.arrive(*self.later)
@@ -594,7 +594,7 @@
         for k in keys:
             final[k, late].finish()
             puts[k, late].wait()
-        copies.start(*[("pass", n, late) for n in ((0, 1) if "x" in keys else (2,))])
+        copies.start(*[("pass", n, late) for n in ARRAYS if ("xzu"[n] in keys)])
 
     def pass_finish(late):
         keys = [("pass", n, late) for n in ARRAYS]
@@ -623,30 +623,51 @@
         gd_ref[late, theirs] = de_ref[...]
         copies.sent("dense pass")
 
-    spread = [
-        lambda: (copies.start("dense pair"), reduce_onward(3), w_finish()),
-        lambda: (dense_sum(), reduce_finish(3), y_finish(), inner_onward()),
-        lambda: (inner_finish(), cross_onward("x", "z"), dense["y"].onward()),
-        lambda: (cross_finish(1, "x", "z"), cross_onward("u", "l"), dense_next("y", "x")),
-        lambda: (final_onward(1, "x", "z"), cross_finish(1, "u", "l"), dense["x"].onward()),
-        lambda: (final_finish(1, "x", "z"), final_onward(1, "u", "l"), dense_next("x", "z")),
-        lambda: (final_finish(1, "u", "l"), dense["z"].onward()),
-        lambda: (pass_finish(1), dense_pass(1)),
+    before = {2: lambda: on_y["w"].start(), 3: lambda: reduce_onward(0), 5: lambda: (reduce_finish(0), y_start()), 6: lambda: reduce_onward(1), 7: lambda: reduce_onward(2)}
+    middle = {7: lambda: reduce_finish(1)}
+    after = {
+        1: lambda: reduce_start(0),
+        4: lambda: (reduce_start(1), on_y["w"].onward(0)),
+        5: lambda: (reduce_start(2), on_y["w"].onward(1)),
+        7: lambda: reduce_start(3),
+    }
+    late_before = [
+        lambda: copies.start("dense pair"),
+        lambda: reduce_onward(3),
+        lambda: dense["y"].onward(),
+        lambda: (reduce_finish(3), y_finish(), dense_next("y", "x")),
+        lambda: dense["x"].onward(),
+        lambda: dense_next("x", "z"),
+        lambda: dense["z"].onward(),
+        lambda: (final_onward(1, "x", "z", "u", "l"), dense_pass(1)),
     ]
+    late_middle = [
+        lambda: (dense_sum(), reduce_finish(2), y_onward()),
+        lambda: w_finish(),
+        lambda: inner_onward(),
+        lambda: inner_finish(),
+        lambda: cross_onward("x", "z", "u", "l"),
+        lambda: cross_finish(1, "x", "z", "u", "l"),
+        lambda: None,
+        lambda: final_finish(1, "x", "z", "u", "l"),
+    ]
 
     def ending():
+        reduce_finish(2)
+        y_onward()
+        reduce_onward(3)
         dense_finish(1)
+        pass_finish(1)
         copies.start("dense pair")
         w_finish()
-        reduce_onward(3)
         dense_sum()
         inner_onward()
         reduce_finish(3)
+        dense["y"].onward()
         y_finish()
-        dense["y"].onward()
         inner_finish()
+        dense_next("y", "x")
         cross_onward("x", "z")
-        dense_next("y", "x")
         cross_onward("u", "l")
         cross_finish(0, "x", "z")
         dense["x"].onward()
@@ -661,11 +682,14 @@
         pass_finish(0)
         dense_finish(0)
 
-    def at(step, body):
-        pl.when(s == step)(lambda: body() and None)
-
-    def each(step, body):
-        pl.when(t == step)(lambda: body() and None)
+    def hook(index, step, body):
+        pl.when(index == step)(lambda: body() and None)
+
+    def hooks(late, always):
+        for step, body in enumerate(late):
+            hook(s, step + SLOTS, body)
+        for step, body in always.items():
+            hook(t, step, body)
 
     def load_grad(x):
         acc_ref[...] = x.astype(F32)
@@ -676,13 +700,7 @@
         greet(place)
         load_grad(dy_ref[...])
 
-    for step, body in enumerate(spread):
-        at(step + SLOTS, body)
-    each(2, lambda: reduce_onward(0))
-    each(3, lambda: (reduce_finish(0), y_start()))
-    each(5, lambda: reduce_onward(1))
-    each(6, lambda: (reduce_onward(2), reduce_finish(1), on_y["w"].onward()))
-    each(7, lambda: (reduce_finish(2), y_onward()))
+    hooks(late_before, before)
 
     grad_gated = (column(gmat_ref, layer, slot, 0.0) * cur_ref[...].astype(F32)).astype(BF16)
     do = dot(one_hot(rank_t_ref, layer, slot, cap), grad_gated).astype(BF16)
@@ -701,6 +719,7 @@
     def weight_grads():
         return dot_tn(z, da), dot_tn(z, db), dot_tn(h, do)
 
+    hooks(late_middle, middle)
     is_own = functools.reduce(jnp.logical_or, [t == step for step in OWN_STEPS])
 
     @pl.when(jnp.logical_not(is_own))
@@ -733,9 +752,7 @@
         dp_ref[...] = dot_tn(x, grad_b).astype(BF16)
         out_ref[...] = (grad + dot_nt(grad_b, wd_ref[layer])).astype(BF16)
 
-    for step, q in OWN_STEPS.items():
-        each(step, lambda q=q: reduce_start(q))
-    each(1, lambda: on_y["w"].start())
+    hooks([], after)
 
     @pl.when(s == SLOTS - 1)
     def _():
@@ -797,7 +814,7 @@
     def device_step(tok_in, tok_grad, route_ids, gate_vals, w_dense, w_gate, w_up, w_down):
         tokens, top_k = route_ids.shape[1:]
         cap = 2 * tokens * top_k // SLOTS
-        y, x1, *kept = forward(cap, tok_in, route_ids, gate_vals, w_dense, w_gate, w_up, w_down)
+        y, x1, *kept = forward(cap, tok_in, jnp.swapaxes(route_ids, 1, 2), jnp.swapaxes(gate_vals, 1, 2), w_dense, w_gate, w_up, w_down)
         return (y, *backward(cap, tok_grad, tok_in, x1, w_dense, *kept))
 
     return jax.shard_map(device_step, mesh=mesh, in_specs=(tok_spec, tok_spec, route_spec, route_spec, whole_spec, expert_spec, expert_spec, expert_spec), out_specs=(tok_spec, tok_spec, whole_spec, expert_spec, expert_spec, expert_spec), check_vma=False)

time: 316 us -> 284 us (0.90)
  Pallas kernels: 298 us -> 270 us
  local copies, waits for them, and re-layouts: 17.1 us -> 13 us
    pallas_call x1, Pallas kernels: 191 us -> 166 us  [backward(): pl.pallas_call(functools.partial(bwd_kernel, cap), grid=(layers * SLOTS,)...]
    unnamed x16 -> x14, local copies, waits for them, and re-layouts: 17.1 us -> 13 us
    pallas_call x1, Pallas kernels: 107 us -> 104 us  [forward(): pl.pallas_call(functools.partial(fwd_kernel, cap), grid=(layers * SLOTS,)...]
where the time goes in v2:
time: 284 us
  Pallas kernels  270 us (95%)
  local copies, waits for them, and re-layouts  13 us (5%)
    pallas_call x1, Pallas kernels, backward(): pl.pallas_call(functools.partial(bwd_kernel, cap), grid=(layers * SLOTS,)...  166 us
    pallas_call x1, Pallas kernels, forward(): pl.pallas_call(functools.partial(fwd_kernel, cap), grid=(layers * SLOTS,)...  104 us
    unnamed x14, local copies, waits for them, and re-layouts  13 us

profile of v2, /device:TPU:1, one launch (start us, length us, event | category | flops | bytes accessed | tf_op | source)
XLA Modules:
  0.0 283.7 jit_solution(16691506425462514551)
XLA Ops:
  0.6 103.8 %forward.1 = (bf16[1024,384]{1,0:T(8,128)(2,1)}, bf16[1024,384]{1,0:T(8,128)(2,1)}, s32[2,1024,128]{2,1,0:T(8,128)}, s32[2,8,1024]{2,1,0:T(8,128)}, f32[2,1024,1...) custom-call(bf16[1024,384]{1,0:T(8,128)(2,1)} %x0_ref.1, ...), custom_call_target="tpu_custom_call" | custom-call | tf_op jit(solution)/shard_map/forward/pallas_call | solution.py:362
  104.5 0.0 copy-start.3
  104.5 166.2 %backward.1 = (bf16[1024,384]{1,0:T(8,128)(2,1)}, bf16[2,384,384]{2,1,0:T(8,128)(2,1)}, bf16[2,2,384,1024]{3,2,1,0:T(8,128)(2,1)}, bf16[2,2,384,1024]{3,2,1,0:T(8,128)(2,1)}, bf16[2,2,1024,384]{3,2,1,0:T(8,128)(2,1)}) custom-call(bf16[1024,384]{1,0:T(8,128)(2,1)} %dy_ref.1, bf16[1024,384]{1,0:T(8,128)(2,1)} %x0_ref.1, ...), custom_call_target="tpu_custom_call" | custom-call | tf_op jit(solution)/shard_map/backward/pallas_call | solution.py:796
  270.7 0.0 copy-start.2
  270.7 0.0 copy-done.3
  270.7 0.9 copy.20
  271.6 2.4 copy.21
  274.0 1.9 copy.22
  276.0 0.0 copy-done.2
  276.0 0.0 copy-start.1
  276.0 1.7 copy.23
  277.6 1.4 copy-done.1
  279.0 0.0 copy-start
  279.0 1.7 copy.24
  280.7 1.4 copy-done
  282.0 1.7 copy.25
Async XLA Ops:
  104.5 166.3 %copy-start.3 = (bf16[1024,384]{1,0:T(8,128)(2,1)S(1)}, bf16[1024,384]{1,0:T(8,128)(2,1)}, u32[]{:S(2)}) copy-start(bf16[1024,384]{1,0:T(8,128)(2,1)} %get-tuple-element.44) | copy-start | bytes 2359300
  270.7 5.3 %copy-start.2 = (bf16[2,2,384,1024]{3,2,1,0:T(8,128)(2,1)S(1)}, bf16[2,2,384,1024]{3,2,1,0:T(8,128)(2,1)}, u32[]{:S(2)}) copy-start(bf16[2,2,384,1024]{3,2,1,0:T(8,128)(2,1)} %get-tuple-element.47) | copy-start | bytes 9437188
  276.0 3.0 %copy-start.1 = (bf16[2,2,384,1024]{3,2,1,0:T(8,128)(2,1)S(1)}, bf16[2,2,384,1024]{3,2,1,0:T(8,128)(2,1)}, u32[]{:S(2)}) copy-start(bf16[2,2,384,1024]{3,2,1,0:T(8,128)(2,1)} %get-tuple-element.48) | copy-start | bytes 9437188
  279.0 3.0 %copy-start = (bf16[2,2,1024,384]{3,2,1,0:T(8,128)(2,1)S(1)}, bf16[2,2,1024,384]{3,2,1,0:T(8,128)(2,1)}, u32[]{:S(2)}) copy-start(bf16[2,2,1024,384]{3,2,1,0:T(8,128)(2,1)} %get-tuple-element.49) | copy-start | bytes 9437188

commit v3 on v2

--- a/solution.py
+++ b/solution.py
@@ -74,10 +74,6 @@
     def sent(self, *keys):
         for key in keys:
             self.made[key].wait_send()
-
-    def drain(self):
-        for copy in self.made.values():
-            copy.wait_send()
 
 
 def greet(place):
@@ -198,11 +194,11 @@
 GATHER_COPIES = 2 * (2 * 2 * (3 + 3 * 4) + 9)
 
 
-def route(ids_ref, gate_ref, rank_ref, rank_t_ref, gmat_ref, place):
+def route(ids_ref, gate_ref, rows_ref, columns_ref, place):
     layers, _, tokens = ids_ref.shape
     below = lax.broadcasted_iota(jnp.int32, (tokens, tokens), 0) < lax.broadcasted_iota(jnp.int32, (tokens, tokens), 1)
     below = jnp.where(below, 1.0, 0.0).astype(BF16)
-    lead = lax.broadcasted_iota(jnp.int32, (LANES, tokens), 0)
+    lead = lax.broadcasted_iota(jnp.int32, (2 * SLOTS, tokens), 0)
     for layer in range(layers):
         ids, gates = ids_ref[layer], gate_ref[layer]
         off = ((ids >> 1) - place.y) & (SIDE - 1)
@@ -211,186 +207,24 @@
         hits = [slot[n : n + 1] == lead for n in BUFS]
         hit = hits[0] | hits[1]
         weight = jnp.where(hits[0], gates[0:1], 0.0) + jnp.where(hits[1], gates[1:2], 0.0)
-        count = dot(jnp.where(hit, 1.0, 0.0)[: 2 * SLOTS].astype(BF16), below)
-        rank = jnp.where(hit, jnp.concatenate([count, jnp.zeros((LANES - 2 * SLOTS, tokens), F32)], axis=0), -1.0)
-        rank_t_ref[layer] = rank[:SLOTS].astype(jnp.int32)
-        rank_ref[layer] = jnp.transpose(rank).astype(jnp.int32)
-        gmat_ref[layer] = jnp.transpose(weight)
-
-
-def one_hot(rank_t_ref, layer, slot, rows):
-    tokens = rank_t_ref.shape[2]
-    place = lax.broadcasted_iota(jnp.int32, (rows, tokens), 0)
-    return jnp.where(rank_t_ref[layer, pl.ds(slot, 1), :] == place, 1.0, 0.0).astype(BF16)
-
-
-def column(ref, layer, slot, zero):
-    tokens = ref.shape[1]
-    lane = lax.broadcasted_iota(jnp.int32, (tokens, LANES), 1)
-    return jnp.sum(jnp.where(lane == slot, ref[layer], zero), axis=1, keepdims=True)
-
-
-def one_hot_t(rank_ref, layer, slot, rows):
-    tokens = rank_ref.shape[1]
-    place = lax.broadcasted_iota(jnp.int32, (tokens, rows), 1)
-    return jnp.where(column(rank_ref, layer, slot, jnp.int32(0)) == place, 1.0, 0.0).astype(BF16)
-
-
-def fwd_kernel(cap, x_ref, ids_ref, gate_ref, wd_ref, o1_ref, o3_ref, o2_ref, y_ref, x1_ref, rank_ref, rank_t_ref, gmat_ref, g1_ref, g3_ref, g2_ref, z_ref, a_ref, b_ref, u_ref, acc_ref, b1_ref, b3_ref, b2_ref, load_sem, keep_sem, send_sem, recv_sem):
-    s = pl.program_id(0)
-    steps = pl.num_programs(0)
-    layer, slot = s // SLOTS, s % SLOTS
-    place = Place()
-    copies = Copies(place, send_sem, recv_sem)
-    own, whole, bufs = (o1_ref, o3_ref, o2_ref), (g1_ref, g3_ref, g2_ref), (b1_ref, b3_ref, b2_ref)
-    g0, g1 = (Gather(l, copies, place, own, whole) for l in BUFS)
-
-    def at(step, body):
-        pl.when(s == step)(body)
-
-    def loads(step, mine):
-        l, k = step // SLOTS, step % SLOTS
-        for n in ARRAYS:
-            src = own[n].at[l, (place.c + k) % 2] if mine else whole[n].at[l, k]
-            yield pltpu.make_async_copy(src, bufs[n].at[step % 2], load_sem.at[step % 2, n])
-
-    def keeps(step):
-        for n in ARRAYS:
-            yield pltpu.make_async_copy(bufs[n].at[step % 2], whole[n].at[step // SLOTS, step % SLOTS], keep_sem.at[step % 2, n])
-
-    def load(step):
-        k = step % SLOTS
-
-        @pl.when(k < 2)
-        def _():
-            for copy in loads(step, True):
-                copy.start()
-
-        @pl.when(k >= 2)
-        def _():
-            for copy in loads(step, False):
-                copy.start()
-
-    @pl.when(s == 0)
-    def _():
-        load(0)
-        greet(place)
-        g0.begin()
-        load(1)
-        route(ids_ref, gate_ref, rank_ref, rank_t_ref, gmat_ref, place)
-
-    plan = [
-        [],
-        [g0.lead],
-        [g0.follow, g0.lead_onward, g0.follow_onward, g0.last, g0.complete_y, lambda: load(s), g1.begin],
-        [g0.passed_left],
-        [g0.last_onward, g1.lead, g0.passed_right],
-        [g1.follow, g0.complete_last],
-        [g0.passed_last],
-        [g1.lead_onward],
-        [g1.follow_onward, g1.last],
-        [g1.complete_y],
-        [],
-        [g1.last_onward, g1.passed_left],
-        [g1.passed_right],
-        [g1.complete_last],
-        [g1.passed_last],
-    ]
-    for step, parts in enumerate(plan):
-
-        @pl.when(s == step)
-        def _(parts=parts):
-            for part in parts:
-                part()
-
-    for copy in loads(s, False):
-        copy.wait()
-
-    @pl.when((s > 0) & (s != 1) & (s < steps - 1))
-    def _():
-        load(s + 1)
-
-    @pl.when(slot < 2)
-    def _():
-        for copy in keeps(s):
-            copy.start()
-
-    def enter(x):
-        u_ref[...] = (x.astype(F32) + dot(x, wd_ref[layer])).astype(BF16)
-        acc_ref[...] = jnp.zeros_like(acc_ref)
-
-    at(0, lambda: enter(x_ref[...]))
-    at(SLOTS, lambda: enter(x1_ref[...]))
-
-    buf = s % 2
-    z = dot(one_hot(rank_t_ref, layer, slot, cap), u_ref[...]).astype(BF16)
-    z_ref[0, 0] = z
-    a = dot(z, b1_ref[buf]).astype(BF16)
-    b = dot(z, b3_ref[buf]).astype(BF16)
-    a_ref[0, 0] = a
-    b_ref[0, 0] = b
-    h = (jax.nn.silu(a.astype(F32)) * b.astype(F32)).astype(BF16)
-    o = dot(h, b2_ref[buf]).astype(BF16)
-    acc_ref[...] += column(gmat_ref, layer, slot, 0.0) * dot(one_hot_t(rank_ref, layer, slot, cap), o)
-
-    def leave(out_ref):
-        out_ref[...] = (u_ref[...].astype(F32) + acc_ref[...]).astype(BF16)
-
-    @pl.when(slot < 2)
-    def _():
-        for copy in keeps(s):
-            copy.wait()
-
-    at(SLOTS - 1, lambda: leave(x1_ref))
-
-    @pl.when(s == steps - 1)
-    def _():
-        leave(y_ref)
-        copies.drain()
-
-
-def forward(cap, x, ids, gates, wd, w1, w3, w2):
-    tokens, width = x.shape
-    layers, _, ff = ids.shape[0], None, w1.shape[3]
-    vmem = pl.BlockSpec(memory_space=pltpu.VMEM)
-    hbm = pl.BlockSpec(memory_space=pl.ANY)
-
-    def saved(n):
-        return pl.BlockSpec((1, 1, cap, n), lambda s: (s // SLOTS, s % SLOTS, 0, 0))
-
-    shape = jax.ShapeDtypeStruct
-    return pl.pallas_call(
-        functools.partial(fwd_kernel, cap),
-        grid=(layers * SLOTS,),
-        in_specs=[vmem] * 4 + [hbm] * 3,
-        out_specs=[vmem] * 5 + [hbm] * 3 + [saved(width), saved(ff), saved(ff)],
-        out_shape=[
-            shape((tokens, width), BF16),
-            shape((tokens, width), BF16),
-            shape((layers, tokens, LANES), jnp.int32),
-            shape((layers, SLOTS, tokens), jnp.int32),
-            shape((layers, tokens, LANES), F32),
-            shape((layers, SLOTS, width, ff), BF16),
-            shape((layers, SLOTS, width, ff), BF16),
-            shape((layers, SLOTS, ff, width), BF16),
-            shape((layers, SLOTS, cap, width), BF16),
-            shape((layers, SLOTS, cap, ff), BF16),
-            shape((layers, SLOTS, cap, ff), BF16),
-        ],
-        scratch_shapes=[
-            pltpu.VMEM((tokens, width), BF16),
-            pltpu.VMEM((tokens, width), F32),
-            pltpu.VMEM((2, width, ff), BF16),
-            pltpu.VMEM((2, width, ff), BF16),
-            pltpu.VMEM((2, ff, width), BF16),
-            pltpu.SemaphoreType.DMA((2, 3)),
-            pltpu.SemaphoreType.DMA((2, 3)),
-            pltpu.SemaphoreType.DMA((GATHER_COPIES,)),
-            pltpu.SemaphoreType.DMA((GATHER_COPIES,)),
-        ],
-        compiler_params=pltpu.CompilerParams(vmem_limit_bytes=VMEM_LIMIT, collective_id=0, has_side_effects=True),
-        name="forward",
-    )(x, ids, gates, wd, w1, w3, w2)
+        rank = jnp.where(hit, dot(jnp.where(hit, 1.0, 0.0).astype(BF16), below), -1.0)
+        rows_ref[layer] = rank[:SLOTS].astype(jnp.int32)
+        columns_ref[layer] = jnp.transpose(jnp.concatenate([rank[:SLOTS], weight[:SLOTS], jnp.zeros((LANES - 2 * SLOTS, tokens), F32)], axis=0))
+
+
+def one_hot(rows_ref, layer, slot, cap):
+    place = lax.broadcasted_iota(jnp.int32, (cap, rows_ref.shape[2]), 0)
+    return jnp.where(rows_ref[layer, pl.ds(slot, 1), :] == place, 1.0, 0.0).astype(BF16)
+
+
+def column(columns_ref, layer, index):
+    lane = lax.broadcasted_iota(jnp.int32, columns_ref.shape[1:], 1)
+    return jnp.sum(jnp.where(lane == index, columns_ref[layer], 0.0), axis=1, keepdims=True)
+
+
+def one_hot_t(columns_ref, layer, slot, cap):
+    place = lax.broadcasted_iota(jnp.int32, (columns_ref.shape[1], cap), 1)
+    return jnp.where(column(columns_ref, layer, slot).astype(jnp.int32) == place, 1.0, 0.0).astype(BF16)
 
 
 def add_to(dst, src):
@@ -408,17 +242,17 @@
     def start(self):
         self.copies.start(*self.early)
 
-    def onward(self, *ways):
-        for half in ways or BUFS:
-            self.copies.arrive(self.early[half])
-        for half in ways or BUFS:
+    def onward(self):
+        self.copies.arrive(*self.early)
+        for half in BUFS:
             add_to(self.block(WAYS[half], half), self.first.at[half])
             self.copies.start(self.later[half])
+        self.copies.sent(*self.early)
 
     def finish(self, out):
         self.copies.arrive(*self.later)
         out[...] = (self.block(0, None)[...].astype(F32) + self.second[0].astype(F32) + self.second[1].astype(F32)).astype(BF16)
-        self.copies.sent(*self.early, *self.later)
+        self.copies.sent(*self.later)
 
 
 class RingSpread:
@@ -471,21 +305,23 @@
 
 OWN_STEPS = {1: 0, 4: 1, 5: 2, 7: 3}
 REDUCE_COPIES = 107
-
-
-def bwd_kernel(cap, dy_ref, x0_ref, x1_ref, wd_ref, rank_ref, rank_t_ref, gmat_ref, w1_ref, w3_ref, w2_ref, z_ref, a_ref, b_ref, dx_ref, gd_ref, g1_ref, g3_ref, g2_ref, acc_ref, cur_ref, m1_ref, m3_ref, m2_ref, d1_ref, d3_ref, d2_ref, s1_ref, s3_ref, s2_ref, r11_ref, r12_ref, r31_ref, r32_ref, t1_ref, t3_ref, y11_ref, y12_ref, y31_ref, y32_ref, y21_ref, y22_ref, u1_ref, u2_ref, l1_ref, l2_ref, c1_ref, c3_ref, cu_ref, cl_ref, f1_ref, f3_ref, fu_ref, fl_ref, dp_ref, dr_ref, dcx_ref, dcy_ref, dcz_ref, ds_ref, de_ref, put_sem, send_sem, recv_sem, credit):
+LAST, LATE, DEFER, STEPS = 2 * SLOTS, 3 * SLOTS, 4 * SLOTS, 5 * SLOTS
+
+
+def kernel(cap, x0_ref, dy_ref, ids_ref, gate_ref, wd_ref, o1_ref, o3_ref, o2_ref, y_ref, dx_ref, gd_ref, g1_ref, g3_ref, g2_ref, h1_ref, h3_ref, h2_ref, kz_ref, ka_ref, kb_ref, kda_ref, kdb_ref, acc_ref, cur_ref, x1_ref, rows_ref, columns_ref, w1_ref, w3_ref, w2_ref, z_ref, a_ref, b_ref, m1_ref, m3_ref, m2_ref, d1_ref, d3_ref, d2_ref, s1_ref, s3_ref, s2_ref, r11_ref, r12_ref, r31_ref, r32_ref, t1_ref, t3_ref, y11_ref, y12_ref, y31_ref, y32_ref, y21_ref, y22_ref, u1_ref, u2_ref, l1_ref, l2_ref, c1_ref, c3_ref, cu_ref, cl_ref, f1_ref, f3_ref, fu_ref, fl_ref, dp_ref, dr_ref, dcx_ref, dcy_ref, dcz_ref, ds_ref, de_ref, put_sem, load_sem, keep_sem, save_sem, gsend_sem, grecv_sem, send_sem, recv_sem, credit):
     s = pl.program_id(0)
-    steps = pl.num_programs(0)
-    layer, slot, t = 1 - s // SLOTS, SLOTS - 1 - s % SLOTS, s % SLOTS
-    group = t // 4 + t // 5 + t // 7
-    into = (t // 2 + t // 3) % 2
     place = Place()
+    gathers = Copies(place, gsend_sem, grecv_sem)
     copies = Copies(place, send_sem, recv_sem)
+    given, whole, bufs = (o1_ref, o3_ref, o2_ref), (h1_ref, h3_ref, h2_ref), (w1_ref, w3_ref, w2_ref)
+    kept, acts = (kz_ref, ka_ref, kb_ref), (z_ref, a_ref, b_ref)
+    deferred = (kda_ref, kdb_ref)
+    g0, g1 = (Gather(l, gathers, place, given, whole) for l in BUFS)
     rows, ff = s1_ref.shape[1], s2_ref.shape[1]
     quarter, part = rows // SIDE, ff // 2 // SIDE
     half_d = rows // 2
 
-    stage, mate, own = (m1_ref, m3_ref, m2_ref), (d1_ref, d3_ref, d2_ref), (s1_ref, s3_ref, s2_ref)
+    stage, mate, mine_of = (m1_ref, m3_ref, m2_ref), (d1_ref, d3_ref, d2_ref), (s1_ref, s3_ref, s2_ref)
     outs = (g1_ref, g3_ref, g2_ref)
     for buf in BUFS:
         for n in ARRAYS:
@@ -623,167 +459,260 @@
         gd_ref[late, theirs] = de_ref[...]
         copies.sent("dense pass")
 
-    before = {2: lambda: on_y["w"].start(), 3: lambda: reduce_onward(0), 5: lambda: (reduce_finish(0), y_start()), 6: lambda: reduce_onward(1), 7: lambda: reduce_onward(2)}
-    middle = {7: lambda: reduce_finish(1)}
-    after = {
-        1: lambda: reduce_start(0),
-        4: lambda: (reduce_start(1), on_y["w"].onward(0)),
-        5: lambda: (reduce_start(2), on_y["w"].onward(1)),
-        7: lambda: reduce_start(3),
-    }
-    late_before = [
-        lambda: copies.start("dense pair"),
-        lambda: reduce_onward(3),
-        lambda: dense["y"].onward(),
-        lambda: (reduce_finish(3), y_finish(), dense_next("y", "x")),
-        lambda: dense["x"].onward(),
-        lambda: dense_next("x", "z"),
-        lambda: dense["z"].onward(),
-        lambda: (final_onward(1, "x", "z", "u", "l"), dense_pass(1)),
-    ]
-    late_middle = [
-        lambda: (dense_sum(), reduce_finish(2), y_onward()),
-        lambda: w_finish(),
-        lambda: inner_onward(),
-        lambda: inner_finish(),
-        lambda: cross_onward("x", "z", "u", "l"),
-        lambda: cross_finish(1, "x", "z", "u", "l"),
-        lambda: None,
-        lambda: final_finish(1, "x", "z", "u", "l"),
-    ]
+    def copy(src, dst, sem):
+        return pltpu.make_async_copy(src, dst, sem)
+
+    def weights(step, layer, slot, arrays, buf, is_given=False):
+        for n in arrays:
+            src = given[n].at[layer, (place.c + slot) % 2] if is_given else whole[n].at[layer, slot]
+            yield copy(src, bufs[n].at[buf], load_sem.at[buf, n])
+
+    def saved(layer, slot, buf):
+        for n in ARRAYS:
+            yield copy(kept[n].at[layer, slot], acts[n].at[buf], load_sem.at[buf, 3 + n])
+
+    def loads(step, do):
+        forth, back = step % 2, (step + 1) % 2
+        slot = step % SLOTS
+        rest = SLOTS - 1 - slot
+
+        def run(when, items):
+            @pl.when(when)
+            def _():
+                for item in items():
+                    do(item)
+
+        run((step < LAST) & (slot < 2), lambda: weights(step, step // SLOTS, slot, ARRAYS, forth, True))
+        run((step < LAST) & (slot >= 2), lambda: weights(step, step // SLOTS, slot, ARRAYS, forth))
+        run((step > LAST) & (step < LATE), lambda: [*weights(step, 1, rest, ARRAYS, back), *saved(1, rest, back)])
+        run((step >= LATE) & (step < DEFER), lambda: [*weights(step, 0, rest, [2], back), *saved(0, rest, back)])
+        run((step >= DEFER) & (step < STEPS), lambda: [*weights(step, 0, rest, BUFS, back)] + [copy(deferred[n].at[rest], acts[n + 1].at[back], load_sem.at[back, 4 + n]) for n in BUFS])
+
+    def load(step):
+        loads(step, lambda item: item.start())
+
+    def keeps(step):
+        return [copy(bufs[n].at[step % 2], whole[n].at[step // SLOTS, step % SLOTS], keep_sem.at[step % 2, n]) for n in ARRAYS]
+
+    def saves(step):
+        return [copy(acts[n].at[step % 2], kept[n].at[step // SLOTS, step % SLOTS], save_sem.at[step % 2, n]) for n in ARRAYS]
+
+    def defers(step):
+        return [copy(acts[n + 1].at[2], deferred[n].at[SLOTS - 1 - step % SLOTS], save_sem.at[0, n]) for n in BUFS]
+
+    def wait(items):
+        for item in items:
+            item.wait()
+
+    def start(items):
+        for item in items:
+            item.start()
 
     def ending():
-        reduce_finish(2)
-        y_onward()
-        reduce_onward(3)
-        dense_finish(1)
+        inner_onward()
+        dense_sum()
+        inner_finish()
+        y_finish()
+        dense["y"].onward()
         pass_finish(1)
-        copies.start("dense pair")
-        w_finish()
-        dense_sum()
-        inner_onward()
-        reduce_finish(3)
-        dense["y"].onward()
-        y_finish()
-        inner_finish()
+        pl.semaphore_signal(credit.at[2], inc=1, device_id=place.at("c", 0), device_id_type=MESH)
+        cross_onward("u", "l")
         dense_next("y", "x")
         cross_onward("x", "z")
-        cross_onward("u", "l")
+        cross_finish(0, "u", "l")
+        dense["x"].onward()
         cross_finish(0, "x", "z")
-        dense["x"].onward()
-        cross_finish(0, "u", "l")
+        final_onward(0, "u", "l")
+        dense_next("x", "z")
         final_onward(0, "x", "z")
-        dense_next("x", "z")
-        final_onward(0, "u", "l")
+        pl.semaphore_wait(credit.at[2], 1)
+        final_finish(0, "u", "l")
+        dense["z"].onward()
         final_finish(0, "x", "z")
-        dense["z"].onward()
-        final_finish(0, "u", "l")
         dense_pass(0)
         pass_finish(0)
         dense_finish(0)
 
-    def hook(index, step, body):
-        pl.when(index == step)(lambda: body() and None)
-
-    def hooks(late, always):
-        for step, body in enumerate(late):
-            hook(s, step + SLOTS, body)
-        for step, body in always.items():
-            hook(t, step, body)
-
-    def load_grad(x):
-        acc_ref[...] = x.astype(F32)
-        cur_ref[...] = x
+    before, middle, after = {}, {}, {}
+
+    def plan(table, first, *stages):
+        for n, stage in enumerate(stages):
+            table.setdefault(first + n, []).extend(stage)
+
+    on, done = lambda q: lambda: reduce_onward(q), lambda q: lambda: reduce_finish(q)
+    plan(before, 1, [g0.lead], [g0.follow, g0.lead_onward, g0.follow_onward, g0.last, g0.complete_y, lambda: load(s), g1.begin], [g0.passed_left])
+    plan(before, 4, [g0.last_onward, g1.lead, g0.passed_right], [g1.follow, g0.complete_last], [g0.passed_last], [g1.lead_onward])
+    plan(before, SLOTS, [g1.follow_onward, g1.last], [g1.complete_y], [], [g1.last_onward, g1.passed_left], [g1.passed_right], [g1.complete_last], [g1.passed_last])
+    plan(before, LAST + 2, [on_y["w"].start], [on(0)], [], [done(0), y_start], [on(1), on_y["w"].onward], [on(2)])
+    plan(middle, LATE - 1, [done(1)])
+    plan(before, LATE, [lambda: copies.start("dense pair")], [on(3)], [dense["y"].onward], [], [inner_onward], [y_finish], [], [lambda: cross_onward("x", "z")])
+    plan(middle, LATE, [dense_sum, done(2), y_onward], [], [w_finish], [done(3), lambda: dense_next("y", "x")], [], [inner_finish, dense["x"].onward], [], [lambda: cross_onward("u", "l"), lambda: dense_next("x", "z")])
+    plan(before, DEFER + 1, [lambda: cross_finish(1, "x", "z", "u", "l")], [dense["z"].onward], [], [lambda: dense_pass(1)], [lambda: final_onward(1, "x", "z", "u", "l")], [], [lambda: final_finish(1, "x", "z", "u", "l"), lambda: dense_finish(1)])
+    plan(after, LATE + 2, [on_y["w"].start])
+    plan(before, LATE + 4, [on(0)], [], [done(0), y_start, on_y["w"].onward], [on(1)], [on(2)], [], [done(1)], [on(3)], [done(2), y_onward], [], [w_finish], [done(3)])
+    for base in (LAST, LATE):
+        for step, q in OWN_STEPS.items():
+            plan(after, base + step, [lambda q=q: reduce_start(q)])
+
+    def hooks(table):
+        for step, stages in sorted(table.items()):
+
+            @pl.when(s == step)
+            def _(stages=stages):
+                for stage in stages:
+                    stage()
+
+    is_forward, is_back = s < LAST, (s >= LAST) & (s < DEFER)
+    forth, back = s % 2, (s + 1) % 2
+    t = s % SLOTS
 
     @pl.when(s == 0)
     def _():
+        load(0)
         greet(place)
-        load_grad(dy_ref[...])
-
-    hooks(late_before, before)
-
-    grad_gated = (column(gmat_ref, layer, slot, 0.0) * cur_ref[...].astype(F32)).astype(BF16)
-    do = dot(one_hot(rank_t_ref, layer, slot, cap), grad_gated).astype(BF16)
-    dh = dot_nt(do, w2_ref[0, 0])
-    a = a_ref[0, 0].astype(F32)
-    b = b_ref[0, 0].astype(F32)
-    sig = jax.nn.sigmoid(a)
-    act = a * sig
-    h = (act * b).astype(BF16)
-    db = (dh * act).astype(BF16)
-    da = (dh * b * sig * (1.0 + a * (1.0 - sig))).astype(BF16)
-    z = z_ref[0, 0]
-    dz = (dot_nt(da, w1_ref[0, 0]) + dot_nt(db, w3_ref[0, 0])).astype(BF16)
-    acc_ref[...] += dot(one_hot_t(rank_ref, layer, slot, cap), dz)
-
-    def weight_grads():
-        return dot_tn(z, da), dot_tn(z, db), dot_tn(h, do)
-
-    hooks(late_middle, middle)
-    is_own = functools.reduce(jnp.logical_or, [t == step for step in OWN_STEPS])
-
-    @pl.when(jnp.logical_not(is_own))
+        g0.begin()
+        load(1)
+        route(ids_ref, gate_ref, rows_ref, columns_ref, place)
+
+    hooks(before)
+    loads(s, lambda item: item.wait())
+    pl.when((s > 1) & (s <= LAST))(lambda: wait(saves(s - 2)))
+    pl.when((s > LATE) & (s <= DEFER))(lambda: wait(defers(s - 1)))
+    pl.when((s > 0) & (s != 1) & (s != LAST - 1))(lambda: load(s + 1))
+    pl.when(is_forward & (t < 2))(lambda: start(keeps(s)))
+
+    def enter(x):
+        cur_ref[...] = (x.astype(F32) + dot(x, wd_ref[s // SLOTS])).astype(BF16)
+        acc_ref[...] = jnp.zeros_like(acc_ref)
+
+    def enter_back(x):
+        cur_ref[...] = x
+        acc_ref[...] = x.astype(F32)
+
+    pl.when(s == 0)(lambda: enter(x0_ref[...]))
+    pl.when(s == SLOTS)(lambda: enter(x1_ref[...]))
+    pl.when(s == LAST)(lambda: enter_back(dy_ref[...]))
+
+    @pl.when(is_forward)
     def _():
-        for buf in BUFS:
-            pl.when((s > 0) & (into == 1 - buf))(lambda buf=buf: copies.sent(*[("pair", buf, n) for n in ARRAYS]))
-
-        for ref, grad in zip(stage, weight_grads()):
-            ref[...] = grad.astype(BF16)
-
-        pl.when(s >= 3)(lambda: pl.semaphore_wait(credit.at[into], 1))
-        for buf in BUFS:
-            pl.when(into == buf)(lambda buf=buf: copies.start(*[("pair", buf, n) for n in ARRAYS]))
-
-    @pl.when(is_own)
+        layer, slot = s // SLOTS, t
+        z = dot(one_hot(rows_ref, layer, slot, cap), cur_ref[...]).astype(BF16)
+        z_ref[forth] = z
+        a = dot(z, w1_ref[forth]).astype(BF16)
+        b = dot(z, w3_ref[forth]).astype(BF16)
+        a_ref[forth] = a
+        b_ref[forth] = b
+        h = (jax.nn.silu(a.astype(F32)) * b.astype(F32)).astype(BF16)
+        o = dot(h, w2_ref[forth]).astype(BF16)
+        acc_ref[...] += column(columns_ref, layer, SLOTS + slot) * dot(one_hot_t(columns_ref, layer, slot, cap), o)
+        pl.when(s < LAST - 1)(lambda: start(saves(s)))
+        pl.when(t < 2)(lambda: wait(keeps(s)))
+
+    def leave(out_ref):
+        out_ref[...] = (cur_ref[...].astype(F32) + acc_ref[...]).astype(BF16)
+
+    pl.when(s == SLOTS - 1)(lambda: leave(x1_ref))
+    pl.when(s == LAST - 1)(lambda: leave(y_ref))
+
+    @pl.when(is_back)
     def _():
-        for buf in BUFS:
-            pl.when(group % 2 == buf)(lambda buf=buf: copies.arrive(*[("pair", buf, n) for n in ARRAYS]))
-
-        for ref, add, grad in zip(own, mate, weight_grads()):
-            ref[group] = (grad + add[group % 2].astype(F32)).astype(BF16)
-
-        @pl.when(s < 13)
+        layer, slot = 1 - (s - LAST) // SLOTS, SLOTS - 1 - t
+        grad_gated = (column(columns_ref, layer, SLOTS + slot) * cur_ref[...].astype(F32)).astype(BF16)
+        do = dot(one_hot(rows_ref, layer, slot, cap), grad_gated).astype(BF16)
+        dh = dot_nt(do, w2_ref[back])
+        a = a_ref[back].astype(F32)
+        b = b_ref[back].astype(F32)
+        sig = jax.nn.sigmoid(a)
+        act = a * sig
+        h = (act * b).astype(BF16)
+        db = (dh * act).astype(BF16)
+        da = (dh * b * sig * (1.0 + a * (1.0 - sig))).astype(BF16)
+        a_ref[2] = da
+        b_ref[2] = db
+        z = z_ref[back]
+        pl.when(s >= LATE)(lambda: start(defers(s)))
+        hooks(middle)
+
+        def weight_grads():
+            return dot_tn(z, da), dot_tn(z, db), dot_tn(h, do)
+
+        is_own = functools.reduce(jnp.logical_or, [t == step for step in OWN_STEPS])
+        group = t // 4 + t // 5 + t // 7
+        into = (t // 2 + t // 3) % 2
+
+        @pl.when(jnp.logical_not(is_own))
         def _():
-            pl.semaphore_signal(credit.at[group % 2], inc=1, device_id=place.at("c", 0), device_id_type=MESH)
-
-    def leave(x, out_ref):
+            for buf in BUFS:
+                pl.when((s > LAST) & (into == 1 - buf))(lambda buf=buf: copies.sent(*[("pair", buf, n) for n in ARRAYS]))
+
+            for ref, grad in zip(stage, weight_grads()):
+                ref[...] = grad.astype(BF16)
+
+            pl.when(s >= LAST + 3)(lambda: pl.semaphore_wait(credit.at[into], 1))
+            for buf in BUFS:
+                pl.when(into == buf)(lambda buf=buf: copies.start(*[("pair", buf, n) for n in ARRAYS]))
+
+        @pl.when(is_own)
+        def _():
+            for buf in BUFS:
+                pl.when(group % 2 == buf)(lambda buf=buf: copies.arrive(*[("pair", buf, n) for n in ARRAYS]))
+
+            for ref, add, grad in zip(mine_of, mate, weight_grads()):
+                ref[group] = (grad + add[group % 2].astype(F32)).astype(BF16)
+
+            @pl.when(s < DEFER - 3)
+            def _():
+                pl.semaphore_signal(credit.at[group % 2], inc=1, device_id=place.at("c", 0), device_id_type=MESH)
+
+    @pl.when(((s >= LAST) & (s < LATE)) | (s >= DEFER))
+    def _():
+        layer, slot = s // LATE * -1 + 1, SLOTS - 1 - t
+        src = back - (s // DEFER - 1) * (2 - back)
+        dz = (dot_nt(a_ref[src], w1_ref[back]) + dot_nt(b_ref[src], w3_ref[back])).astype(BF16)
+        acc_ref[...] += dot(one_hot_t(columns_ref, layer, slot, cap), dz)
+
+    def leave_back(layer, x, out_ref):
         grad = acc_ref[...]
         grad_b = grad.astype(BF16)
         dp_ref[...] = dot_tn(x, grad_b).astype(BF16)
         out_ref[...] = (grad + dot_nt(grad_b, wd_ref[layer])).astype(BF16)
 
-    hooks([], after)
-
-    @pl.when(s == SLOTS - 1)
+    @pl.when(s == LATE - 1)
     def _():
-        leave(x1_ref[...], cur_ref)
+        leave_back(1, x1_ref[...], cur_ref)
         acc_ref[...] = cur_ref[...].astype(F32)
 
-    @pl.when(s == steps - 1)
+    hooks(after)
+
+    @pl.when(s == STEPS - 1)
     def _():
-        leave(x0_ref[...], dx_ref)
+        leave_back(0, x0_ref[...], dx_ref)
+        copies.start("dense pair")
         ending()
         copies.sent(*[("pair", 1, n) for n in ARRAYS])
-
-
-def backward(cap, dy, x0, x1, wd, rank, rank_t, gmat, w1, w3, w2, z, a, b):
+        gathers.sent(*gathers.made)
+
+
+def step(cap, x0, dy, ids, gates, wd, w1, w3, w2):
     tokens, width = dy.shape
-    layers, ff = w1.shape[0], w1.shape[3]
-    local, quarter, part = SLOTS // SIDE, width // SIDE, ff // 2 // SIDE
+    layers, local, _, ff = w1.shape
+    quarter, part = width // SIDE, ff // 2 // SIDE
     hbm = pl.BlockSpec(memory_space=pl.ANY)
 
     def fixed(shape):
         return pl.BlockSpec(shape, lambda s: (0,) * len(shape), pipeline_mode=pl.Buffered(1))
 
-    def stream(*shape):
-        return pl.BlockSpec((1, 1, *shape), lambda s: (1 - s // SLOTS, SLOTS - 1 - s % SLOTS, 0, 0))
-
     def buf(*shape):
         return pltpu.VMEM(shape, BF16)
 
+    def dma(*shape):
+        return pltpu.SemaphoreType.DMA(shape)
+
     shape = jax.ShapeDtypeStruct
     ups, downs = [(width, ff), (width, ff), (ff, width)], [(quarter, ff), (part, width)]
-    scratch = [pltpu.VMEM((tokens, width), F32), buf(tokens, width)]
+    acts = [(cap, width), (cap, ff), (cap, ff)]
+    scratch = [pltpu.VMEM((tokens, width), F32), buf(tokens, width), buf(tokens, width), pltpu.VMEM((layers, SLOTS, tokens), jnp.int32), pltpu.VMEM((layers, tokens, LANES), F32)]
+    scratch += [buf(2, *u) for u in ups] + [buf(2, *acts[0]), buf(3, *acts[1]), buf(3, *acts[2])]
     scratch += [buf(*u) for u in ups] + [buf(2, *u) for u in ups] + [buf(SIDE, *u) for u in ups]
     scratch += [buf(SIDE, 2, quarter // 2, ff), buf(SIDE, 2, quarter, ff)] * 2
     scratch += [buf(SIDE, quarter, ff)] * 2
@@ -792,17 +721,19 @@
     scratch += [buf(SIDE, quarter, ff)] * 2 + [buf(SIDE, part, width)] * 2
     scratch += [buf(quarter, ff)] * 2 + [buf(part, width)] * 2
     scratch += [buf(width, width), buf(width // 2, width)] + [buf(SIDE, width // 2, width)] * 3 + [buf(width // 2, width)] * 2
-    scratch += [pltpu.SemaphoreType.DMA((4,)), pltpu.SemaphoreType.DMA((REDUCE_COPIES,)), pltpu.SemaphoreType.DMA((REDUCE_COPIES,)), pltpu.SemaphoreType.REGULAR((2,))]
+    scratch += [dma(4), dma(2, 6), dma(2, 3), dma(2, 3), dma(GATHER_COPIES), dma(GATHER_COPIES), dma(REDUCE_COPIES), dma(REDUCE_COPIES), pltpu.SemaphoreType.REGULAR((3,))]
+    results = [(tokens, width), (tokens, width), (layers, width, width)]
+    kept = [(layers, local, *u) for u in ups] + [(layers, SLOTS, *u) for u in ups + acts] + [(SLOTS, cap, ff)] * 2
     return pl.pallas_call(
-        functools.partial(bwd_kernel, cap),
-        grid=(layers * SLOTS,),
-        in_specs=[fixed(v.shape) for v in (dy, x0, x1, wd, rank, rank_t, gmat)] + [stream(*u) for u in ups] + [stream(cap, width), stream(cap, ff), stream(cap, ff)],
-        out_specs=[fixed((tokens, width)), fixed((layers, width, width))] + [hbm] * 3,
-        out_shape=[shape((tokens, width), BF16), shape((layers, width, width), BF16)] + [shape((layers, local, *u), BF16) for u in ups],
+        functools.partial(kernel, cap),
+        grid=(STEPS,),
+        in_specs=[fixed(v.shape) for v in (x0, dy, ids, gates, wd)] + [hbm] * 3,
+        out_specs=[fixed(r) for r in results] + [hbm] * len(kept),
+        out_shape=[shape(r, BF16) for r in results + kept],
         scratch_shapes=scratch,
-        compiler_params=pltpu.CompilerParams(vmem_limit_bytes=VMEM_LIMIT, collective_id=1, has_side_effects=True),
-        name="backward",
-    )(dy, x0, x1, wd, rank, rank_t, gmat, w1, w3, w2, z, a, b)
+        compiler_params=pltpu.CompilerParams(vmem_limit_bytes=VMEM_LIMIT, collective_id=0, has_side_effects=True),
+        name="step",
+    )(x0, dy, ids, gates, wd, w1, w3, w2)[:6]
 
 
 def solution(mesh):
@@ -811,10 +742,8 @@
     expert_spec = P(None, "ep", None, None)
     whole_spec = P(None, None, None)
 
-    def device_step(tok_in, tok_grad, route_ids, gate_vals, w_dense, w_gate, w_up, w_down):
+    def device_step(tok_in, tok_grad, route_ids, gate_vals, *weights):
         tokens, top_k = route_ids.shape[1:]
-        cap = 2 * tokens * top_k // SLOTS
-        y, x1, *kept = forward(cap, tok_in, jnp.swapaxes(route_ids, 1, 2), jnp.swapaxes(gate_vals, 1, 2), w_dense, w_gate, w_up, w_down)
-        return (y, *backward(cap, tok_grad, tok_in, x1, w_dense, *kept))
+        return tuple(step(2 * tokens * top_k // SLOTS, tok_in, tok_grad, jnp.swapaxes(route_ids, 1, 2), jnp.swapaxes(gate_vals, 1, 2), *weights))
 
     return jax.shard_map(device_step, mesh=mesh, in_specs=(tok_spec, tok_spec, route_spec, route_spec, whole_spec, expert_spec, expert_spec, expert_spec), out_specs=(tok_spec, tok_spec, whole_spec, expert_spec, expert_spec, expert_spec), check_vma=False)

time: 284 us -> 287 us (1.011)
    pallas_call x2 -> x1, Pallas kernels: 270 us -> 272 us  [step(): pl.pallas_call(functools.partial(kernel, cap), grid=(STEPS,), in_specs=[f...]
    unnamed x14 -> x12, local copies, waits for them, and re-layouts: 13 us -> 14 us
where the time goes in v3:
time: 287 us; the launch traced here: 286 us
  Pallas kernels  272 us (95%)
  local copies, waits for them, and re-layouts  14 us (5%)
    pallas_call x1, Pallas kernels, step(): pl.pallas_call(functools.partial(kernel, cap), grid=(STEPS,), in_specs=[f...  272 us
    unnamed x12, local copies, waits for them, and re-layouts  14 us

profile of v3, /device:TPU:1, one launch (start us, length us, event | category | flops | bytes accessed | tf_op | source)
XLA Modules:
  0.0 286.3 jit_solution(12894982146853018348)
XLA Ops:
  0.6 271.7 %step.1 = (bf16[1024,384]{1,0:T(8,128)(2,1)}, bf16[1024,384]{1,0:T(8,128)(2,1)}, bf16[2,384,384]{2,1,0:T(8,128)(2,1)}, bf16[2,2,384,1024]{3,2,1,0:T(8,128)(2,1)}...) custom-call(bf16[1024,384]{1,0:T(8,128)(2,1)} %x0_ref.1, ...), custom_call_target="tpu_custom_call" | custom-call | tf_op jit(solution)/shard_map/step/pallas_call | solution.py:727
  272.3 0.0 copy-start.2
  272.3 2.2 copy.20
  274.6 2.1 copy.21
  276.7 1.9 copy.22
  278.6 0.0 copy-done.2
  278.6 0.0 copy-start.1
  278.6 1.7 copy.23
  280.3 1.4 copy-done.1
  281.6 0.0 copy-start
  281.6 1.7 copy.24
  283.3 1.4 copy-done
  284.7 1.7 copy.25
Async XLA Ops:
  272.3 6.3 %copy-start.2 = (bf16[2,2,384,1024]{3,2,1,0:T(8,128)(2,1)S(1)}, bf16[2,2,384,1024]{3,2,1,0:T(8,128)(2,1)}, u32[]{:S(2)}) copy-start(bf16[2,2,384,1024]{3,2,1,0:T(8,128)(2,1)} %get-tuple-element.27) | copy-start | bytes 9437188
  278.6 3.0 %copy-start.1 = (bf16[2,2,384,1024]{3,2,1,0:T(8,128)(2,1)S(1)}, bf16[2,2,384,1024]{3,2,1,0:T(8,128)(2,1)}, u32[]{:S(2)}) copy-start(bf16[2,2,384,1024]{3,2,1,0:T(8,128)(2,1)} %get-tuple-element.28) | copy-start | bytes 9437188
  281.6 3.0 %copy-start = (bf16[2,2,1024,384]{3,2,1,0:T(8,128)(2,1)S(1)}, bf16[2,2,1024,384]{3,2,1,0:T(8,128)(2,1)}, u32[]{:S(2)}) copy-start(bf16[2,2,1024,384]{3,2,1,0:T(8,128)(2,1)} %get-tuple-element.29) | copy-start | bytes 9437188

commit v4 on v3

--- a/solution.py
+++ b/solution.py
@@ -305,7 +305,7 @@
 
 OWN_STEPS = {1: 0, 4: 1, 5: 2, 7: 3}
 REDUCE_COPIES = 107
-LAST, LATE, DEFER, STEPS = 2 * SLOTS, 3 * SLOTS, 4 * SLOTS, 5 * SLOTS
+WEIGHTS1, INPUTS1, WEIGHTS0, INPUTS0, STEPS = (n * SLOTS for n in range(2, 7))
 
 
 def kernel(cap, x0_ref, dy_ref, ids_ref, gate_ref, wd_ref, o1_ref, o3_ref, o2_ref, y_ref, dx_ref, gd_ref, g1_ref, g3_ref, g2_ref, h1_ref, h3_ref, h2_ref, kz_ref, ka_ref, kb_ref, kda_ref, kdb_ref, acc_ref, cur_ref, x1_ref, rows_ref, columns_ref, w1_ref, w3_ref, w2_ref, z_ref, a_ref, b_ref, m1_ref, m3_ref, m2_ref, d1_ref, d3_ref, d2_ref, s1_ref, s3_ref, s2_ref, r11_ref, r12_ref, r31_ref, r32_ref, t1_ref, t3_ref, y11_ref, y12_ref, y31_ref, y32_ref, y21_ref, y22_ref, u1_ref, u2_ref, l1_ref, l2_ref, c1_ref, c3_ref, cu_ref, cl_ref, f1_ref, f3_ref, fu_ref, fl_ref, dp_ref, dr_ref, dcx_ref, dcy_ref, dcz_ref, ds_ref, de_ref, put_sem, load_sem, keep_sem, save_sem, gsend_sem, grecv_sem, send_sem, recv_sem, credit):
@@ -462,7 +462,7 @@
     def copy(src, dst, sem):
         return pltpu.make_async_copy(src, dst, sem)
 
-    def weights(step, layer, slot, arrays, buf, is_given=False):
+    def weights(layer, slot, arrays, buf, is_given=False):
         for n in arrays:
             src = given[n].at[layer, (place.c + slot) % 2] if is_given else whole[n].at[layer, slot]
             yield copy(src, bufs[n].at[buf], load_sem.at[buf, n])
@@ -471,25 +471,28 @@
         for n in ARRAYS:
             yield copy(kept[n].at[layer, slot], acts[n].at[buf], load_sem.at[buf, 3 + n])
 
-    def loads(step, do):
-        forth, back = step % 2, (step + 1) % 2
-        slot = step % SLOTS
-        rest = SLOTS - 1 - slot
-
-        def run(when, items):
-            @pl.when(when)
+    def forward_loads(step, do):
+        buf, slot = step % 2, step % SLOTS
+        for is_given in (True, False):
+
+            @pl.when((slot < 2) == is_given)
             def _():
-                for item in items():
+                for item in weights(step // SLOTS, slot, ARRAYS, buf, is_given):
                     do(item)
 
-        run((step < LAST) & (slot < 2), lambda: weights(step, step // SLOTS, slot, ARRAYS, forth, True))
-        run((step < LAST) & (slot >= 2), lambda: weights(step, step // SLOTS, slot, ARRAYS, forth))
-        run((step > LAST) & (step < LATE), lambda: [*weights(step, 1, rest, ARRAYS, back), *saved(1, rest, back)])
-        run((step >= LATE) & (step < DEFER), lambda: [*weights(step, 0, rest, [2], back), *saved(0, rest, back)])
-        run((step >= DEFER) & (step < STEPS), lambda: [*weights(step, 0, rest, BUFS, back)] + [copy(deferred[n].at[rest], acts[n + 1].at[back], load_sem.at[back, 4 + n]) for n in BUFS])
+    def weights_loads(step):
+        layer, slot, buf = layer_of(step), SLOTS - 1 - step % SLOTS, (step + 1) % 2
+        return [*weights(layer, slot, [2], buf), *saved(layer, slot, buf)]
+
+    def inputs_loads(step):
+        layer, slot, buf = layer_of(step), SLOTS - 1 - step % SLOTS, (step + 1) % 2
+        return [*weights(layer, slot, BUFS, buf)] + [copy(deferred[n].at[slot], acts[n + 1].at[buf], load_sem.at[buf, 4 + n]) for n in BUFS]
 
     def load(step):
-        loads(step, lambda item: item.start())
+        forward_loads(step, lambda item: item.start())
+
+    def layer_of(step):
+        return 1 - (step - WEIGHTS1) // (2 * SLOTS)
 
     def keeps(step):
         return [copy(bufs[n].at[step % 2], whole[n].at[step // SLOTS, step % SLOTS], keep_sem.at[step % 2, n]) for n in ARRAYS]
@@ -509,26 +512,22 @@
             item.start()
 
     def ending():
-        inner_onward()
         dense_sum()
+        y_finish()
         inner_finish()
-        y_finish()
         dense["y"].onward()
-        pass_finish(1)
-        pl.semaphore_signal(credit.at[2], inc=1, device_id=place.at("c", 0), device_id_type=MESH)
+        cross_onward("x", "z")
+        dense_next("y", "x")
         cross_onward("u", "l")
-        dense_next("y", "x")
-        cross_onward("x", "z")
+        cross_finish(0, "x", "z")
+        dense["x"].onward()
         cross_finish(0, "u", "l")
-        dense["x"].onward()
-        cross_finish(0, "x", "z")
+        final_onward(0, "x", "z")
+        dense_next("x", "z")
         final_onward(0, "u", "l")
-        dense_next("x", "z")
-        final_onward(0, "x", "z")
-        pl.semaphore_wait(credit.at[2], 1)
+        final_finish(0, "x", "z")
+        dense["z"].onward()
         final_finish(0, "u", "l")
-        dense["z"].onward()
-        final_finish(0, "x", "z")
         dense_pass(0)
         pass_finish(0)
         dense_finish(0)
@@ -543,28 +542,34 @@
     plan(before, 1, [g0.lead], [g0.follow, g0.lead_onward, g0.follow_onward, g0.last, g0.complete_y, lambda: load(s), g1.begin], [g0.passed_left])
     plan(before, 4, [g0.last_onward, g1.lead, g0.passed_right], [g1.follow, g0.complete_last], [g0.passed_last], [g1.lead_onward])
     plan(before, SLOTS, [g1.follow_onward, g1.last], [g1.complete_y], [], [g1.last_onward, g1.passed_left], [g1.passed_right], [g1.complete_last], [g1.passed_last])
-    plan(before, LAST + 2, [on_y["w"].start], [on(0)], [], [done(0), y_start], [on(1), on_y["w"].onward], [on(2)])
-    plan(middle, LATE - 1, [done(1)])
-    plan(before, LATE, [lambda: copies.start("dense pair")], [on(3)], [dense["y"].onward], [], [inner_onward], [y_finish], [], [lambda: cross_onward("x", "z")])
-    plan(middle, LATE, [dense_sum, done(2), y_onward], [], [w_finish], [done(3), lambda: dense_next("y", "x")], [], [inner_finish, dense["x"].onward], [], [lambda: cross_onward("u", "l"), lambda: dense_next("x", "z")])
-    plan(before, DEFER + 1, [lambda: cross_finish(1, "x", "z", "u", "l")], [dense["z"].onward], [], [lambda: dense_pass(1)], [lambda: final_onward(1, "x", "z", "u", "l")], [], [lambda: final_finish(1, "x", "z", "u", "l"), lambda: dense_finish(1)])
-    plan(after, LATE + 2, [on_y["w"].start])
-    plan(before, LATE + 4, [on(0)], [], [done(0), y_start, on_y["w"].onward], [on(1)], [on(2)], [], [done(1)], [on(3)], [done(2), y_onward], [], [w_finish], [done(3)])
-    for base in (LAST, LATE):
+    late = ("x", "z", "u", "l")
+    plan(before, WEIGHTS0, [lambda: copies.start("dense pair")], [inner_finish], [dense["y"].onward], [lambda: cross_onward(*late), lambda: dense_next("y", "x")])
+    plan(before, WEIGHTS0 + 5, [dense["x"].onward], [lambda: dense_next("x", "z")], [lambda: final_onward(1, *late)])
+    plan(middle, WEIGHTS0, [dense_sum, y_finish], [], [], [], [lambda: cross_finish(1, *late)], [], [], [dense["z"].onward])
+    plan(before, INPUTS0 + 1, [lambda: dense_pass(1), lambda: final_finish(1, *late)], [], [lambda: dense_finish(1)], [], [lambda: pass_finish(1)])
+    for base in (WEIGHTS1, WEIGHTS0):
+        plan(before, base + 2, [on_y["w"].start], [], [], [], [on_y["w"].onward])
+        plan(middle, base + 3, [on(0)], [], [done(0), y_start], [on(1)], [on(2)])
+        plan(before, base + SLOTS, [done(1)], [], [done(2), y_onward], [on(3)], [], [w_finish], [done(3)], [inner_onward])
         for step, q in OWN_STEPS.items():
             plan(after, base + step, [lambda q=q: reduce_start(q)])
 
-    def hooks(table):
-        for step, stages in sorted(table.items()):
-
-            @pl.when(s == step)
-            def _(stages=stages):
-                for stage in stages:
-                    stage()
-
-    is_forward, is_back = s < LAST, (s >= LAST) & (s < DEFER)
+    def hooks(table, *phases):
+        for phase in phases:
+            mine = {step: stages for step, stages in sorted(table.items()) if phase <= step < phase + SLOTS}
+            if mine:
+
+                @pl.when(s // SLOTS == phase // SLOTS)
+                def _(mine=mine):
+                    for step, stages in mine.items():
+
+                        @pl.when(s == step)
+                        def _(stages=stages):
+                            for stage in stages:
+                                stage()
+
+    phase, t = s // SLOTS, s % SLOTS
     forth, back = s % 2, (s + 1) % 2
-    t = s % SLOTS
 
     @pl.when(s == 0)
     def _():
@@ -574,28 +579,27 @@
         load(1)
         route(ids_ref, gate_ref, rows_ref, columns_ref, place)
 
-    hooks(before)
-    loads(s, lambda item: item.wait())
-    pl.when((s > 1) & (s <= LAST))(lambda: wait(saves(s - 2)))
-    pl.when((s > LATE) & (s <= DEFER))(lambda: wait(defers(s - 1)))
-    pl.when((s > 0) & (s != 1) & (s != LAST - 1))(lambda: load(s + 1))
-    pl.when(is_forward & (t < 2))(lambda: start(keeps(s)))
-
     def enter(x):
-        cur_ref[...] = (x.astype(F32) + dot(x, wd_ref[s // SLOTS])).astype(BF16)
+        cur_ref[...] = (x.astype(F32) + dot(x, wd_ref[phase])).astype(BF16)
         acc_ref[...] = jnp.zeros_like(acc_ref)
 
-    def enter_back(x):
-        cur_ref[...] = x
-        acc_ref[...] = x.astype(F32)
-
-    pl.when(s == 0)(lambda: enter(x0_ref[...]))
-    pl.when(s == SLOTS)(lambda: enter(x1_ref[...]))
-    pl.when(s == LAST)(lambda: enter_back(dy_ref[...]))
-
-    @pl.when(is_forward)
+    def leave(out_ref):
+        out_ref[...] = (cur_ref[...].astype(F32) + acc_ref[...]).astype(BF16)
+
+    @pl.when(s < WEIGHTS1)
     def _():
-        layer, slot = s // SLOTS, t
+        hooks(before, 0, SLOTS)
+        forward_loads(s, lambda item: item.wait())
+        pl.when(s > 1)(lambda: wait(saves(s - 2)))
+        pl.when((s > 0) & (s != 1) & (s < WEIGHTS1 - 1))(lambda: load(s + 1))
+
+        @pl.when(t < 2)
+        def _():
+            start(keeps(s))
+            pl.when(s == 0)(lambda: enter(x0_ref[...]))
+            pl.when(s == SLOTS)(lambda: enter(x1_ref[...]))
+
+        layer, slot = phase, t
         z = dot(one_hot(rows_ref, layer, slot, cap), cur_ref[...]).astype(BF16)
         z_ref[forth] = z
         a = dot(z, w1_ref[forth]).astype(BF16)
@@ -605,18 +609,30 @@
         h = (jax.nn.silu(a.astype(F32)) * b.astype(F32)).astype(BF16)
         o = dot(h, w2_ref[forth]).astype(BF16)
         acc_ref[...] += column(columns_ref, layer, SLOTS + slot) * dot(one_hot_t(columns_ref, layer, slot, cap), o)
-        pl.when(s < LAST - 1)(lambda: start(saves(s)))
+        pl.when(s < WEIGHTS1 - 1)(lambda: start(saves(s)))
         pl.when(t < 2)(lambda: wait(keeps(s)))
 
-    def leave(out_ref):
-        out_ref[...] = (cur_ref[...].astype(F32) + acc_ref[...]).astype(BF16)
-
-    pl.when(s == SLOTS - 1)(lambda: leave(x1_ref))
-    pl.when(s == LAST - 1)(lambda: leave(y_ref))
-
-    @pl.when(is_back)
+        @pl.when(t == SLOTS - 1)
+        def _():
+            pl.when(s == SLOTS - 1)(lambda: leave(x1_ref))
+            pl.when(s == WEIGHTS1 - 1)(lambda: leave(y_ref))
+
+    @pl.when((phase == WEIGHTS1 // SLOTS) | (phase == WEIGHTS0 // SLOTS))
     def _():
-        layer, slot = 1 - (s - LAST) // SLOTS, SLOTS - 1 - t
+        layer, slot = layer_of(s), SLOTS - 1 - t
+        hooks(before, WEIGHTS1, WEIGHTS0)
+
+        @pl.when(s == WEIGHTS1)
+        def _():
+            wait(saves(s - 2))
+            cur_ref[...] = dy_ref[...]
+            acc_ref[...] = dy_ref[...].astype(F32)
+
+        pl.when(s > WEIGHTS1)(lambda: wait(weights_loads(s)))
+        pl.when(t > 0)(lambda: wait(defers(s - 1)))
+        pl.when(t < SLOTS - 1)(lambda: start(weights_loads(s + 1)))
+        pl.when(t == SLOTS - 1)(lambda: start(inputs_loads(s + 1)))
+
         grad_gated = (column(columns_ref, layer, SLOTS + slot) * cur_ref[...].astype(F32)).astype(BF16)
         do = dot(one_hot(rows_ref, layer, slot, cap), grad_gated).astype(BF16)
         dh = dot_nt(do, w2_ref[back])
@@ -630,8 +646,8 @@
         a_ref[2] = da
         b_ref[2] = db
         z = z_ref[back]
-        pl.when(s >= LATE)(lambda: start(defers(s)))
-        hooks(middle)
+        start(defers(s))
+        hooks(middle, WEIGHTS1, WEIGHTS0)
 
         def weight_grads():
             return dot_tn(z, da), dot_tn(z, db), dot_tn(h, do)
@@ -639,16 +655,17 @@
         is_own = functools.reduce(jnp.logical_or, [t == step for step in OWN_STEPS])
         group = t // 4 + t // 5 + t // 7
         into = (t // 2 + t // 3) % 2
+        turn = t + (1 - layer) * SLOTS
 
         @pl.when(jnp.logical_not(is_own))
         def _():
             for buf in BUFS:
-                pl.when((s > LAST) & (into == 1 - buf))(lambda buf=buf: copies.sent(*[("pair", buf, n) for n in ARRAYS]))
+                pl.when((turn > 0) & (into == 1 - buf))(lambda buf=buf: copies.sent(*[("pair", buf, n) for n in ARRAYS]))
 
             for ref, grad in zip(stage, weight_grads()):
                 ref[...] = grad.astype(BF16)
 
-            pl.when(s >= LAST + 3)(lambda: pl.semaphore_wait(credit.at[into], 1))
+            pl.when(turn >= 3)(lambda: pl.semaphore_wait(credit.at[into], 1))
             for buf in BUFS:
                 pl.when(into == buf)(lambda buf=buf: copies.start(*[("pair", buf, n) for n in ARRAYS]))
 
@@ -660,16 +677,11 @@
             for ref, add, grad in zip(mine_of, mate, weight_grads()):
                 ref[group] = (grad + add[group % 2].astype(F32)).astype(BF16)
 
-            @pl.when(s < DEFER - 3)
+            @pl.when(turn < 2 * SLOTS - 3)
             def _():
                 pl.semaphore_signal(credit.at[group % 2], inc=1, device_id=place.at("c", 0), device_id_type=MESH)
 
-    @pl.when(((s >= LAST) & (s < LATE)) | (s >= DEFER))
-    def _():
-        layer, slot = s // LATE * -1 + 1, SLOTS - 1 - t
-        src = back - (s // DEFER - 1) * (2 - back)
-        dz = (dot_nt(a_ref[src], w1_ref[back]) + dot_nt(b_ref[src], w3_ref[back])).astype(BF16)
-        acc_ref[...] += dot(one_hot_t(columns_ref, layer, slot, cap), dz)
+            hooks(after, WEIGHTS1, WEIGHTS0)
 
     def leave_back(layer, x, out_ref):
         grad = acc_ref[...]
@@ -677,20 +689,29 @@
         dp_ref[...] = dot_tn(x, grad_b).astype(BF16)
         out_ref[...] = (grad + dot_nt(grad_b, wd_ref[layer])).astype(BF16)
 
-    @pl.when(s == LATE - 1)
+    @pl.when((phase == INPUTS1 // SLOTS) | (phase == INPUTS0 // SLOTS))
     def _():
-        leave_back(1, x1_ref[...], cur_ref)
-        acc_ref[...] = cur_ref[...].astype(F32)
-
-    hooks(after)
-
-    @pl.when(s == STEPS - 1)
-    def _():
-        leave_back(0, x0_ref[...], dx_ref)
-        copies.start("dense pair")
-        ending()
-        copies.sent(*[("pair", 1, n) for n in ARRAYS])
-        gathers.sent(*gathers.made)
+        layer, slot = layer_of(s), SLOTS - 1 - t
+        hooks(before, INPUTS1, INPUTS0)
+        wait(inputs_loads(s))
+        pl.when(t == 0)(lambda: wait(defers(s - 1)))
+        pl.when(t < SLOTS - 1)(lambda: start(inputs_loads(s + 1)))
+        pl.when(s == WEIGHTS0 - 1)(lambda: start(weights_loads(s + 1)))
+        dz = (dot_nt(a_ref[back], w1_ref[back]) + dot_nt(b_ref[back], w3_ref[back])).astype(BF16)
+        acc_ref[...] += dot(one_hot_t(columns_ref, layer, slot, cap), dz)
+
+        @pl.when(s == WEIGHTS0 - 1)
+        def _():
+            leave_back(1, x1_ref[...], cur_ref)
+            acc_ref[...] = cur_ref[...].astype(F32)
+
+        @pl.when(s == STEPS - 1)
+        def _():
+            leave_back(0, x0_ref[...], dx_ref)
+            copies.start("dense pair")
+            ending()
+            copies.sent(*[("pair", 1, n) for n in ARRAYS])
+            gathers.sent(*gathers.made)
 
 
 def step(cap, x0, dy, ids, gates, wd, w1, w3, w2):
@@ -721,7 +742,7 @@
     scratch += [buf(SIDE, quarter, ff)] * 2 + [buf(SIDE, part, width)] * 2
     scratch += [buf(quarter, ff)] * 2 + [buf(part, width)] * 2
     scratch += [buf(width, width), buf(width // 2, width)] + [buf(SIDE, width // 2, width)] * 3 + [buf(width // 2, width)] * 2
-    scratch += [dma(4), dma(2, 6), dma(2, 3), dma(2, 3), dma(GATHER_COPIES), dma(GATHER_COPIES), dma(REDUCE_COPIES), dma(REDUCE_COPIES), pltpu.SemaphoreType.REGULAR((3,))]
+    scratch += [dma(4), dma(2, 6), dma(2, 3), dma(2, 3), dma(GATHER_COPIES), dma(GATHER_COPIES), dma(REDUCE_COPIES), dma(REDUCE_COPIES), pltpu.SemaphoreType.REGULAR((2,))]
     results = [(tokens, width), (tokens, width), (layers, width, width)]
     kept = [(layers, local, *u) for u in ups] + [(layers, SLOTS, *u) for u in ups + acts] + [(SLOTS, cap, ff)] * 2
     return pl.pallas_call(

time: 287 us -> 282 us (0.983)
  Pallas kernels: 272 us -> 267 us
    pallas_call x1, Pallas kernels: 272 us -> 267 us  [step(): pl.pallas_call(functools.partial(kernel, cap), grid=(STEPS,), in_specs=[f...]
where the time goes in v4:
time: 282 us
  Pallas kernels  267 us (95%)
  local copies, waits for them, and re-layouts  14 us (5%)
    pallas_call x1, Pallas kernels, step(): pl.pallas_call(functools.partial(kernel, cap), grid=(STEPS,), in_specs=[f...  267 us
    unnamed x12, local copies, waits for them, and re-layouts  14 us

profile of v4, /device:TPU:1, one launch (start us, length us, event | category | flops | bytes accessed | tf_op | source)
XLA Modules:
  0.0 281.9 jit_solution(14200343172397501852)
XLA Ops:
  0.6 267.2 %step.1 = (bf16[1024,384]{1,0:T(8,128)(2,1)}, bf16[1024,384]{1,0:T(8,128)(2,1)}, bf16[2,384,384]{2,1,0:T(8,128)(2,1)}, bf16[2,2,384,1024]{3,2,1,0:T(8,128)(2,1)}...) custom-call(bf16[1024,384]{1,0:T(8,128)(2,1)} %x0_ref.1, ...), custom_call_target="tpu_custom_call" | custom-call | tf_op jit(solution)/shard_map/step/pallas_call | solution.py:748
  267.9 0.0 copy-start.2
  267.9 2.2 copy.20
  270.1 2.1 copy.21
  272.2 1.9 copy.22
  274.2 0.0 copy-done.2
  274.2 0.0 copy-start.1
  274.2 1.7 copy.23
  275.8 1.4 copy-done.1
  277.2 0.0 copy-start
  277.2 1.7 copy.24
  278.9 1.4 copy-done
  280.2 1.7 copy.25
Async XLA Ops:
  267.9 6.3 %copy-start.2 = (bf16[2,2,384,1024]{3,2,1,0:T(8,128)(2,1)S(1)}, bf16[2,2,384,1024]{3,2,1,0:T(8,128)(2,1)}, u32[]{:S(2)}) copy-start(bf16[2,2,384,1024]{3,2,1,0:T(8,128)(2,1)} %get-tuple-element.27) | copy-start | bytes 9437188
  274.2 3.0 %copy-start.1 = (bf16[2,2,384,1024]{3,2,1,0:T(8,128)(2,1)S(1)}, bf16[2,2,384,1024]{3,2,1,0:T(8,128)(2,1)}, u32[]{:S(2)}) copy-start(bf16[2,2,384,1024]{3,2,1,0:T(8,128)(2,1)} %get-tuple-element.28) | copy-start | bytes 9437188
  277.2 3.0 %copy-start = (bf16[2,2,1024,384]{3,2,1,0:T(8,128)(2,1)S(1)}, bf16[2,2,1024,384]{3,2,1,0:T(8,128)(2,1)}, u32[]{:S(2)}) copy-start(bf16[2,2,1024,384]{3,2,1,0:T(8,128)(2,1)} %get-tuple-element.29) | copy-start | bytes 9437188

commit v5 on v4

--- a/solution.py
+++ b/solution.py
@@ -53,7 +53,7 @@
 
 class Copies:
     def __init__(self, place, send, recv):
-        self.place, self.send, self.recv, self.made, self.number, self.count = place, send, recv, {}, {}, 0
+        self.place, self.send, self.recv, self.made, self.number, self.count, self.over = place, send, recv, {}, {}, 0, set()
 
     def add(self, key, src, dst, axis, step, like=None):
         if like is None:
@@ -74,6 +74,10 @@
     def sent(self, *keys):
         for key in keys:
             self.made[key].wait_send()
+            self.over.add(key)
+
+    def drain(self):
+        self.sent(*[key for key in self.made if key not in self.over])
 
 
 def greet(place):
@@ -166,13 +170,18 @@
         self.passed(6)
 
     def begin(self):
-        for slot, color in ((2, "x"), (3, "z"), (2, "z"), (3, "x")):
-            self.copies.start(*self._keys("y", slot, color))
+        self.copies.start(*self._keys("y", 2, "x"), *self._keys("y", 3, "z"))
+
+    def second(self):
+        self.copies.sent(*self._keys("y", 2, "x"), *self._keys("y", 3, "z"))
+        self.copies.start(*self._keys("y", 2, "z"), *self._keys("y", 3, "x"))
+
+    def third(self):
+        self.copies.sent(*self._keys("y", 2, "z"), *self._keys("y", 3, "x"))
+        self.copies.start(*self._keys("y", 6, "x"), *self._keys("y", 6, "z"))
 
     def spread(self, slot, color):
         self.copies.arrive(*self._keys("y", slot, color))
-        if (slot, color) in ((2, "x"), (3, "z")):
-            self.copies.start(*self._keys("y", 6, color))
         for step in WAYS:
             self.copies.start(*self._keys("near", slot, color, extra=(step,)))
 
@@ -308,7 +317,7 @@
 WEIGHTS1, INPUTS1, WEIGHTS0, INPUTS0, STEPS = (n * SLOTS for n in range(2, 7))
 
 
-def kernel(cap, x0_ref, dy_ref, ids_ref, gate_ref, wd_ref, o1_ref, o3_ref, o2_ref, y_ref, dx_ref, gd_ref, g1_ref, g3_ref, g2_ref, h1_ref, h3_ref, h2_ref, kz_ref, ka_ref, kb_ref, kda_ref, kdb_ref, acc_ref, cur_ref, x1_ref, rows_ref, columns_ref, w1_ref, w3_ref, w2_ref, z_ref, a_ref, b_ref, m1_ref, m3_ref, m2_ref, d1_ref, d3_ref, d2_ref, s1_ref, s3_ref, s2_ref, r11_ref, r12_ref, r31_ref, r32_ref, t1_ref, t3_ref, y11_ref, y12_ref, y31_ref, y32_ref, y21_ref, y22_ref, u1_ref, u2_ref, l1_ref, l2_ref, c1_ref, c3_ref, cu_ref, cl_ref, f1_ref, f3_ref, fu_ref, fl_ref, dp_ref, dr_ref, dcx_ref, dcy_ref, dcz_ref, ds_ref, de_ref, put_sem, load_sem, keep_sem, save_sem, gsend_sem, grecv_sem, send_sem, recv_sem, credit):
+def kernel(cap, x0_ref, dy_ref, ids_ref, gate_ref, wd_ref, o1_ref, o3_ref, o2_ref, y_ref, dx_ref, gdense_ref, g1_ref, g3_ref, g2_ref, h1_ref, h3_ref, h2_ref, kz_ref, ka_ref, kb_ref, kda_ref, kdb_ref, acc_ref, cur_ref, x1_ref, hold_ref, gd_ref, rows_ref, columns_ref, w1_ref, w3_ref, w2_ref, z_ref, a_ref, b_ref, m1_ref, m3_ref, m2_ref, d1_ref, d3_ref, d2_ref, s1_ref, s3_ref, s2_ref, r11_ref, r12_ref, r31_ref, r32_ref, t1_ref, t3_ref, y11_ref, y12_ref, y31_ref, y32_ref, y21_ref, y22_ref, u1_ref, u2_ref, l1_ref, l2_ref, c1_ref, c3_ref, cu_ref, cl_ref, f1_ref, f3_ref, fu_ref, fl_ref, dp_ref, dr_ref, dcx_ref, dcy_ref, dcz_ref, ds_ref, de_ref, put_sem, load_sem, keep_sem, save_sem, gsend_sem, grecv_sem, send_sem, recv_sem, credit):
     s = pl.program_id(0)
     place = Place()
     gathers = Copies(place, gsend_sem, grecv_sem)
@@ -512,22 +521,24 @@
             item.start()
 
     def ending():
-        dense_sum()
         y_finish()
         inner_finish()
+        dense_finish(1)
+        copies.start("dense pair")
+        dense_sum()
+        cross_onward("x", "z")
+        cross_onward("u", "l")
         dense["y"].onward()
-        cross_onward("x", "z")
+        cross_finish(0, "x", "z")
+        cross_finish(0, "u", "l")
         dense_next("y", "x")
-        cross_onward("u", "l")
-        cross_finish(0, "x", "z")
+        final_onward(0, "x", "z")
         dense["x"].onward()
-        cross_finish(0, "u", "l")
-        final_onward(0, "x", "z")
+        final_onward(0, "u", "l")
         dense_next("x", "z")
-        final_onward(0, "u", "l")
         final_finish(0, "x", "z")
+        final_finish(0, "u", "l")
         dense["z"].onward()
-        final_finish(0, "u", "l")
         dense_pass(0)
         pass_finish(0)
         dense_finish(0)
@@ -539,18 +550,19 @@
             table.setdefault(first + n, []).extend(stage)
 
     on, done = lambda q: lambda: reduce_onward(q), lambda q: lambda: reduce_finish(q)
-    plan(before, 1, [g0.lead], [g0.follow, g0.lead_onward, g0.follow_onward, g0.last, g0.complete_y, lambda: load(s), g1.begin], [g0.passed_left])
-    plan(before, 4, [g0.last_onward, g1.lead, g0.passed_right], [g1.follow, g0.complete_last], [g0.passed_last], [g1.lead_onward])
-    plan(before, SLOTS, [g1.follow_onward, g1.last], [g1.complete_y], [], [g1.last_onward, g1.passed_left], [g1.passed_right], [g1.complete_last], [g1.passed_last])
+    now = lambda: load(s)
+    plan(before, 0, [g0.second, g0.lead], [g0.third, g0.follow, g0.lead_onward], [g1.begin, g0.follow_onward, g0.complete_y, now, g0.last])
+    plan(before, 3, [g0.passed_left, g1.second], [g0.passed_right, g0.last_onward, g1.lead], [g1.third], [g0.complete_last, now, g1.follow], [g0.passed_last, now, g1.lead_onward])
+    plan(before, SLOTS + 1, [g1.follow_onward], [g1.complete_y, now, g1.last], [g1.passed_left], [g1.passed_right], [g1.last_onward], [g1.complete_last, now], [g1.passed_last, now])
+    unready = (1, 5, 6, SLOTS + 1, SLOTS + 5, SLOTS + 6)
     late = ("x", "z", "u", "l")
-    plan(before, WEIGHTS0, [lambda: copies.start("dense pair")], [inner_finish], [dense["y"].onward], [lambda: cross_onward(*late), lambda: dense_next("y", "x")])
-    plan(before, WEIGHTS0 + 5, [dense["x"].onward], [lambda: dense_next("x", "z")], [lambda: final_onward(1, *late)])
-    plan(middle, WEIGHTS0, [dense_sum, y_finish], [], [], [], [lambda: cross_finish(1, *late)], [], [], [dense["z"].onward])
-    plan(before, INPUTS0 + 1, [lambda: dense_pass(1), lambda: final_finish(1, *late)], [], [lambda: dense_finish(1)], [], [lambda: pass_finish(1)])
+    plan(before, WEIGHTS0, [lambda: copies.start("dense pair")], [inner_finish], [], [lambda: cross_onward(*late), dense["y"].onward], [], [], [lambda: dense_next("y", "x")])
+    plan(middle, WEIGHTS0, [dense_sum, y_finish], [], [], [], [lambda: cross_finish(1, *late)], [], [], [lambda: final_onward(1, *late)])
+    plan(before, INPUTS0 + 1, [dense["x"].onward], [lambda: final_finish(1, *late)], [lambda: dense_next("x", "z")], [], [dense["z"].onward], [lambda: pass_finish(1)], [lambda: dense_pass(1)])
     for base in (WEIGHTS1, WEIGHTS0):
         plan(before, base + 2, [on_y["w"].start], [], [], [], [on_y["w"].onward])
         plan(middle, base + 3, [on(0)], [], [done(0), y_start], [on(1)], [on(2)])
-        plan(before, base + SLOTS, [done(1)], [], [done(2), y_onward], [on(3)], [], [w_finish], [done(3)], [inner_onward])
+        plan(before, base + SLOTS, [done(1)], [], [done(2), y_onward], [on(3)], [w_finish], [], [done(3), inner_onward])
         for step, q in OWN_STEPS.items():
             plan(after, base + step, [lambda q=q: reduce_start(q)])
 
@@ -591,7 +603,8 @@
         hooks(before, 0, SLOTS)
         forward_loads(s, lambda item: item.wait())
         pl.when(s > 1)(lambda: wait(saves(s - 2)))
-        pl.when((s > 0) & (s != 1) & (s < WEIGHTS1 - 1))(lambda: load(s + 1))
+        ahead = functools.reduce(jnp.logical_and, [s != step for step in unready], (s > 0) & (s < WEIGHTS1 - 1))
+        pl.when(ahead)(lambda: load(s + 1))
 
         @pl.when(t < 2)
         def _():
@@ -615,7 +628,7 @@
         @pl.when(t == SLOTS - 1)
         def _():
             pl.when(s == SLOTS - 1)(lambda: leave(x1_ref))
-            pl.when(s == WEIGHTS1 - 1)(lambda: leave(y_ref))
+            pl.when(s == WEIGHTS1 - 1)(lambda: leave(hold_ref))
 
     @pl.when((phase == WEIGHTS1 // SLOTS) | (phase == WEIGHTS0 // SLOTS))
     def _():
@@ -624,7 +637,11 @@
 
         @pl.when(s == WEIGHTS1)
         def _():
+            moved = copy(hold_ref, y_ref, keep_sem.at[0, 0])
+            moved.start()
             wait(saves(s - 2))
+            gathers.drain()
+            moved.wait()
             cur_ref[...] = dy_ref[...]
             acc_ref[...] = dy_ref[...].astype(F32)
 
@@ -649,8 +666,8 @@
         start(defers(s))
         hooks(middle, WEIGHTS1, WEIGHTS0)
 
-        def weight_grads():
-            return dot_tn(z, da), dot_tn(z, db), dot_tn(h, do)
+        def weight_grad(n):
+            return dot_tn(*((z, da), (z, db), (h, do))[n])
 
         is_own = functools.reduce(jnp.logical_or, [t == step for step in OWN_STEPS])
         group = t // 4 + t // 5 + t // 7
@@ -659,23 +676,20 @@
 
         @pl.when(jnp.logical_not(is_own))
         def _():
-            for buf in BUFS:
-                pl.when((turn > 0) & (into == 1 - buf))(lambda buf=buf: copies.sent(*[("pair", buf, n) for n in ARRAYS]))
-
-            for ref, grad in zip(stage, weight_grads()):
-                ref[...] = grad.astype(BF16)
-
             pl.when(turn >= 3)(lambda: pl.semaphore_wait(credit.at[into], 1))
-            for buf in BUFS:
-                pl.when(into == buf)(lambda buf=buf: copies.start(*[("pair", buf, n) for n in ARRAYS]))
+            for n, ref in enumerate(stage):
+                for buf in BUFS:
+                    pl.when((turn > 0) & (into == 1 - buf))(lambda: copies.sent(("pair", buf, n)))
+                ref[...] = weight_grad(n).astype(BF16)
+                for buf in BUFS:
+                    pl.when(into == buf)(lambda: copies.start(("pair", buf, n)))
 
         @pl.when(is_own)
         def _():
-            for buf in BUFS:
-                pl.when(group % 2 == buf)(lambda buf=buf: copies.arrive(*[("pair", buf, n) for n in ARRAYS]))
-
-            for ref, add, grad in zip(mine_of, mate, weight_grads()):
-                ref[group] = (grad + add[group % 2].astype(F32)).astype(BF16)
+            for n, ref in enumerate(mine_of):
+                for buf in BUFS:
+                    pl.when(group % 2 == buf)(lambda: copies.arrive(("pair", buf, n)))
+                ref[group] = (weight_grad(n) + mate[n][group % 2].astype(F32)).astype(BF16)
 
             @pl.when(turn < 2 * SLOTS - 3)
             def _():
@@ -707,11 +721,15 @@
 
         @pl.when(s == STEPS - 1)
         def _():
-            leave_back(0, x0_ref[...], dx_ref)
-            copies.start("dense pair")
+            leave_back(0, x0_ref[...], hold_ref)
+            moved = copy(hold_ref, dx_ref, keep_sem.at[0, 0])
+            moved.start()
             ending()
+            dense_out = copy(gd_ref, gdense_ref, keep_sem.at[0, 1])
+            dense_out.start()
             copies.sent(*[("pair", 1, n) for n in ARRAYS])
-            gathers.sent(*gathers.made)
+            moved.wait()
+            dense_out.wait()
 
 
 def step(cap, x0, dy, ids, gates, wd, w1, w3, w2):
@@ -732,7 +750,7 @@
     shape = jax.ShapeDtypeStruct
     ups, downs = [(width, ff), (width, ff), (ff, width)], [(quarter, ff), (part, width)]
     acts = [(cap, width), (cap, ff), (cap, ff)]
-    scratch = [pltpu.VMEM((tokens, width), F32), buf(tokens, width), buf(tokens, width), pltpu.VMEM((layers, SLOTS, tokens), jnp.int32), pltpu.VMEM((layers, tokens, LANES), F32)]
+    scratch = [pltpu.VMEM((tokens, width), F32)] + [buf(tokens, width)] * 3 + [buf(layers, width, width), pltpu.VMEM((layers, SLOTS, tokens), jnp.int32), pltpu.VMEM((layers, tokens, LANES), F32)]
     scratch += [buf(2, *u) for u in ups] + [buf(2, *acts[0]), buf(3, *acts[1]), buf(3, *acts[2])]
     scratch += [buf(*u) for u in ups] + [buf(2, *u) for u in ups] + [buf(SIDE, *u) for u in ups]
     scratch += [buf(SIDE, 2, quarter // 2, ff), buf(SIDE, 2, quarter, ff)] * 2
@@ -749,7 +767,7 @@
         functools.partial(kernel, cap),
         grid=(STEPS,),
         in_specs=[fixed(v.shape) for v in (x0, dy, ids, gates, wd)] + [hbm] * 3,
-        out_specs=[fixed(r) for r in results] + [hbm] * len(kept),
+        out_specs=[hbm] * len(results + kept),
         out_shape=[shape(r, BF16) for r in results + kept],
         scratch_shapes=scratch,
         compiler_params=pltpu.CompilerParams(vmem_limit_bytes=VMEM_LIMIT, collective_id=0, has_side_effects=True),
@@ -757,6 +775,33 @@
     )(x0, dy, ids, gates, wd, w1, w3, w2)[:6]
 
 
+def take_kernel(count, *refs):
+    sources, targets, holds, (come, go) = refs[:count], refs[count : 2 * count], refs[2 * count : 3 * count], refs[3 * count :]
+    comes = [pltpu.make_async_copy(a, b, come.at[n]) for n, (a, b) in enumerate(zip(sources, holds))]
+    goes = [pltpu.make_async_copy(a, b, go.at[n]) for n, (a, b) in enumerate(zip(holds, targets))]
+    for item in comes:
+        item.start()
+    for first, then in zip(comes, goes):
+        first.wait()
+        then.start()
+    for item in goes:
+        item.wait()
+
+
+def take(arrays):
+    count = len(arrays)
+    hbm = pl.BlockSpec(memory_space=pl.ANY)
+    return pl.pallas_call(
+        functools.partial(take_kernel, count),
+        in_specs=[hbm] * count,
+        out_specs=[hbm] * count,
+        out_shape=[jax.ShapeDtypeStruct(a.shape, a.dtype) for a in arrays],
+        scratch_shapes=[pltpu.VMEM(a.shape, a.dtype) for a in arrays] + [pltpu.SemaphoreType.DMA((count,))] * 2,
+        compiler_params=pltpu.CompilerParams(vmem_limit_bytes=VMEM_LIMIT),
+        name="take",
+    )(*arrays)
+
+
 def solution(mesh):
     tok_spec = P(TOK_AXES, None)
     route_spec = P(None, TOK_AXES, None)
@@ -765,6 +810,6 @@
 
     def device_step(tok_in, tok_grad, route_ids, gate_vals, *weights):
         tokens, top_k = route_ids.shape[1:]
-        return tuple(step(2 * tokens * top_k // SLOTS, tok_in, tok_grad, jnp.swapaxes(route_ids, 1, 2), jnp.swapaxes(gate_vals, 1, 2), *weights))
+        return tuple(take(step(2 * tokens * top_k // SLOTS, tok_in, tok_grad, jnp.swapaxes(route_ids, 1, 2), jnp.swapaxes(gate_vals, 1, 2), *weights)))
 
     return jax.shard_map(device_step, mesh=mesh, in_specs=(tok_spec, tok_spec, route_spec, route_spec, whole_spec, expert_spec, expert_spec, expert_spec), out_specs=(tok_spec, tok_spec, whole_spec, expert_spec, expert_spec, expert_spec), check_vma=False)

time: 282 us -> 279 us (0.989)
  local copies, waits for them, and re-layouts: 14 us -> 0 us
  Pallas kernels: 267 us -> 278 us
    unnamed x12 -> x0, local copies, waits for them, and re-layouts: 14 us -> none
    pallas_call x0 -> x1, Pallas kernels: none -> 8.93 us  [take(): pl.pallas_call(functools.partial(take_kernel, count), in_specs=[hbm] * co...]
where the time goes in v5:
time: 279 us; the launch traced here: 278 us
  Pallas kernels  278 us (100%)
    pallas_call x1, Pallas kernels, step(): pl.pallas_call(functools.partial(kernel, cap), grid=(STEPS,), in_specs=[f...  269 us
    pallas_call x1, Pallas kernels, take(): pl.pallas_call(functools.partial(take_kernel, count), in_specs=[hbm] * co...  8.93 us

profile of v5, /device:TPU:1, one launch (start us, length us, event | category | flops | bytes accessed | tf_op | source)
XLA Modules:
  0.0 278.2 jit_solution(6023651158506095843)
XLA Ops:
  0.6 268.7 %step.1 = (bf16[1024,384]{1,0:T(8,128)(2,1)}, bf16[1024,384]{1,0:T(8,128)(2,1)}, bf16[2,384,384]{2,1,0:T(8,128)(2,1)}, bf16[2,2,384,1024]{3,2,1,0:T(8,128)(2,1)}...) custom-call(bf16[1024,384]{1,0:T(8,128)(2,1)} %x0_ref.1, ...), custom_call_target="tpu_custom_call" | custom-call | tf_op jit(solution)/shard_map/step/pallas_call | solution.py:766
  269.3 8.9 %take.1 = (bf16[1024,384]{1,0:T(8,128)(2,1)}, bf16[1024,384]{1,0:T(8,128)(2,1)}, bf16[2,384,384]{2,1,0:T(8,128)(2,1)}, bf16[2,2,384,1024]{3,2,1,0:T(8,128)(2,1)}...) custom-call(bf16[1024,384]{1,0:T(8,128)(2,1)} %get-tuple-element.12.refs_0_, ...), custom_call_target="tpu_custom_call" | custom-call | tf_op jit(solution)/shard_map/take/pallas_call | solution.py:794

commit v6 on v5

--- a/solution.py
+++ b/solution.py
@@ -18,7 +18,7 @@
 ARRAYS = range(3)
 SLOTS = 8
 MESH = pl.DeviceIdType.MESH
-VMEM_LIMIT = 63 << 20
+VMEM_LIMIT = 67_043_328
 
 
 def dot(a, b):
@@ -89,8 +89,7 @@
 
 
 class Gather:
-    FROM = {2: -1, 3: 1, 6: 2}
-    PASS = {2: 4, 3: 5, 6: 7}
+    PASS = {2: 4, 3: 6, 5: 7}
 
     def __init__(self, layer, copies, place, own, whole):
         self.layer, self.copies, self.place, self.own, self.whole = layer, copies, place, own, whole
@@ -102,10 +101,10 @@
                 self._add(("y", 2, color, part), color, part, None, 2, mine[color], None, "y", 1)
                 self._add(("y", 3, color, part), color, part, None, 3, mine[color], None, "y", -1)
                 if color == "x":
-                    self._add(("y", 6, color, part), color, part, 2, 6, mine[color], None, "y", 1)
+                    self._add(("y", 5, color, part), color, part, 2, 5, mine[color], None, "y", 1)
                 else:
-                    self._add(("y", 6, color, part), color, part, 3, 6, mine[color], None, "y", -1)
-                for slot in (2, 3, 6):
+                    self._add(("y", 5, color, part), color, part, 3, 5, mine[color], None, "y", -1)
+                for slot in (2, 3, 5):
                     for step in WAYS:
                         self._add(("near", slot, color, part, step), color, part, slot, slot, mine[color], None, color, step)
                         behind = (mine[color] - step + SIDE) % SIDE
@@ -146,19 +145,19 @@
         self.onward(3, "x")
 
     def last(self):
-        self.spread(6, "x")
-        self.spread(6, "z")
+        self.spread(5, "x")
+        self.spread(5, "z")
 
     def last_onward(self):
-        self.onward(6, "x")
-        self.onward(6, "z")
+        self.onward(5, "x")
+        self.onward(5, "z")
 
     def complete_y(self):
         self.complete(2)
         self.complete(3)
 
     def complete_last(self):
-        self.complete(6)
+        self.complete(5)
 
     def passed_left(self):
         self.passed(2)
@@ -167,7 +166,7 @@
         self.passed(3)
 
     def passed_last(self):
-        self.passed(6)
+        self.passed(5)
 
     def begin(self):
         self.copies.start(*self._keys("y", 2, "x"), *self._keys("y", 3, "z"))
@@ -178,7 +177,7 @@
 
     def third(self):
         self.copies.sent(*self._keys("y", 2, "z"), *self._keys("y", 3, "x"))
-        self.copies.start(*self._keys("y", 6, "x"), *self._keys("y", 6, "z"))
+        self.copies.start(*self._keys("y", 5, "x"), *self._keys("y", 5, "z"))
 
     def spread(self, slot, color):
         self.copies.arrive(*self._keys("y", slot, color))
@@ -212,7 +211,7 @@
         ids, gates = ids_ref[layer], gate_ref[layer]
         off = ((ids >> 1) - place.y) & (SIDE - 1)
         odd = (ids + place.c) & 1
-        slot = jnp.where(off == 0, odd, jnp.where(off == SIDE - 1, 2 + 2 * odd, jnp.where(off == 1, 3 + 2 * odd, 6 + odd)))
+        slot = jnp.where(off == 0, odd, jnp.where(off == SIDE - 1, 2 + 2 * odd, jnp.where(off == 1, 3 + 3 * odd, 5 + 2 * odd)))
         hits = [slot[n : n + 1] == lead for n in BUFS]
         hit = hits[0] | hits[1]
         weight = jnp.where(hits[0], gates[0:1], 0.0) + jnp.where(hits[1], gates[1:2], 0.0)
@@ -312,18 +311,18 @@
     return (ref[0].astype(F32) + ref[1].astype(F32) + ref[2].astype(F32) + ref[3].astype(F32)).astype(BF16)
 
 
-OWN_STEPS = {1: 0, 4: 1, 5: 2, 7: 3}
+OWN_STEPS = {2: 0, 4: 1, 5: 2, 7: 3}
 REDUCE_COPIES = 107
 WEIGHTS1, INPUTS1, WEIGHTS0, INPUTS0, STEPS = (n * SLOTS for n in range(2, 7))
 
 
-def kernel(cap, x0_ref, dy_ref, ids_ref, gate_ref, wd_ref, o1_ref, o3_ref, o2_ref, y_ref, dx_ref, gdense_ref, g1_ref, g3_ref, g2_ref, h1_ref, h3_ref, h2_ref, kz_ref, ka_ref, kb_ref, kda_ref, kdb_ref, acc_ref, cur_ref, x1_ref, hold_ref, gd_ref, rows_ref, columns_ref, w1_ref, w3_ref, w2_ref, z_ref, a_ref, b_ref, m1_ref, m3_ref, m2_ref, d1_ref, d3_ref, d2_ref, s1_ref, s3_ref, s2_ref, r11_ref, r12_ref, r31_ref, r32_ref, t1_ref, t3_ref, y11_ref, y12_ref, y31_ref, y32_ref, y21_ref, y22_ref, u1_ref, u2_ref, l1_ref, l2_ref, c1_ref, c3_ref, cu_ref, cl_ref, f1_ref, f3_ref, fu_ref, fl_ref, dp_ref, dr_ref, dcx_ref, dcy_ref, dcz_ref, ds_ref, de_ref, put_sem, load_sem, keep_sem, save_sem, gsend_sem, grecv_sem, send_sem, recv_sem, credit):
+def kernel(cap, x0_ref, dy_ref, ids_ref, gate_ref, wd_ref, o1_ref, o3_ref, o2_ref, y_ref, dx_ref, gdense_ref, g1_ref, g3_ref, g2_ref, h1_ref, h3_ref, h2_ref, kz_ref, kp_ref, kq_ref, kh_ref, kda_ref, kdb_ref, acc_ref, cur_ref, x1_ref, hold_ref, gd_ref, rows_ref, columns_ref, w1_ref, w3_ref, w2_ref, z_ref, p_ref, q_ref, h_ref, m1_ref, m3_ref, m2_ref, d1_ref, d3_ref, d2_ref, s1_ref, s3_ref, s2_ref, r11_ref, r12_ref, r31_ref, r32_ref, t1_ref, t3_ref, y11_ref, y12_ref, y31_ref, y32_ref, y21_ref, y22_ref, u1_ref, u2_ref, l1_ref, l2_ref, c1_ref, c3_ref, cu_ref, cl_ref, f1_ref, f3_ref, fu_ref, fl_ref, dp_ref, dr_ref, dcx_ref, dcy_ref, dcz_ref, ds_ref, de_ref, put_sem, load_sem, keep_sem, save_sem, gsend_sem, grecv_sem, send_sem, recv_sem, credit):
     s = pl.program_id(0)
     place = Place()
     gathers = Copies(place, gsend_sem, grecv_sem)
     copies = Copies(place, send_sem, recv_sem)
     given, whole, bufs = (o1_ref, o3_ref, o2_ref), (h1_ref, h3_ref, h2_ref), (w1_ref, w3_ref, w2_ref)
-    kept, acts = (kz_ref, ka_ref, kb_ref), (z_ref, a_ref, b_ref)
+    kept, acts = (kz_ref, kp_ref, kq_ref, kh_ref), (z_ref, p_ref, q_ref, h_ref)
     deferred = (kda_ref, kdb_ref)
     g0, g1 = (Gather(l, gathers, place, given, whole) for l in BUFS)
     rows, ff = s1_ref.shape[1], s2_ref.shape[1]
@@ -334,7 +333,7 @@
     outs = (g1_ref, g3_ref, g2_ref)
     for buf in BUFS:
         for n in ARRAYS:
-            copies.add(("pair", buf, n), stage[n], mate[n].at[buf], "c", 0)
+            copies.add(("pair", buf, n), stage[n].at[buf], mate[n].at[buf], "c", 0)
 
     def ring_blocks(ref, q, me, base, size):
         block = slices(ref, (q,), base, size)
@@ -457,16 +456,22 @@
         dense_refs[follow][index_of[follow]] = total(dense_refs[k])
         dense[follow].start()
 
+    def dense_out(late):
+        return pltpu.make_async_copy(gd_ref, gdense_ref.at[late], keep_sem.at[0, 1])
+
     def dense_pass(late):
         dense["z"].finish()
         ds_ref[...] = total(dcz_ref)
-        gd_ref[late, mine] = ds_ref[...]
+        if late == 0:
+            dense_out(1).wait()
+        gd_ref[mine] = ds_ref[...]
         copies.start("dense pass")
 
     def dense_finish(late):
         copies.arrive("dense pass")
-        gd_ref[late, theirs] = de_ref[...]
+        gd_ref[theirs] = de_ref[...]
         copies.sent("dense pass")
+        dense_out(late).start()
 
     def copy(src, dst, sem):
         return pltpu.make_async_copy(src, dst, sem)
@@ -477,8 +482,8 @@
             yield copy(src, bufs[n].at[buf], load_sem.at[buf, n])
 
     def saved(layer, slot, buf):
-        for n in ARRAYS:
-            yield copy(kept[n].at[layer, slot], acts[n].at[buf], load_sem.at[buf, 3 + n])
+        for n, (src, dst) in enumerate(zip(kept, acts)):
+            yield copy(src.at[layer, slot], dst.at[buf], load_sem.at[buf, 3 + n])
 
     def forward_loads(step, do):
         buf, slot = step % 2, step % SLOTS
@@ -507,7 +512,7 @@
         return [copy(bufs[n].at[step % 2], whole[n].at[step // SLOTS, step % SLOTS], keep_sem.at[step % 2, n]) for n in ARRAYS]
 
     def saves(step):
-        return [copy(acts[n].at[step % 2], kept[n].at[step // SLOTS, step % SLOTS], save_sem.at[step % 2, n]) for n in ARRAYS]
+        return [copy(src.at[step % 2], dst.at[step // SLOTS, step % SLOTS], save_sem.at[step % 2, n]) for n, (src, dst) in enumerate(zip(acts, kept))]
 
     def defers(step):
         return [copy(acts[n + 1].at[2], deferred[n].at[SLOTS - 1 - step % SLOTS], save_sem.at[0, n]) for n in BUFS]
@@ -552,17 +557,17 @@
     on, done = lambda q: lambda: reduce_onward(q), lambda q: lambda: reduce_finish(q)
     now = lambda: load(s)
     plan(before, 0, [g0.second, g0.lead], [g0.third, g0.follow, g0.lead_onward], [g1.begin, g0.follow_onward, g0.complete_y, now, g0.last])
-    plan(before, 3, [g0.passed_left, g1.second], [g0.passed_right, g0.last_onward, g1.lead], [g1.third], [g0.complete_last, now, g1.follow], [g0.passed_last, now, g1.lead_onward])
-    plan(before, SLOTS + 1, [g1.follow_onward], [g1.complete_y, now, g1.last], [g1.passed_left], [g1.passed_right], [g1.last_onward], [g1.complete_last, now], [g1.passed_last, now])
-    unready = (1, 5, 6, SLOTS + 1, SLOTS + 5, SLOTS + 6)
+    plan(before, 3, [g0.passed_left, g1.second], [g0.last_onward, g1.lead], [g0.complete_last, now, g1.third, g0.passed_right], [g1.follow], [g0.passed_last, now, g1.lead_onward])
+    plan(before, SLOTS + 1, [g1.follow_onward], [g1.complete_y, now, g1.last], [g1.passed_left], [g1.last_onward], [g1.complete_last, now, g1.passed_right], [], [g1.passed_last, now])
+    unready = (1, 4, 6, SLOTS + 1, SLOTS + 4, SLOTS + 6)
     late = ("x", "z", "u", "l")
     plan(before, WEIGHTS0, [lambda: copies.start("dense pair")], [inner_finish], [], [lambda: cross_onward(*late), dense["y"].onward], [], [], [lambda: dense_next("y", "x")])
     plan(middle, WEIGHTS0, [dense_sum, y_finish], [], [], [], [lambda: cross_finish(1, *late)], [], [], [lambda: final_onward(1, *late)])
     plan(before, INPUTS0 + 1, [dense["x"].onward], [lambda: final_finish(1, *late)], [lambda: dense_next("x", "z")], [], [dense["z"].onward], [lambda: pass_finish(1)], [lambda: dense_pass(1)])
     for base in (WEIGHTS1, WEIGHTS0):
-        plan(before, base + 2, [on_y["w"].start], [], [], [], [on_y["w"].onward])
-        plan(middle, base + 3, [on(0)], [], [done(0), y_start], [on(1)], [on(2)])
-        plan(before, base + SLOTS, [done(1)], [], [done(2), y_onward], [on(3)], [w_finish], [], [done(3), inner_onward])
+        plan(before, base + 3, [on_y["w"].start], [], [], [done(0), y_start, on_y["w"].onward])
+        plan(middle, base + 4, [on(0)], [], [on(1)], [on(2)])
+        plan(before, base + SLOTS, [], [done(1)], [done(2), y_onward], [on(3)], [], [w_finish], [done(3)], [inner_onward])
         for step, q in OWN_STEPS.items():
             plan(after, base + step, [lambda q=q: reduce_start(q)])
 
@@ -583,13 +588,18 @@
     phase, t = s // SLOTS, s % SLOTS
     forth, back = s % 2, (s + 1) % 2
 
+    def bring(ref, hold):
+        return copy(ref, hold, keep_sem.at[1, 0])
+
     @pl.when(s == 0)
     def _():
+        bring(x0_ref, hold_ref).start()
         load(0)
         greet(place)
         g0.begin()
         load(1)
         route(ids_ref, gate_ref, rows_ref, columns_ref, place)
+        bring(x0_ref, hold_ref).wait()
 
     def enter(x):
         cur_ref[...] = (x.astype(F32) + dot(x, wd_ref[phase])).astype(BF16)
@@ -609,7 +619,7 @@
         @pl.when(t < 2)
         def _():
             start(keeps(s))
-            pl.when(s == 0)(lambda: enter(x0_ref[...]))
+            pl.when(s == 0)(lambda: enter(hold_ref[...]))
             pl.when(s == SLOTS)(lambda: enter(x1_ref[...]))
 
         layer, slot = phase, t
@@ -617,9 +627,13 @@
         z_ref[forth] = z
         a = dot(z, w1_ref[forth]).astype(BF16)
         b = dot(z, w3_ref[forth]).astype(BF16)
-        a_ref[forth] = a
-        b_ref[forth] = b
-        h = (jax.nn.silu(a.astype(F32)) * b.astype(F32)).astype(BF16)
+        a, b = a.astype(F32), b.astype(F32)
+        sig = jax.nn.sigmoid(a)
+        act = a * sig
+        h = (act * b).astype(BF16)
+        p_ref[forth] = act.astype(BF16)
+        q_ref[forth] = (b * (sig + act * (1.0 - sig))).astype(BF16)
+        h_ref[forth] = h
         o = dot(h, w2_ref[forth]).astype(BF16)
         acc_ref[...] += column(columns_ref, layer, SLOTS + slot) * dot(one_hot_t(columns_ref, layer, slot, cap), o)
         pl.when(s < WEIGHTS1 - 1)(lambda: start(saves(s)))
@@ -639,11 +653,12 @@
         def _():
             moved = copy(hold_ref, y_ref, keep_sem.at[0, 0])
             moved.start()
+            bring(dy_ref, cur_ref).start()
             wait(saves(s - 2))
             gathers.drain()
+            bring(dy_ref, cur_ref).wait()
             moved.wait()
-            cur_ref[...] = dy_ref[...]
-            acc_ref[...] = dy_ref[...].astype(F32)
+            acc_ref[...] = cur_ref[...].astype(F32)
 
         pl.when(s > WEIGHTS1)(lambda: wait(weights_loads(s)))
         pl.when(t > 0)(lambda: wait(defers(s - 1)))
@@ -653,43 +668,41 @@
         grad_gated = (column(columns_ref, layer, SLOTS + slot) * cur_ref[...].astype(F32)).astype(BF16)
         do = dot(one_hot(rows_ref, layer, slot, cap), grad_gated).astype(BF16)
         dh = dot_nt(do, w2_ref[back])
-        a = a_ref[back].astype(F32)
-        b = b_ref[back].astype(F32)
-        sig = jax.nn.sigmoid(a)
-        act = a * sig
-        h = (act * b).astype(BF16)
-        db = (dh * act).astype(BF16)
-        da = (dh * b * sig * (1.0 + a * (1.0 - sig))).astype(BF16)
-        a_ref[2] = da
-        b_ref[2] = db
-        z = z_ref[back]
+        db = (dh * p_ref[back].astype(F32)).astype(BF16)
+        da = (dh * q_ref[back].astype(F32)).astype(BF16)
+        p_ref[2] = da
+        q_ref[2] = db
+        z, h = z_ref[back], h_ref[back]
         start(defers(s))
         hooks(middle, WEIGHTS1, WEIGHTS0)
 
-        def weight_grad(n):
-            return dot_tn(*((z, da), (z, db), (h, do))[n])
+        def weight_grads():
+            return dot_tn(z, da), dot_tn(z, db), dot_tn(h, do)
 
         is_own = functools.reduce(jnp.logical_or, [t == step for step in OWN_STEPS])
         group = t // 4 + t // 5 + t // 7
-        into = (t // 2 + t // 3) % 2
+        into = (t + t // 3 + t // 6) % 2
         turn = t + (1 - layer) * SLOTS
 
         @pl.when(jnp.logical_not(is_own))
         def _():
+            for buf in BUFS:
+                pl.when((turn >= 3) & (into == buf))(lambda: copies.sent(*[("pair", buf, n) for n in ARRAYS]))
+
+            for ref, grad in zip(stage, weight_grads()):
+                ref[into] = grad.astype(BF16)
+
             pl.when(turn >= 3)(lambda: pl.semaphore_wait(credit.at[into], 1))
-            for n, ref in enumerate(stage):
-                for buf in BUFS:
-                    pl.when((turn > 0) & (into == 1 - buf))(lambda: copies.sent(("pair", buf, n)))
-                ref[...] = weight_grad(n).astype(BF16)
-                for buf in BUFS:
-                    pl.when(into == buf)(lambda: copies.start(("pair", buf, n)))
+            for buf in BUFS:
+                pl.when(into == buf)(lambda: copies.start(*[("pair", buf, n) for n in ARRAYS]))
 
         @pl.when(is_own)
         def _():
-            for n, ref in enumerate(mine_of):
-                for buf in BUFS:
-                    pl.when(group % 2 == buf)(lambda: copies.arrive(("pair", buf, n)))
-                ref[group] = (weight_grad(n) + mate[n][group % 2].astype(F32)).astype(BF16)
+            for buf in BUFS:
+                pl.when(group % 2 == buf)(lambda: copies.arrive(*[("pair", buf, n) for n in ARRAYS]))
+
+            for ref, add, grad in zip(mine_of, mate, weight_grads()):
+                ref[group] = (grad + add[group % 2].astype(F32)).astype(BF16)
 
             @pl.when(turn < 2 * SLOTS - 3)
             def _():
@@ -711,25 +724,25 @@
         pl.when(t == 0)(lambda: wait(defers(s - 1)))
         pl.when(t < SLOTS - 1)(lambda: start(inputs_loads(s + 1)))
         pl.when(s == WEIGHTS0 - 1)(lambda: start(weights_loads(s + 1)))
-        dz = (dot_nt(a_ref[back], w1_ref[back]) + dot_nt(b_ref[back], w3_ref[back])).astype(BF16)
+        dz = (dot_nt(p_ref[back], w1_ref[back]) + dot_nt(q_ref[back], w3_ref[back])).astype(BF16)
         acc_ref[...] += dot(one_hot_t(columns_ref, layer, slot, cap), dz)
 
         @pl.when(s == WEIGHTS0 - 1)
         def _():
             leave_back(1, x1_ref[...], cur_ref)
             acc_ref[...] = cur_ref[...].astype(F32)
+            bring(x0_ref, x1_ref).start()
+            bring(x0_ref, x1_ref).wait()
 
         @pl.when(s == STEPS - 1)
         def _():
-            leave_back(0, x0_ref[...], hold_ref)
+            leave_back(0, x1_ref[...], hold_ref)
             moved = copy(hold_ref, dx_ref, keep_sem.at[0, 0])
             moved.start()
             ending()
-            dense_out = copy(gd_ref, gdense_ref, keep_sem.at[0, 1])
-            dense_out.start()
-            copies.sent(*[("pair", 1, n) for n in ARRAYS])
+            copies.sent(*[("pair", buf, n) for buf in BUFS for n in ARRAYS])
             moved.wait()
-            dense_out.wait()
+            dense_out(0).wait()
 
 
 def step(cap, x0, dy, ids, gates, wd, w1, w3, w2):
@@ -749,10 +762,10 @@
 
     shape = jax.ShapeDtypeStruct
     ups, downs = [(width, ff), (width, ff), (ff, width)], [(quarter, ff), (part, width)]
-    acts = [(cap, width), (cap, ff), (cap, ff)]
-    scratch = [pltpu.VMEM((tokens, width), F32)] + [buf(tokens, width)] * 3 + [buf(layers, width, width), pltpu.VMEM((layers, SLOTS, tokens), jnp.int32), pltpu.VMEM((layers, tokens, LANES), F32)]
-    scratch += [buf(2, *u) for u in ups] + [buf(2, *acts[0]), buf(3, *acts[1]), buf(3, *acts[2])]
-    scratch += [buf(*u) for u in ups] + [buf(2, *u) for u in ups] + [buf(SIDE, *u) for u in ups]
+    acts = [(cap, width), (cap, ff), (cap, ff), (cap, ff)]
+    scratch = [pltpu.VMEM((tokens, width), F32)] + [buf(tokens, width)] * 3 + [buf(width, width), pltpu.VMEM((layers, SLOTS, tokens), jnp.int32), pltpu.VMEM((layers, tokens, LANES), F32)]
+    scratch += [buf(2, *u) for u in ups] + [buf(n, *a) for n, a in zip((2, 3, 3, 2), acts)]
+    scratch += [buf(2, *u) for u in ups] * 2 + [buf(SIDE, *u) for u in ups]
     scratch += [buf(SIDE, 2, quarter // 2, ff), buf(SIDE, 2, quarter, ff)] * 2
     scratch += [buf(SIDE, quarter, ff)] * 2
     scratch += [buf(2, quarter // 2, ff), buf(2, quarter, ff)] * 2 + [buf(2, ff // 2, width), buf(2, ff, width)]
@@ -760,13 +773,13 @@
     scratch += [buf(SIDE, quarter, ff)] * 2 + [buf(SIDE, part, width)] * 2
     scratch += [buf(quarter, ff)] * 2 + [buf(part, width)] * 2
     scratch += [buf(width, width), buf(width // 2, width)] + [buf(SIDE, width // 2, width)] * 3 + [buf(width // 2, width)] * 2
-    scratch += [dma(4), dma(2, 6), dma(2, 3), dma(2, 3), dma(GATHER_COPIES), dma(GATHER_COPIES), dma(REDUCE_COPIES), dma(REDUCE_COPIES), pltpu.SemaphoreType.REGULAR((2,))]
+    scratch += [dma(4), dma(2, 7), dma(2, 3), dma(2, 4), dma(GATHER_COPIES), dma(GATHER_COPIES), dma(REDUCE_COPIES), dma(REDUCE_COPIES), pltpu.SemaphoreType.REGULAR((2,))]
     results = [(tokens, width), (tokens, width), (layers, width, width)]
     kept = [(layers, local, *u) for u in ups] + [(layers, SLOTS, *u) for u in ups + acts] + [(SLOTS, cap, ff)] * 2
     return pl.pallas_call(
         functools.partial(kernel, cap),
         grid=(STEPS,),
-        in_specs=[fixed(v.shape) for v in (x0, dy, ids, gates, wd)] + [hbm] * 3,
+        in_specs=[hbm] * 2 + [fixed(v.shape) for v in (ids, gates, wd)] + [hbm] * 3,
         out_specs=[hbm] * len(results + kept),
         out_shape=[shape(r, BF16) for r in results + kept],
         scratch_shapes=scratch,

time: 279 us -> 282 us (1.011)
  Pallas kernels: 278 us -> 281 us
    pallas_call x1, Pallas kernels: 269 us -> 272 us  [step(): pl.pallas_call(functools.partial(kernel, cap), grid=(STEPS,), in_specs=[h...]
where the time goes in v6:
time: 282 us
  Pallas kernels  281 us (100%)
    pallas_call x1, Pallas kernels, step(): pl.pallas_call(functools.partial(kernel, cap), grid=(STEPS,), in_specs=[h...  272 us
    pallas_call x1, Pallas kernels, take(): pl.pallas_call(functools.partial(take_kernel, count), in_specs=[hbm] * co...  8.93 us

profile of v6, /device:TPU:1, one launch (start us, length us, event | category | flops | bytes accessed | tf_op | source)
XLA Modules:
  0.0 281.9 jit_solution(12880335192667482067)
XLA Ops:
  0.6 272.4 %step.1 = (bf16[1024,384]{1,0:T(8,128)(2,1)}, bf16[1024,384]{1,0:T(8,128)(2,1)}, bf16[2,384,384]{2,1,0:T(8,128)(2,1)}, bf16[2,2,384,1024]{3,2,1,0:T(8,128)(2,1)}...) custom-call(bf16[1024,384]{1,0:T(8,128)(2,1)} %x0_ref.1, ...), custom_call_target="tpu_custom_call" | custom-call | tf_op jit(solution)/shard_map/step/pallas_call | solution.py:779
  273.0 8.9 %take.1 = (bf16[1024,384]{1,0:T(8,128)(2,1)}, bf16[1024,384]{1,0:T(8,128)(2,1)}, bf16[2,384,384]{2,1,0:T(8,128)(2,1)}, bf16[2,2,384,1024]{3,2,1,0:T(8,128)(2,1)}...) custom-call(bf16[1024,384]{1,0:T(8,128)(2,1)} %get-tuple-element.12.refs_0_, ...), custom_call_target="tpu_custom_call" | custom-call | tf_op jit(solution)/shard_map/take/pallas_call | solution.py:807

commit v7 on v6

--- a/solution.py
+++ b/solution.py
@@ -239,12 +239,18 @@
     dst[...] = (dst[...].astype(F32) + src[...].astype(F32)).astype(BF16)
 
 
+def cut(rows, half):
+    first = (rows // 2 + 15) // 16 * 16
+    return (half * first, first + half * (rows - 2 * first))
+
+
 class RingSum:
     def __init__(self, copies, name, axis, block, first, second):
-        self.copies, self.name, self.block, self.first, self.second = copies, name, block, first, second
+        self.copies, self.block, self.second = copies, block, second
+        self.first = [first.at[half, pl.ds(0, block(2, half).shape[0])] for half in BUFS]
         self.early, self.later = ([(name, when, step) for step in WAYS] for when in ("early", "later"))
         for half, step in enumerate(WAYS):
-            copies.add(self.early[half], block(2, half), first.at[half], axis, step)
+            copies.add(self.early[half], block(2, half), self.first[half], axis, step)
             copies.add(self.later[half], block(step, None), second.at[half], axis, step)
 
     def start(self):
@@ -253,7 +259,7 @@
     def onward(self):
         self.copies.arrive(*self.early)
         for half in BUFS:
-            add_to(self.block(WAYS[half], half), self.first.at[half])
+            add_to(self.block(WAYS[half], half), self.first[half])
             self.copies.start(self.later[half])
         self.copies.sent(*self.early)
 
@@ -290,8 +296,8 @@
     def block(index, half):
         start, rows = base + index * size, size
         if half is not None:
-            rows = size // 2
-            start = start + half * rows
+            skip, rows = cut(size, half)
+            start = start + skip
         return ref.at[(*lead, pl.ds(pl.multiple_of(start, 16), rows))]
 
     return block
@@ -301,8 +307,7 @@
     def block(index, half):
         if half is None:
             return ref.at[index]
-        rows = ref.shape[1] // 2
-        return ref.at[index, pl.ds(half * rows, rows)]
+        return ref.at[index, pl.ds(*cut(ref.shape[1], half))]
 
     return block
 
@@ -312,17 +317,17 @@
 
 
 OWN_STEPS = {2: 0, 4: 1, 5: 2, 7: 3}
-REDUCE_COPIES = 107
+REDUCE_COPIES = 111
 WEIGHTS1, INPUTS1, WEIGHTS0, INPUTS0, STEPS = (n * SLOTS for n in range(2, 7))
 
 
-def kernel(cap, x0_ref, dy_ref, ids_ref, gate_ref, wd_ref, o1_ref, o3_ref, o2_ref, y_ref, dx_ref, gdense_ref, g1_ref, g3_ref, g2_ref, h1_ref, h3_ref, h2_ref, kz_ref, kp_ref, kq_ref, kh_ref, kda_ref, kdb_ref, acc_ref, cur_ref, x1_ref, hold_ref, gd_ref, rows_ref, columns_ref, w1_ref, w3_ref, w2_ref, z_ref, p_ref, q_ref, h_ref, m1_ref, m3_ref, m2_ref, d1_ref, d3_ref, d2_ref, s1_ref, s3_ref, s2_ref, r11_ref, r12_ref, r31_ref, r32_ref, t1_ref, t3_ref, y11_ref, y12_ref, y31_ref, y32_ref, y21_ref, y22_ref, u1_ref, u2_ref, l1_ref, l2_ref, c1_ref, c3_ref, cu_ref, cl_ref, f1_ref, f3_ref, fu_ref, fl_ref, dp_ref, dr_ref, dcx_ref, dcy_ref, dcz_ref, ds_ref, de_ref, put_sem, load_sem, keep_sem, save_sem, gsend_sem, grecv_sem, send_sem, recv_sem, credit):
+def kernel(cap, x0_ref, dy_ref, ids_ref, gate_ref, wd_ref, o1_ref, o3_ref, o2_ref, y_ref, dx_ref, gdense_ref, g1_ref, g3_ref, g2_ref, h1_ref, h3_ref, h2_ref, kz_ref, ka_ref, kb_ref, kda_ref, kdb_ref, acc_ref, cur_ref, x1_ref, hold_ref, gd_ref, rows_ref, columns_ref, w1_ref, w3_ref, w2_ref, z_ref, a_ref, b_ref, m1_ref, m3_ref, m2_ref, d1_ref, d3_ref, d2_ref, s1_ref, s3_ref, s2_ref, r11_ref, r12_ref, r31_ref, r32_ref, t1_ref, t3_ref, y11_ref, y12_ref, y31_ref, y32_ref, y21_ref, y22_ref, u1_ref, u2_ref, l1_ref, l2_ref, c1_ref, c3_ref, cu_ref, cl_ref, f1_ref, f3_ref, fu_ref, fl_ref, dp_ref, dr_ref, ds_ref, e1_ref, e2_ref, dcx_ref, dcz_ref, dcy_ref, de_ref, put_sem, load_sem, keep_sem, save_sem, gsend_sem, grecv_sem, send_sem, recv_sem, credit):
     s = pl.program_id(0)
     place = Place()
     gathers = Copies(place, gsend_sem, grecv_sem)
     copies = Copies(place, send_sem, recv_sem)
     given, whole, bufs = (o1_ref, o3_ref, o2_ref), (h1_ref, h3_ref, h2_ref), (w1_ref, w3_ref, w2_ref)
-    kept, acts = (kz_ref, kp_ref, kq_ref, kh_ref), (z_ref, p_ref, q_ref, h_ref)
+    kept, acts = (kz_ref, ka_ref, kb_ref), (z_ref, a_ref, b_ref)
     deferred = (kda_ref, kdb_ref)
     g0, g1 = (Gather(l, gathers, place, given, whole) for l in BUFS)
     rows, ff = s1_ref.shape[1], s2_ref.shape[1]
@@ -375,10 +380,11 @@
         for n, out in enumerate(outs):
             copies.add(("pass", n, late), out.at[late, place.c], out.at[late, place.c], "c", 0, None if late else ("pass", n, 1))
     copies.add("dense pair", dp_ref.at[theirs], dr_ref, "c", 0)
-    copies.add("dense pass", ds_ref, de_ref, "c", 0)
-    dense_refs = {"y": dcy_ref, "x": dcx_ref, "z": dcz_ref}
-    index_of = {"y": place.y, "x": place.x, "z": place.z}
-    dense = {k: RingSpread(copies, ("dense", k), k, index_of[k], slabs(ref)) for k, ref in dense_refs.items()}
+    copies.add("dense pass", dcy_ref, de_ref, "c", 0)
+    piece = half_d // SIDE
+    dense_block = slices(ds_ref, (), 0, piece)
+    dense_sums = RingSum(copies, "dense sums", "y", lambda offset, half: dense_block((place.y + offset + SIDE) % SIDE, half), e1_ref, e2_ref)
+    dense = {k: RingSpread(copies, ("dense", k), k, me, block) for k, me, block in (("x", place.x, slabs(dcx_ref)), ("z", place.z, slabs(dcz_ref)), ("y", place.y, slices(dcy_ref, (), 0, piece)))}
 
     def reduce_start(q):
         for k in ("x", "z"):
@@ -447,24 +453,32 @@
 
     def dense_sum():
         copies.arrive("dense pair")
-        dcy_ref[place.y] = (dp_ref[mine].astype(F32) + dr_ref[...].astype(F32)).astype(BF16)
+        ds_ref[...] = (dp_ref[mine].astype(F32) + dr_ref[...].astype(F32)).astype(BF16)
         copies.sent("dense pair")
+        dense_sums.start()
+
+    def dense_to_x():
+        dense_sums.finish(dcx_ref.at[place.x])
+        dense["x"].start()
+
+    def dense_to_z():
+        dense["x"].finish()
+        dcz_ref[place.z] = total(dcx_ref)
+        dense["z"].start()
+
+    def dense_to_y():
+        dense["z"].finish()
+        dcy_ref[pl.ds(pl.multiple_of(place.y * piece, 16), piece)] = total(dcz_ref)
         dense["y"].start()
-
-    def dense_next(k, follow):
-        dense[k].finish()
-        dense_refs[follow][index_of[follow]] = total(dense_refs[k])
-        dense[follow].start()
 
     def dense_out(late):
         return pltpu.make_async_copy(gd_ref, gdense_ref.at[late], keep_sem.at[0, 1])
 
     def dense_pass(late):
-        dense["z"].finish()
-        ds_ref[...] = total(dcz_ref)
+        dense["y"].finish()
         if late == 0:
             dense_out(1).wait()
-        gd_ref[mine] = ds_ref[...]
+        gd_ref[mine] = dcy_ref[...]
         copies.start("dense pass")
 
     def dense_finish(late):
@@ -485,15 +499,6 @@
         for n, (src, dst) in enumerate(zip(kept, acts)):
             yield copy(src.at[layer, slot], dst.at[buf], load_sem.at[buf, 3 + n])
 
-    def forward_loads(step, do):
-        buf, slot = step % 2, step % SLOTS
-        for is_given in (True, False):
-
-            @pl.when((slot < 2) == is_given)
-            def _():
-                for item in weights(step // SLOTS, slot, ARRAYS, buf, is_given):
-                    do(item)
-
     def weights_loads(step):
         layer, slot, buf = layer_of(step), SLOTS - 1 - step % SLOTS, (step + 1) % 2
         return [*weights(layer, slot, [2], buf), *saved(layer, slot, buf)]
@@ -503,7 +508,9 @@
         return [*weights(layer, slot, BUFS, buf)] + [copy(deferred[n].at[slot], acts[n + 1].at[buf], load_sem.at[buf, 4 + n]) for n in BUFS]
 
     def load(step):
-        forward_loads(step, lambda item: item.start())
+        slot = step % SLOTS
+        for is_given in (True, False):
+            pl.when((slot < 2) == is_given)(lambda: start(weights(step // SLOTS, slot, ARRAYS, step % 2, is_given)))
 
     def layer_of(step):
         return 1 - (step - WEIGHTS1) // (2 * SLOTS)
@@ -526,27 +533,29 @@
             item.start()
 
     def ending():
+        dense_finish(1)
+        copies.start("dense pair")
         y_finish()
         inner_finish()
-        dense_finish(1)
-        copies.start("dense pair")
         dense_sum()
+        dense_sums.onward()
         cross_onward("x", "z")
+        dense_to_x()
         cross_onward("u", "l")
+        dense["x"].onward()
+        cross_finish(0, "x", "z")
+        dense_to_z()
+        cross_finish(0, "u", "l")
+        dense["z"].onward()
+        dense_to_y()
+        final_onward(0, "x", "z")
         dense["y"].onward()
-        cross_finish(0, "x", "z")
-        cross_finish(0, "u", "l")
-        dense_next("y", "x")
-        final_onward(0, "x", "z")
-        dense["x"].onward()
         final_onward(0, "u", "l")
-        dense_next("x", "z")
+        dense_pass(0)
         final_finish(0, "x", "z")
         final_finish(0, "u", "l")
-        dense["z"].onward()
-        dense_pass(0)
+        dense_finish(0)
         pass_finish(0)
-        dense_finish(0)
 
     before, middle, after = {}, {}, {}
 
@@ -561,13 +570,15 @@
     plan(before, SLOTS + 1, [g1.follow_onward], [g1.complete_y, now, g1.last], [g1.passed_left], [g1.last_onward], [g1.complete_last, now, g1.passed_right], [], [g1.passed_last, now])
     unready = (1, 4, 6, SLOTS + 1, SLOTS + 4, SLOTS + 6)
     late = ("x", "z", "u", "l")
-    plan(before, WEIGHTS0, [lambda: copies.start("dense pair")], [inner_finish], [], [lambda: cross_onward(*late), dense["y"].onward], [], [], [lambda: dense_next("y", "x")])
-    plan(middle, WEIGHTS0, [dense_sum, y_finish], [], [], [], [lambda: cross_finish(1, *late)], [], [], [lambda: final_onward(1, *late)])
-    plan(before, INPUTS0 + 1, [dense["x"].onward], [lambda: final_finish(1, *late)], [lambda: dense_next("x", "z")], [], [dense["z"].onward], [lambda: pass_finish(1)], [lambda: dense_pass(1)])
+    plan(before, WEIGHTS0, [lambda: copies.start("dense pair"), inner_onward], [], [inner_finish, dense_sums.onward], [lambda: cross_onward("x", "z"), dense_to_x], [lambda: cross_onward("u", "l")])
+    plan(middle, WEIGHTS0, [dense_sum, y_finish], [], [], [], [dense["x"].onward], [lambda: cross_finish(1, *late)], [dense_to_z])
+    plan(before, INPUTS0, [dense["z"].onward], [lambda: final_onward(1, *late)], [dense_to_y], [lambda: final_finish(1, *late)], [dense["y"].onward], [], [lambda: dense_pass(1)], [lambda: pass_finish(1)])
+    plan(before, INPUTS1 + 6, [w_finish])
+    plan(before, INPUTS0 + 5, [w_finish], [], [inner_onward])
     for base in (WEIGHTS1, WEIGHTS0):
-        plan(before, base + 3, [on_y["w"].start], [], [], [done(0), y_start, on_y["w"].onward])
-        plan(middle, base + 4, [on(0)], [], [on(1)], [on(2)])
-        plan(before, base + SLOTS, [], [done(1)], [done(2), y_onward], [on(3)], [], [w_finish], [done(3)], [inner_onward])
+        plan(before, base + 3, [on_y["w"].start], [], [], [on_y["w"].onward])
+        plan(middle, base + 4, [on(0)], [], [done(0), y_start, on(1)], [on(2)])
+        plan(before, base + SLOTS, [], [done(1)], [done(2), y_onward], [on(3)], [], [], [done(3)])
         for step, q in OWN_STEPS.items():
             plan(after, base + step, [lambda q=q: reduce_start(q)])
 
@@ -611,29 +622,27 @@
     @pl.when(s < WEIGHTS1)
     def _():
         hooks(before, 0, SLOTS)
-        forward_loads(s, lambda item: item.wait())
         pl.when(s > 1)(lambda: wait(saves(s - 2)))
         ahead = functools.reduce(jnp.logical_and, [s != step for step in unready], (s > 0) & (s < WEIGHTS1 - 1))
         pl.when(ahead)(lambda: load(s + 1))
 
         @pl.when(t < 2)
         def _():
-            start(keeps(s))
             pl.when(s == 0)(lambda: enter(hold_ref[...]))
             pl.when(s == SLOTS)(lambda: enter(x1_ref[...]))
 
         layer, slot = phase, t
         z = dot(one_hot(rows_ref, layer, slot, cap), cur_ref[...]).astype(BF16)
         z_ref[forth] = z
+        come = list(weights(layer, slot, ARRAYS, forth))
+        wait(come[:2])
         a = dot(z, w1_ref[forth]).astype(BF16)
         b = dot(z, w3_ref[forth]).astype(BF16)
-        a, b = a.astype(F32), b.astype(F32)
-        sig = jax.nn.sigmoid(a)
-        act = a * sig
-        h = (act * b).astype(BF16)
-        p_ref[forth] = act.astype(BF16)
-        q_ref[forth] = (b * (sig + act * (1.0 - sig))).astype(BF16)
-        h_ref[forth] = h
+        a_ref[forth] = a
+        b_ref[forth] = b
+        h = (jax.nn.silu(a.astype(F32)) * b.astype(F32)).astype(BF16)
+        wait(come[2:])
+        pl.when(t < 2)(lambda: start(keeps(s)))
         o = dot(h, w2_ref[forth]).astype(BF16)
         acc_ref[...] += column(columns_ref, layer, SLOTS + slot) * dot(one_hot_t(columns_ref, layer, slot, cap), o)
         pl.when(s < WEIGHTS1 - 1)(lambda: start(saves(s)))
@@ -668,11 +677,16 @@
         grad_gated = (column(columns_ref, layer, SLOTS + slot) * cur_ref[...].astype(F32)).astype(BF16)
         do = dot(one_hot(rows_ref, layer, slot, cap), grad_gated).astype(BF16)
         dh = dot_nt(do, w2_ref[back])
-        db = (dh * p_ref[back].astype(F32)).astype(BF16)
-        da = (dh * q_ref[back].astype(F32)).astype(BF16)
-        p_ref[2] = da
-        q_ref[2] = db
-        z, h = z_ref[back], h_ref[back]
+        a = a_ref[back].astype(F32)
+        b = b_ref[back].astype(F32)
+        sig = jax.nn.sigmoid(a)
+        act = a * sig
+        h = (act * b).astype(BF16)
+        db = (dh * act).astype(BF16)
+        da = (dh * b * (sig + act * (1.0 - sig))).astype(BF16)
+        a_ref[2] = da
+        b_ref[2] = db
+        z = z_ref[back]
         start(defers(s))
         hooks(middle, WEIGHTS1, WEIGHTS0)
 
@@ -724,7 +738,7 @@
         pl.when(t == 0)(lambda: wait(defers(s - 1)))
         pl.when(t < SLOTS - 1)(lambda: start(inputs_loads(s + 1)))
         pl.when(s == WEIGHTS0 - 1)(lambda: start(weights_loads(s + 1)))
-        dz = (dot_nt(p_ref[back], w1_ref[back]) + dot_nt(q_ref[back], w3_ref[back])).astype(BF16)
+        dz = (dot_nt(a_ref[back], w1_ref[back]) + dot_nt(b_ref[back], w3_ref[back])).astype(BF16)
         acc_ref[...] += dot(one_hot_t(columns_ref, layer, slot, cap), dz)
 
         @pl.when(s == WEIGHTS0 - 1)
@@ -748,7 +762,7 @@
 def step(cap, x0, dy, ids, gates, wd, w1, w3, w2):
     tokens, width = dy.shape
     layers, local, _, ff = w1.shape
-    quarter, part = width // SIDE, ff // 2 // SIDE
+    quarter, part, piece = width // SIDE, ff // 2 // SIDE, width // 2 // SIDE
     hbm = pl.BlockSpec(memory_space=pl.ANY)
 
     def fixed(shape):
@@ -762,9 +776,9 @@
 
     shape = jax.ShapeDtypeStruct
     ups, downs = [(width, ff), (width, ff), (ff, width)], [(quarter, ff), (part, width)]
-    acts = [(cap, width), (cap, ff), (cap, ff), (cap, ff)]
+    acts = [(cap, width), (cap, ff), (cap, ff)]
     scratch = [pltpu.VMEM((tokens, width), F32)] + [buf(tokens, width)] * 3 + [buf(width, width), pltpu.VMEM((layers, SLOTS, tokens), jnp.int32), pltpu.VMEM((layers, tokens, LANES), F32)]
-    scratch += [buf(2, *u) for u in ups] + [buf(n, *a) for n, a in zip((2, 3, 3, 2), acts)]
+    scratch += [buf(2, *u) for u in ups] + [buf(n, *a) for n, a in zip((2, 3, 3), acts)]
     scratch += [buf(2, *u) for u in ups] * 2 + [buf(SIDE, *u) for u in ups]
     scratch += [buf(SIDE, 2, quarter // 2, ff), buf(SIDE, 2, quarter, ff)] * 2
     scratch += [buf(SIDE, quarter, ff)] * 2
@@ -772,8 +786,8 @@
     scratch += [buf(2, part // 2, width), buf(2, part, width)] * 2
     scratch += [buf(SIDE, quarter, ff)] * 2 + [buf(SIDE, part, width)] * 2
     scratch += [buf(quarter, ff)] * 2 + [buf(part, width)] * 2
-    scratch += [buf(width, width), buf(width // 2, width)] + [buf(SIDE, width // 2, width)] * 3 + [buf(width // 2, width)] * 2
-    scratch += [dma(4), dma(2, 7), dma(2, 3), dma(2, 4), dma(GATHER_COPIES), dma(GATHER_COPIES), dma(REDUCE_COPIES), dma(REDUCE_COPIES), pltpu.SemaphoreType.REGULAR((2,))]
+    scratch += [buf(width, width)] + [buf(width // 2, width)] * 2 + [buf(2, piece, width)] * 2 + [buf(SIDE, piece, width)] * 2 + [buf(width // 2, width)] * 2
+    scratch += [dma(4), dma(2, 6), dma(2, 3), dma(2, 3), dma(GATHER_COPIES), dma(GATHER_COPIES), dma(REDUCE_COPIES), dma(REDUCE_COPIES), pltpu.SemaphoreType.REGULAR((2,))]
     results = [(tokens, width), (tokens, width), (layers, width, width)]
     kept = [(layers, local, *u) for u in ups] + [(layers, SLOTS, *u) for u in ups + acts] + [(SLOTS, cap, ff)] * 2
     return pl.pallas_call(

time: 282 us -> 276 us (0.979)
  Pallas kernels: 281 us -> 275 us
    pallas_call x1, Pallas kernels: 272 us -> 266 us  [step(): pl.pallas_call(functools.partial(kernel, cap), grid=(STEPS,), in_specs=[h...]
where the time goes in v7:
time: 276 us; the launch traced here: 275 us
  Pallas kernels  275 us (100%)
    pallas_call x1, Pallas kernels, step(): pl.pallas_call(functools.partial(kernel, cap), grid=(STEPS,), in_specs=[h...  266 us
    pallas_call x1, Pallas kernels, take(): pl.pallas_call(functools.partial(take_kernel, count), in_specs=[hbm] * co...  8.93 us

profile of v7, /device:TPU:1, one launch (start us, length us, event | category | flops | bytes accessed | tf_op | source)
XLA Modules:
  0.0 275.3 jit_solution(939827732924635763)
XLA Ops:
  0.6 265.8 %step.1 = (bf16[1024,384]{1,0:T(8,128)(2,1)}, bf16[1024,384]{1,0:T(8,128)(2,1)}, bf16[2,384,384]{2,1,0:T(8,128)(2,1)}, bf16[2,2,384,1024]{3,2,1,0:T(8,128)(2,1)}...) custom-call(bf16[1024,384]{1,0:T(8,128)(2,1)} %x0_ref.1, ...), custom_call_target="tpu_custom_call" | custom-call | tf_op jit(solution)/shard_map/step/pallas_call | solution.py:793
  266.4 8.9 %take.1 = (bf16[1024,384]{1,0:T(8,128)(2,1)}, bf16[1024,384]{1,0:T(8,128)(2,1)}, bf16[2,384,384]{2,1,0:T(8,128)(2,1)}, bf16[2,2,384,1024]{3,2,1,0:T(8,128)(2,1)}...) custom-call(bf16[1024,384]{1,0:T(8,128)(2,1)} %get-tuple-element.12.refs_0_, ...), custom_call_target="tpu_custom_call" | custom-call | tf_op jit(solution)/shard_map/take/pallas_call | solution.py:821

commit v8 on v7

--- a/solution.py
+++ b/solution.py
@@ -82,7 +82,7 @@
 
 def greet(place):
     barrier = pltpu.get_barrier_semaphore()
-    peers = [(axis, step) for axis in "xyz" for step in WAYS] + [("c", 0)]
+    peers = [(axis, step) for axis in "xyz" for step in range(1, SIDE)] + [("c", 0)]
     for axis, step in peers:
         pl.semaphore_signal(barrier, inc=1, device_id=place.at(axis, step), device_id_type=MESH)
     pl.semaphore_wait(barrier, len(peers))
@@ -169,25 +169,21 @@
         self.passed(5)
 
     def begin(self):
-        self.copies.start(*self._keys("y", 2, "x"), *self._keys("y", 3, "z"))
-
-    def second(self):
-        self.copies.sent(*self._keys("y", 2, "x"), *self._keys("y", 3, "z"))
-        self.copies.start(*self._keys("y", 2, "z"), *self._keys("y", 3, "x"))
-
-    def third(self):
-        self.copies.sent(*self._keys("y", 2, "z"), *self._keys("y", 3, "x"))
-        self.copies.start(*self._keys("y", 5, "x"), *self._keys("y", 5, "z"))
+        for slot, color in ((2, "x"), (3, "z"), (2, "z"), (3, "x")):
+            self.copies.start(*self._keys("y", slot, color))
 
     def spread(self, slot, color):
-        self.copies.arrive(*self._keys("y", slot, color))
-        for step in WAYS:
-            self.copies.start(*self._keys("near", slot, color, extra=(step,)))
+        for part in BUFS:
+            self.copies.arrive((self.layer, "y", slot, color, part))
+            self.copies.start(*[(self.layer, "near", slot, color, part, step) for step in WAYS])
+        if (slot, color) in ((2, "x"), (3, "z")):
+            self.copies.start(*self._keys("y", 5, color))
 
     def onward(self, slot, color):
-        for step in WAYS:
-            self.copies.arrive(*self._keys("near", slot, color, extra=(step,)))
-            self.copies.start(*self._keys("far", slot, color, extra=(step,)))
+        for part in BUFS:
+            for step in WAYS:
+                self.copies.arrive((self.layer, "near", slot, color, part, step))
+                self.copies.start((self.layer, "far", slot, color, part, step))
 
     def complete(self, slot):
         for color in ("x", "z"):
@@ -292,6 +288,20 @@
         self.copies.sent(*self.near, *self.far)
 
 
+class Direct:
+    def __init__(self, copies, name, axis, source, target):
+        self.copies, self.keys = copies, [(name, step) for step in range(1, SIDE)]
+        for name, step in self.keys:
+            copies.add((name, step), source(step), target(step), axis, step)
+
+    def start(self):
+        self.copies.start(*self.keys)
+
+    def finish(self):
+        self.copies.arrive(*self.keys)
+        self.copies.sent(*self.keys)
+
+
 def slices(ref, lead, base, size):
     def block(index, half):
         start, rows = base + index * size, size
@@ -317,11 +327,11 @@
 
 
 OWN_STEPS = {2: 0, 4: 1, 5: 2, 7: 3}
-REDUCE_COPIES = 111
+REDUCE_COPIES = 107
 WEIGHTS1, INPUTS1, WEIGHTS0, INPUTS0, STEPS = (n * SLOTS for n in range(2, 7))
 
 
-def kernel(cap, x0_ref, dy_ref, ids_ref, gate_ref, wd_ref, o1_ref, o3_ref, o2_ref, y_ref, dx_ref, gdense_ref, g1_ref, g3_ref, g2_ref, h1_ref, h3_ref, h2_ref, kz_ref, ka_ref, kb_ref, kda_ref, kdb_ref, acc_ref, cur_ref, x1_ref, hold_ref, gd_ref, rows_ref, columns_ref, w1_ref, w3_ref, w2_ref, z_ref, a_ref, b_ref, m1_ref, m3_ref, m2_ref, d1_ref, d3_ref, d2_ref, s1_ref, s3_ref, s2_ref, r11_ref, r12_ref, r31_ref, r32_ref, t1_ref, t3_ref, y11_ref, y12_ref, y31_ref, y32_ref, y21_ref, y22_ref, u1_ref, u2_ref, l1_ref, l2_ref, c1_ref, c3_ref, cu_ref, cl_ref, f1_ref, f3_ref, fu_ref, fl_ref, dp_ref, dr_ref, ds_ref, e1_ref, e2_ref, dcx_ref, dcz_ref, dcy_ref, de_ref, put_sem, load_sem, keep_sem, save_sem, gsend_sem, grecv_sem, send_sem, recv_sem, credit):
+def kernel(cap, x0_ref, dy_ref, ids_ref, gate_ref, wd_ref, o1_ref, o3_ref, o2_ref, y_ref, dx_ref, gdense_ref, g1_ref, g3_ref, g2_ref, h1_ref, h3_ref, h2_ref, kz_ref, ka_ref, kb_ref, kda_ref, kdb_ref, acc_ref, cur_ref, x1_ref, hold_ref, gd_ref, rows_ref, columns_ref, w1_ref, w3_ref, w2_ref, z_ref, a_ref, b_ref, m1_ref, m3_ref, m2_ref, d1_ref, d3_ref, d2_ref, s1_ref, s3_ref, s2_ref, r11_ref, r12_ref, r31_ref, r32_ref, t1_ref, t3_ref, y11_ref, y12_ref, y31_ref, y32_ref, y21_ref, y22_ref, u1_ref, u2_ref, l1_ref, l2_ref, c1_ref, c3_ref, cu_ref, cl_ref, f1_ref, f3_ref, fu_ref, fl_ref, dp_ref, dr_ref, ds_ref, e_ref, dcx_ref, dcz_ref, dcy_ref, de_ref, put_sem, load_sem, keep_sem, save_sem, gsend_sem, grecv_sem, send_sem, recv_sem, credit):
     s = pl.program_id(0)
     place = Place()
     gathers = Copies(place, gsend_sem, grecv_sem)
@@ -383,8 +393,10 @@
     copies.add("dense pass", dcy_ref, de_ref, "c", 0)
     piece = half_d // SIDE
     dense_block = slices(ds_ref, (), 0, piece)
-    dense_sums = RingSum(copies, "dense sums", "y", lambda offset, half: dense_block((place.y + offset + SIDE) % SIDE, half), e1_ref, e2_ref)
-    dense = {k: RingSpread(copies, ("dense", k), k, me, block) for k, me, block in (("x", place.x, slabs(dcx_ref)), ("z", place.z, slabs(dcz_ref)), ("y", place.y, slices(dcy_ref, (), 0, piece)))}
+    dense_sums = Direct(copies, "dense sums", "y", lambda step: dense_block((place.y + step) % SIDE, None), lambda step: e_ref.at[step - 1])
+    gather_block = slices(dcy_ref, (), 0, piece)(place.y, None)
+    own_piece = {"x": dcx_ref.at[place.x], "z": dcz_ref.at[place.z], "y": gather_block}
+    dense = {k: Direct(copies, ("dense", k), k, lambda step, k=k: own_piece[k], lambda step, k=k: own_piece[k]) for k in own_piece}
 
     def reduce_start(q):
         for k in ("x", "z"):
@@ -458,18 +470,21 @@
         dense_sums.start()
 
     def dense_to_x():
-        dense_sums.finish(dcx_ref.at[place.x])
+        dense_sums.finish()
+        mine = dense_block(place.y, None)[...].astype(F32)
+        own_piece["x"][...] = (mine + e_ref[0].astype(F32) + e_ref[1].astype(F32) + e_ref[2].astype(F32)).astype(BF16)
         dense["x"].start()
 
+    def dense_next(k, ref, follow):
+        dense[k].finish()
+        own_piece[follow][...] = total(ref)
+        dense[follow].start()
+
     def dense_to_z():
-        dense["x"].finish()
-        dcz_ref[place.z] = total(dcx_ref)
-        dense["z"].start()
+        dense_next("x", dcx_ref, "z")
 
     def dense_to_y():
-        dense["z"].finish()
-        dcy_ref[pl.ds(pl.multiple_of(place.y * piece, 16), piece)] = total(dcz_ref)
-        dense["y"].start()
+        dense_next("z", dcz_ref, "y")
 
     def dense_out(late):
         return pltpu.make_async_copy(gd_ref, gdense_ref.at[late], keep_sem.at[0, 1])
@@ -538,23 +553,22 @@
         y_finish()
         inner_finish()
         dense_sum()
-        dense_sums.onward()
+        dense_to_x()
         cross_onward("x", "z")
-        dense_to_x()
+        pass_finish(1)
+        pl.semaphore_signal(credit.at[2], inc=1, device_id=place.at("c", 0), device_id_type=MESH)
         cross_onward("u", "l")
-        dense["x"].onward()
+        dense_to_z()
         cross_finish(0, "x", "z")
-        dense_to_z()
         cross_finish(0, "u", "l")
-        dense["z"].onward()
         dense_to_y()
+        dense_pass(0)
         final_onward(0, "x", "z")
-        dense["y"].onward()
+        dense_finish(0)
         final_onward(0, "u", "l")
-        dense_pass(0)
+        pl.semaphore_wait(credit.at[2], 1)
         final_finish(0, "x", "z")
         final_finish(0, "u", "l")
-        dense_finish(0)
         pass_finish(0)
 
     before, middle, after = {}, {}, {}
@@ -565,19 +579,19 @@
 
     on, done = lambda q: lambda: reduce_onward(q), lambda q: lambda: reduce_finish(q)
     now = lambda: load(s)
-    plan(before, 0, [g0.second, g0.lead], [g0.third, g0.follow, g0.lead_onward], [g1.begin, g0.follow_onward, g0.complete_y, now, g0.last])
-    plan(before, 3, [g0.passed_left, g1.second], [g0.last_onward, g1.lead], [g0.complete_last, now, g1.third, g0.passed_right], [g1.follow], [g0.passed_last, now, g1.lead_onward])
-    plan(before, SLOTS + 1, [g1.follow_onward], [g1.complete_y, now, g1.last], [g1.passed_left], [g1.last_onward], [g1.complete_last, now, g1.passed_right], [], [g1.passed_last, now])
-    unready = (1, 4, 6, SLOTS + 1, SLOTS + 4, SLOTS + 6)
+    plan(before, 1, [g0.lead], [g0.follow, g0.lead_onward, g1.begin, g0.follow_onward, g0.last, g0.complete_y, now], [g0.passed_left])
+    plan(before, 4, [g0.last_onward, g1.lead], [g0.complete_last, now, g0.passed_right, g1.follow], [], [g0.passed_last, now, g1.lead_onward])
+    plan(before, SLOTS + 1, [g1.follow_onward, g1.last], [g1.complete_y, now], [g1.passed_left], [g1.last_onward], [g1.complete_last, now, g1.passed_right], [g1.passed_last])
+    unready = (1, 4, 6, SLOTS + 1, SLOTS + 4)
     late = ("x", "z", "u", "l")
-    plan(before, WEIGHTS0, [lambda: copies.start("dense pair"), inner_onward], [], [inner_finish, dense_sums.onward], [lambda: cross_onward("x", "z"), dense_to_x], [lambda: cross_onward("u", "l")])
-    plan(middle, WEIGHTS0, [dense_sum, y_finish], [], [], [], [dense["x"].onward], [lambda: cross_finish(1, *late)], [dense_to_z])
-    plan(before, INPUTS0, [dense["z"].onward], [lambda: final_onward(1, *late)], [dense_to_y], [lambda: final_finish(1, *late)], [dense["y"].onward], [], [lambda: dense_pass(1)], [lambda: pass_finish(1)])
-    plan(before, INPUTS1 + 6, [w_finish])
+    plan(before, INPUTS1 + 5, [w_finish], [], [inner_onward])
+    plan(before, WEIGHTS0, [lambda: copies.start("dense pair")], [inner_finish], [], [lambda: cross_onward("x", "z"), dense_to_x], [lambda: cross_onward("u", "l")], [dense_to_z])
+    plan(middle, WEIGHTS0, [dense_sum, y_finish], [], [], [], [], [], [], [dense_to_y])
+    plan(before, INPUTS0, [lambda: cross_finish(1, *late)], [], [lambda: dense_pass(1)], [], [lambda: final_onward(1, *late)], [], [lambda: final_finish(1, *late)])
     plan(before, INPUTS0 + 5, [w_finish], [], [inner_onward])
     for base in (WEIGHTS1, WEIGHTS0):
-        plan(before, base + 3, [on_y["w"].start], [], [], [on_y["w"].onward])
-        plan(middle, base + 4, [on(0)], [], [done(0), y_start, on(1)], [on(2)])
+        plan(before, base + 3, [on_y["w"].start], [], [], [done(0), y_start, on_y["w"].onward])
+        plan(middle, base + 4, [on(0)], [], [on(1)], [on(2)])
         plan(before, base + SLOTS, [], [done(1)], [done(2), y_onward], [on(3)], [], [], [done(3)])
         for step, q in OWN_STEPS.items():
             plan(after, base + step, [lambda q=q: reduce_start(q)])
@@ -624,6 +638,7 @@
         hooks(before, 0, SLOTS)
         pl.when(s > 1)(lambda: wait(saves(s - 2)))
         ahead = functools.reduce(jnp.logical_and, [s != step for step in unready], (s > 0) & (s < WEIGHTS1 - 1))
+        pl.when((t == 1) | (t == 2))(lambda: wait(keeps(s - 1)))
         pl.when(ahead)(lambda: load(s + 1))
 
         @pl.when(t < 2)
@@ -632,22 +647,28 @@
             pl.when(s == SLOTS)(lambda: enter(x1_ref[...]))
 
         layer, slot = phase, t
-        z = dot(one_hot(rows_ref, layer, slot, cap), cur_ref[...]).astype(BF16)
-        z_ref[forth] = z
         come = list(weights(layer, slot, ARRAYS, forth))
-        wait(come[:2])
-        a = dot(z, w1_ref[forth]).astype(BF16)
-        b = dot(z, w3_ref[forth]).astype(BF16)
-        a_ref[forth] = a
-        b_ref[forth] = b
-        h = (jax.nn.silu(a.astype(F32)) * b.astype(F32)).astype(BF16)
-        wait(come[2:])
+
+        def forward_step(is_ready):
+            if is_ready:
+                wait(come)
+            z = dot(one_hot(rows_ref, layer, slot, cap), cur_ref[...]).astype(BF16)
+            z_ref[forth] = z
+            if not is_ready:
+                wait(come)
+            a = dot(z, w1_ref[forth]).astype(BF16)
+            b = dot(z, w3_ref[forth]).astype(BF16)
+            a_ref[forth] = a
+            b_ref[forth] = b
+            h = (jax.nn.silu(a.astype(F32)) * b.astype(F32)).astype(BF16)
+            o = dot(h, w2_ref[forth]).astype(BF16)
+            acc_ref[...] += column(columns_ref, layer, SLOTS + slot) * dot(one_hot_t(columns_ref, layer, slot, cap), o)
+
+        is_late = functools.reduce(jnp.logical_or, [s == step + 1 for step in unready])
+        pl.when(is_late)(lambda: forward_step(False))
+        pl.when(jnp.logical_not(is_late))(lambda: forward_step(True))
         pl.when(t < 2)(lambda: start(keeps(s)))
-        o = dot(h, w2_ref[forth]).astype(BF16)
-        acc_ref[...] += column(columns_ref, layer, SLOTS + slot) * dot(one_hot_t(columns_ref, layer, slot, cap), o)
         pl.when(s < WEIGHTS1 - 1)(lambda: start(saves(s)))
-        pl.when(t < 2)(lambda: wait(keeps(s)))
-
         @pl.when(t == SLOTS - 1)
         def _():
             pl.when(s == SLOTS - 1)(lambda: leave(x1_ref))
@@ -786,8 +807,8 @@
     scratch += [buf(2, part // 2, width), buf(2, part, width)] * 2
     scratch += [buf(SIDE, quarter, ff)] * 2 + [buf(SIDE, part, width)] * 2
     scratch += [buf(quarter, ff)] * 2 + [buf(part, width)] * 2
-    scratch += [buf(width, width)] + [buf(width // 2, width)] * 2 + [buf(2, piece, width)] * 2 + [buf(SIDE, piece, width)] * 2 + [buf(width // 2, width)] * 2
-    scratch += [dma(4), dma(2, 6), dma(2, 3), dma(2, 3), dma(GATHER_COPIES), dma(GATHER_COPIES), dma(REDUCE_COPIES), dma(REDUCE_COPIES), pltpu.SemaphoreType.REGULAR((2,))]
+    scratch += [buf(width, width)] + [buf(width // 2, width)] * 2 + [buf(SIDE - 1, piece, width)] + [buf(SIDE, piece, width)] * 2 + [buf(width // 2, width)] * 2
+    scratch += [dma(4), dma(2, 6), dma(2, 3), dma(2, 3), dma(GATHER_COPIES), dma(GATHER_COPIES), dma(REDUCE_COPIES), dma(REDUCE_COPIES), pltpu.SemaphoreType.REGULAR((3,))]
     results = [(tokens, width), (tokens, width), (layers, width, width)]
     kept = [(layers, local, *u) for u in ups] + [(layers, SLOTS, *u) for u in ups + acts] + [(SLOTS, cap, ff)] * 2
     return pl.pallas_call(

time: 276 us -> 269 us (0.975)
  Pallas kernels: 275 us -> 268 us
    pallas_call x1, Pallas kernels: 266 us -> 259 us  [step(): pl.pallas_call(functools.partial(kernel, cap), grid=(STEPS,), in_specs=[h...]
where the time goes in v8:
time: 269 us
  Pallas kernels  268 us (100%)
    pallas_call x1, Pallas kernels, step(): pl.pallas_call(functools.partial(kernel, cap), grid=(STEPS,), in_specs=[h...  259 us
    pallas_call x1, Pallas kernels, take(): pl.pallas_call(functools.partial(take_kernel, count), in_specs=[hbm] * co...  8.93 us

profile of v8, /device:TPU:1, one launch (start us, length us, event | category | flops | bytes accessed | tf_op | source)
XLA Modules:
  0.0 268.9 jit_solution(1668173417518693556)
XLA Ops:
  0.6 259.3 %step.1 = (bf16[1024,384]{1,0:T(8,128)(2,1)}, bf16[1024,384]{1,0:T(8,128)(2,1)}, bf16[2,384,384]{2,1,0:T(8,128)(2,1)}, bf16[2,2,384,1024]{3,2,1,0:T(8,128)(2,1)}...) custom-call(bf16[1024,384]{1,0:T(8,128)(2,1)} %x0_ref.1, ...), custom_call_target="tpu_custom_call" | custom-call | tf_op jit(solution)/shard_map/step/pallas_call | solution.py:814
  259.9 8.9 %take.1 = (bf16[1024,384]{1,0:T(8,128)(2,1)}, bf16[1024,384]{1,0:T(8,128)(2,1)}, bf16[2,384,384]{2,1,0:T(8,128)(2,1)}, bf16[2,2,384,1024]{3,2,1,0:T(8,128)(2,1)}...) custom-call(bf16[1024,384]{1,0:T(8,128)(2,1)} %get-tuple-element.12.refs_0_, ...), custom_call_target="tpu_custom_call" | custom-call | tf_op jit(solution)/shard_map/take/pallas_call | solution.py:842

commit v9 on v8

--- a/solution.py
+++ b/solution.py
@@ -23,6 +23,10 @@
 
 def dot(a, b):
     return jnp.dot(a, b, preferred_element_type=F32)
+
+
+def sigmoid(a):
+    return 0.5 + 0.5 * jnp.tanh(0.5 * a)
 
 
 def dot_nt(a, b):
@@ -327,7 +331,7 @@
 
 
 OWN_STEPS = {2: 0, 4: 1, 5: 2, 7: 3}
-REDUCE_COPIES = 107
+REDUCE_COPIES = 120
 WEIGHTS1, INPUTS1, WEIGHTS0, INPUTS0, STEPS = (n * SLOTS for n in range(2, 7))
 
 
@@ -345,7 +349,6 @@
     half_d = rows // 2
 
     stage, mate, mine_of = (m1_ref, m3_ref, m2_ref), (d1_ref, d3_ref, d2_ref), (s1_ref, s3_ref, s2_ref)
-    outs = (g1_ref, g3_ref, g2_ref)
     for buf in BUFS:
         for n in ARRAYS:
             copies.add(("pair", buf, n), stage[n].at[buf], mate[n].at[buf], "c", 0)
@@ -384,11 +387,12 @@
         for late in LAYERS:
             block = slices(ref, (late, place.c), base, size)
             final[k, late] = RingSpread(copies, ("final", k, late), *ring_of[k], block, source=done_ref[k], like=final.get((k, 1)))
-            puts[k, late] = pltpu.make_async_copy(done_ref[k], block(ring_of[k][1], None), put_sem.at[i])
+            me = ring_of[k][1]
+            puts[k, late] = pltpu.make_async_copy(done_ref[k], block(me, None), put_sem.at[i])
+            for offset in (0, *WAYS, 2):
+                quarter_at = block((me + offset) % SIDE if offset >= 0 else (me + SIDE - 1) % SIDE, None)
+                copies.add(("pass", k, offset, late), quarter_at if offset else done_ref[k], quarter_at, "c", 0, None if late else ("pass", k, offset, 1))
     mine, theirs = (pl.ds(pl.multiple_of(c * half_d, 16), half_d) for c in (place.c, 1 - place.c))
-    for late in LAYERS:
-        for n, out in enumerate(outs):
-            copies.add(("pass", n, late), out.at[late, place.c], out.at[late, place.c], "c", 0, None if late else ("pass", n, 1))
     copies.add("dense pair", dp_ref.at[theirs], dr_ref, "c", 0)
     copies.add("dense pass", dcy_ref, de_ref, "c", 0)
     piece = half_d // SIDE
@@ -447,19 +451,21 @@
             done_ref[k][...] = total(cross_ref[k])
             puts[k, late].start()
             final[k, late].start()
+            copies.start(("pass", k, 0, late))
 
     def final_onward(late, *keys):
         for k in keys:
             final[k, late].onward()
+            copies.start(*[("pass", k, way, late) for way in WAYS])
 
     def final_finish(late, *keys):
         for k in keys:
             final[k, late].finish()
             puts[k, late].wait()
-        copies.start(*[("pass", n, late) for n in ARRAYS if ("xzu"[n] in keys)])
+            copies.start(("pass", k, 2, late))
 
     def pass_finish(late):
-        keys = [("pass", n, late) for n in ARRAYS]
+        keys = [("pass", k, offset, late) for k in out_of for offset in (0, *WAYS, 2)]
         copies.arrive(*keys)
         copies.sent(*keys)
 
@@ -559,6 +565,7 @@
         pl.semaphore_signal(credit.at[2], inc=1, device_id=place.at("c", 0), device_id_type=MESH)
         cross_onward("u", "l")
         dense_to_z()
+        pl.semaphore_wait(credit.at[2], 1)
         cross_finish(0, "x", "z")
         cross_finish(0, "u", "l")
         dense_to_y()
@@ -566,7 +573,6 @@
         final_onward(0, "x", "z")
         dense_finish(0)
         final_onward(0, "u", "l")
-        pl.semaphore_wait(credit.at[2], 1)
         final_finish(0, "x", "z")
         final_finish(0, "u", "l")
         pass_finish(0)
@@ -584,10 +590,10 @@
     plan(before, SLOTS + 1, [g1.follow_onward, g1.last], [g1.complete_y, now], [g1.passed_left], [g1.last_onward], [g1.complete_last, now, g1.passed_right], [g1.passed_last])
     unready = (1, 4, 6, SLOTS + 1, SLOTS + 4)
     late = ("x", "z", "u", "l")
-    plan(before, INPUTS1 + 5, [w_finish], [], [inner_onward])
-    plan(before, WEIGHTS0, [lambda: copies.start("dense pair")], [inner_finish], [], [lambda: cross_onward("x", "z"), dense_to_x], [lambda: cross_onward("u", "l")], [dense_to_z])
+    plan(before, INPUTS1 + 6, [w_finish], [], [inner_onward])
+    plan(before, WEIGHTS0, [lambda: copies.start("dense pair")], [], [inner_finish], [lambda: cross_onward("x", "z"), dense_to_x], [lambda: cross_onward("u", "l")], [dense_to_z])
     plan(middle, WEIGHTS0, [dense_sum, y_finish], [], [], [], [], [], [], [dense_to_y])
-    plan(before, INPUTS0, [lambda: cross_finish(1, *late)], [], [lambda: dense_pass(1)], [], [lambda: final_onward(1, *late)], [], [lambda: final_finish(1, *late)])
+    plan(before, INPUTS0, [lambda: cross_finish(1, *late)], [], [], [], [lambda: final_onward(1, *late)], [], [lambda: final_finish(1, *late)], [lambda: dense_pass(1)])
     plan(before, INPUTS0 + 5, [w_finish], [], [inner_onward])
     for base in (WEIGHTS1, WEIGHTS0):
         plan(before, base + 3, [on_y["w"].start], [], [], [done(0), y_start, on_y["w"].onward])
@@ -660,7 +666,8 @@
             b = dot(z, w3_ref[forth]).astype(BF16)
             a_ref[forth] = a
             b_ref[forth] = b
-            h = (jax.nn.silu(a.astype(F32)) * b.astype(F32)).astype(BF16)
+            a = a.astype(F32)
+            h = (a * sigmoid(a) * b.astype(F32)).astype(BF16)
             o = dot(h, w2_ref[forth]).astype(BF16)
             acc_ref[...] += column(columns_ref, layer, SLOTS + slot) * dot(one_hot_t(columns_ref, layer, slot, cap), o)
 
@@ -700,7 +707,7 @@
         dh = dot_nt(do, w2_ref[back])
         a = a_ref[back].astype(F32)
         b = b_ref[back].astype(F32)
-        sig = jax.nn.sigmoid(a)
+        sig = sigmoid(a)
         act = a * sig
         h = (act * b).astype(BF16)
         db = (dh * act).astype(BF16)

time: 269 us -> 262 us (0.974)
  Pallas kernels: 268 us -> 262 us
    pallas_call x1, Pallas kernels: 259 us -> 253 us  [step(): pl.pallas_call(functools.partial(kernel, cap), grid=(STEPS,), in_specs=[h...]
where the time goes in v9:
time: 262 us
  Pallas kernels  262 us (100%)
    pallas_call x1, Pallas kernels, step(): pl.pallas_call(functools.partial(kernel, cap), grid=(STEPS,), in_specs=[h...  253 us
    pallas_call x1, Pallas kernels, take(): pl.pallas_call(functools.partial(take_kernel, count), in_specs=[hbm] * co...  8.93 us

profile of v9, /device:TPU:1, one launch (start us, length us, event | category | flops | bytes accessed | tf_op | source)
XLA Modules:
  0.0 262.2 jit_solution(7992525394164092427)
XLA Ops:
  0.6 252.6 %step.1 = (bf16[1024,384]{1,0:T(8,128)(2,1)}, bf16[1024,384]{1,0:T(8,128)(2,1)}, bf16[2,384,384]{2,1,0:T(8,128)(2,1)}, bf16[2,2,384,1024]{3,2,1,0:T(8,128)(2,1)}...) custom-call(bf16[1024,384]{1,0:T(8,128)(2,1)} %x0_ref.1, ...), custom_call_target="tpu_custom_call" | custom-call | tf_op jit(solution)/shard_map/step/pallas_call | solution.py:821
  253.2 8.9 %take.1 = (bf16[1024,384]{1,0:T(8,128)(2,1)}, bf16[1024,384]{1,0:T(8,128)(2,1)}, bf16[2,384,384]{2,1,0:T(8,128)(2,1)}, bf16[2,2,384,1024]{3,2,1,0:T(8,128)(2,1)}...) custom-call(bf16[1024,384]{1,0:T(8,128)(2,1)} %get-tuple-element.12.refs_0_, ...), custom_call_target="tpu_custom_call" | custom-call | tf_op jit(solution)/shard_map/take/pallas_call | solution.py:849

commit v10 on v9

--- a/solution.py
+++ b/solution.py
@@ -23,10 +23,6 @@
 
 def dot(a, b):
     return jnp.dot(a, b, preferred_element_type=F32)
-
-
-def sigmoid(a):
-    return 0.5 + 0.5 * jnp.tanh(0.5 * a)
 
 
 def dot_nt(a, b):
@@ -335,7 +331,7 @@
 WEIGHTS1, INPUTS1, WEIGHTS0, INPUTS0, STEPS = (n * SLOTS for n in range(2, 7))
 
 
-def kernel(cap, x0_ref, dy_ref, ids_ref, gate_ref, wd_ref, o1_ref, o3_ref, o2_ref, y_ref, dx_ref, gdense_ref, g1_ref, g3_ref, g2_ref, h1_ref, h3_ref, h2_ref, kz_ref, ka_ref, kb_ref, kda_ref, kdb_ref, acc_ref, cur_ref, x1_ref, hold_ref, gd_ref, rows_ref, columns_ref, w1_ref, w3_ref, w2_ref, z_ref, a_ref, b_ref, m1_ref, m3_ref, m2_ref, d1_ref, d3_ref, d2_ref, s1_ref, s3_ref, s2_ref, r11_ref, r12_ref, r31_ref, r32_ref, t1_ref, t3_ref, y11_ref, y12_ref, y31_ref, y32_ref, y21_ref, y22_ref, u1_ref, u2_ref, l1_ref, l2_ref, c1_ref, c3_ref, cu_ref, cl_ref, f1_ref, f3_ref, fu_ref, fl_ref, dp_ref, dr_ref, ds_ref, e_ref, dcx_ref, dcz_ref, dcy_ref, de_ref, put_sem, load_sem, keep_sem, save_sem, gsend_sem, grecv_sem, send_sem, recv_sem, credit):
+def kernel(cap, x0_ref, dy_ref, ids_ref, gate_ref, wd_ref, o1_ref, o3_ref, o2_ref, y_ref, dx_ref, gdense_ref, g1_ref, g3_ref, g2_ref, h1_ref, h3_ref, h2_ref, kz_ref, ka_ref, kb_ref, kda_ref, kdb_ref, acc_ref, cur_ref, x1_ref, hold_ref, gd_ref, rows_ref, columns_ref, w1_ref, w3_ref, w2_ref, z_ref, a_ref, b_ref, d1_ref, d3_ref, d2_ref, s1_ref, s3_ref, s2_ref, r11_ref, r12_ref, r31_ref, r32_ref, t1_ref, t3_ref, y11_ref, y12_ref, y31_ref, y32_ref, y21_ref, y22_ref, u1_ref, u2_ref, l1_ref, l2_ref, c1_ref, c3_ref, cu_ref, cl_ref, f1_ref, f3_ref, fu_ref, fl_ref, dp_ref, dr_ref, ds_ref, e_ref, dcx_ref, dcz_ref, dcy_ref, de_ref, put_sem, load_sem, keep_sem, save_sem, gsend_sem, grecv_sem, send_sem, recv_sem, credit):
     s = pl.program_id(0)
     place = Place()
     gathers = Copies(place, gsend_sem, grecv_sem)
@@ -348,10 +344,10 @@
     quarter, part = rows // SIDE, ff // 2 // SIDE
     half_d = rows // 2
 
-    stage, mate, mine_of = (m1_ref, m3_ref, m2_ref), (d1_ref, d3_ref, d2_ref), (s1_ref, s3_ref, s2_ref)
+    mate, mine_of = (d1_ref, d3_ref, d2_ref), (s1_ref, s3_ref, s2_ref)
     for buf in BUFS:
         for n in ARRAYS:
-            copies.add(("pair", buf, n), stage[n].at[buf], mate[n].at[buf], "c", 0)
+            copies.add(("pair", buf, n), mine_of[n].at[SIDE + buf], mate[n].at[buf], "c", 0)
 
     def ring_blocks(ref, q, me, base, size):
         block = slices(ref, (q,), base, size)
@@ -593,7 +589,7 @@
     plan(before, INPUTS1 + 6, [w_finish], [], [inner_onward])
     plan(before, WEIGHTS0, [lambda: copies.start("dense pair")], [], [inner_finish], [lambda: cross_onward("x", "z"), dense_to_x], [lambda: cross_onward("u", "l")], [dense_to_z])
     plan(middle, WEIGHTS0, [dense_sum, y_finish], [], [], [], [], [], [], [dense_to_y])
-    plan(before, INPUTS0, [lambda: cross_finish(1, *late)], [], [], [], [lambda: final_onward(1, *late)], [], [lambda: final_finish(1, *late)], [lambda: dense_pass(1)])
+    plan(before, INPUTS0, [lambda: cross_finish(1, *late)], [], [], [], [], [lambda: final_onward(1, *late)], [], [lambda: dense_pass(1), lambda: final_finish(1, *late)])
     plan(before, INPUTS0 + 5, [w_finish], [], [inner_onward])
     for base in (WEIGHTS1, WEIGHTS0):
         plan(before, base + 3, [on_y["w"].start], [], [], [done(0), y_start, on_y["w"].onward])
@@ -667,7 +663,7 @@
             a_ref[forth] = a
             b_ref[forth] = b
             a = a.astype(F32)
-            h = (a * sigmoid(a) * b.astype(F32)).astype(BF16)
+            h = (a * jax.nn.sigmoid(a) * b.astype(F32)).astype(BF16)
             o = dot(h, w2_ref[forth]).astype(BF16)
             acc_ref[...] += column(columns_ref, layer, SLOTS + slot) * dot(one_hot_t(columns_ref, layer, slot, cap), o)
 
@@ -702,55 +698,53 @@
         pl.when(t < SLOTS - 1)(lambda: start(weights_loads(s + 1)))
         pl.when(t == SLOTS - 1)(lambda: start(inputs_loads(s + 1)))
 
-        grad_gated = (column(columns_ref, layer, SLOTS + slot) * cur_ref[...].astype(F32)).astype(BF16)
-        do = dot(one_hot(rows_ref, layer, slot, cap), grad_gated).astype(BF16)
-        dh = dot_nt(do, w2_ref[back])
-        a = a_ref[back].astype(F32)
-        b = b_ref[back].astype(F32)
-        sig = sigmoid(a)
-        act = a * sig
-        h = (act * b).astype(BF16)
-        db = (dh * act).astype(BF16)
-        da = (dh * b * (sig + act * (1.0 - sig))).astype(BF16)
-        a_ref[2] = da
-        b_ref[2] = db
-        z = z_ref[back]
-        start(defers(s))
-        hooks(middle, WEIGHTS1, WEIGHTS0)
-
-        def weight_grads():
-            return dot_tn(z, da), dot_tn(z, db), dot_tn(h, do)
-
         is_own = functools.reduce(jnp.logical_or, [t == step for step in OWN_STEPS])
         group = t // 4 + t // 5 + t // 7
         into = (t + t // 3 + t // 6) % 2
         turn = t + (1 - layer) * SLOTS
+        for buf in BUFS:
+            pl.when(is_own & (group % 2 == buf))(lambda: copies.arrive(*[("pair", buf, n) for n in ARRAYS]))
+            pl.when(jnp.logical_not(is_own) & (turn >= 3) & (into == buf))(lambda: copies.sent(*[("pair", buf, n) for n in ARRAYS]))
+
+        def back_step(adds):
+            grad_gated = (column(columns_ref, layer, SLOTS + slot) * cur_ref[...].astype(F32)).astype(BF16)
+            do = dot(one_hot(rows_ref, layer, slot, cap), grad_gated).astype(BF16)
+            dh = dot_nt(do, w2_ref[back])
+            a = a_ref[back].astype(F32)
+            b = b_ref[back].astype(F32)
+            sig = jax.nn.sigmoid(a)
+            act = a * sig
+            h = (act * b).astype(BF16)
+            db = (dh * act).astype(BF16)
+            da = (dh * b * (sig + act * (1.0 - sig))).astype(BF16)
+            a_ref[2] = da
+            b_ref[2] = db
+            z = z_ref[back]
+            for ref, add, grad in zip(mine_of, mate, (dot_tn(z, da), dot_tn(z, db), dot_tn(h, do))):
+                if adds:
+                    ref[group] = (grad + add[group % 2].astype(F32)).astype(BF16)
+                else:
+                    ref[SIDE + into] = grad.astype(BF16)
+
+        pl.when(is_own)(lambda: back_step(True))
+        pl.when(jnp.logical_not(is_own))(lambda: back_step(False))
+        start(defers(s))
 
         @pl.when(jnp.logical_not(is_own))
         def _():
-            for buf in BUFS:
-                pl.when((turn >= 3) & (into == buf))(lambda: copies.sent(*[("pair", buf, n) for n in ARRAYS]))
-
-            for ref, grad in zip(stage, weight_grads()):
-                ref[into] = grad.astype(BF16)
-
             pl.when(turn >= 3)(lambda: pl.semaphore_wait(credit.at[into], 1))
             for buf in BUFS:
                 pl.when(into == buf)(lambda: copies.start(*[("pair", buf, n) for n in ARRAYS]))
 
         @pl.when(is_own)
         def _():
-            for buf in BUFS:
-                pl.when(group % 2 == buf)(lambda: copies.arrive(*[("pair", buf, n) for n in ARRAYS]))
-
-            for ref, add, grad in zip(mine_of, mate, weight_grads()):
-                ref[group] = (grad + add[group % 2].astype(F32)).astype(BF16)
-
             @pl.when(turn < 2 * SLOTS - 3)
             def _():
                 pl.semaphore_signal(credit.at[group % 2], inc=1, device_id=place.at("c", 0), device_id_type=MESH)
 
             hooks(after, WEIGHTS1, WEIGHTS0)
+
+        hooks(middle, WEIGHTS1, WEIGHTS0)
 
     def leave_back(layer, x, out_ref):
         grad = acc_ref[...]
@@ -807,7 +801,7 @@
     acts = [(cap, width), (cap, ff), (cap, ff)]
     scratch = [pltpu.VMEM((tokens, width), F32)] + [buf(tokens, width)] * 3 + [buf(width, width), pltpu.VMEM((layers, SLOTS, tokens), jnp.int32), pltpu.VMEM((layers, tokens, LANES), F32)]
     scratch += [buf(2, *u) for u in ups] + [buf(n, *a) for n, a in zip((2, 3, 3), acts)]
-    scratch += [buf(2, *u) for u in ups] * 2 + [buf(SIDE, *u) for u in ups]
+    scratch += [buf(2, *u) for u in ups] + [buf(SIDE + 2, *u) for u in ups]
     scratch += [buf(SIDE, 2, quarter // 2, ff), buf(SIDE, 2, quarter, ff)] * 2
     scratch += [buf(SIDE, quarter, ff)] * 2
     scratch += [buf(2, quarter // 2, ff), buf(2, quarter, ff)] * 2 + [buf(2, ff // 2, width), buf(2, ff, width)]

time: 262 us -> 280 us (1.069)
  Pallas kernels: 262 us -> 279 us
    pallas_call x1, Pallas kernels: 253 us -> 270 us  [step(): pl.pallas_call(functools.partial(kernel, cap), grid=(STEPS,), in_specs=[h...]
where the time goes in v10:
time: 280 us
  Pallas kernels  279 us (100%)
    pallas_call x1, Pallas kernels, step(): pl.pallas_call(functools.partial(kernel, cap), grid=(STEPS,), in_specs=[h...  270 us
    pallas_call x1, Pallas kernels, take(): pl.pallas_call(functools.partial(take_kernel, count), in_specs=[hbm] * co...  8.93 us

profile of v10, /device:TPU:1, one launch (start us, length us, event | category | flops | bytes accessed | tf_op | source)
XLA Modules:
  0.0 280.0 jit_solution(11760340488229809389)
XLA Ops:
  0.6 270.4 %step.1 = (bf16[1024,384]{1,0:T(8,128)(2,1)}, bf16[1024,384]{1,0:T(8,128)(2,1)}, bf16[2,384,384]{2,1,0:T(8,128)(2,1)}, bf16[2,2,384,1024]{3,2,1,0:T(8,128)(2,1)}...) custom-call(bf16[1024,384]{1,0:T(8,128)(2,1)} %x0_ref.1, ...), custom_call_target="tpu_custom_call" | custom-call | tf_op jit(solution)/shard_map/step/pallas_call | solution.py:815
  271.0 8.9 %take.1 = (bf16[1024,384]{1,0:T(8,128)(2,1)}, bf16[1024,384]{1,0:T(8,128)(2,1)}, bf16[2,384,384]{2,1,0:T(8,128)(2,1)}, bf16[2,2,384,1024]{3,2,1,0:T(8,128)(2,1)}...) custom-call(bf16[1024,384]{1,0:T(8,128)(2,1)} %get-tuple-element.12.refs_0_, ...), custom_call_target="tpu_custom_call" | custom-call | tf_op jit(solution)/shard_map/take/pallas_call | solution.py:843

commit v11 on v9

--- a/solution.py
+++ b/solution.py
@@ -23,10 +23,6 @@
 
 def dot(a, b):
     return jnp.dot(a, b, preferred_element_type=F32)
-
-
-def sigmoid(a):
-    return 0.5 + 0.5 * jnp.tanh(0.5 * a)
 
 
 def dot_nt(a, b):
@@ -593,7 +589,7 @@
     plan(before, INPUTS1 + 6, [w_finish], [], [inner_onward])
     plan(before, WEIGHTS0, [lambda: copies.start("dense pair")], [], [inner_finish], [lambda: cross_onward("x", "z"), dense_to_x], [lambda: cross_onward("u", "l")], [dense_to_z])
     plan(middle, WEIGHTS0, [dense_sum, y_finish], [], [], [], [], [], [], [dense_to_y])
-    plan(before, INPUTS0, [lambda: cross_finish(1, *late)], [], [], [], [lambda: final_onward(1, *late)], [], [lambda: final_finish(1, *late)], [lambda: dense_pass(1)])
+    plan(before, INPUTS0, [lambda: cross_finish(1, *late)], [], [], [], [], [lambda: final_onward(1, *late)], [], [lambda: dense_pass(1), lambda: final_finish(1, *late)])
     plan(before, INPUTS0 + 5, [w_finish], [], [inner_onward])
     for base in (WEIGHTS1, WEIGHTS0):
         plan(before, base + 3, [on_y["w"].start], [], [], [done(0), y_start, on_y["w"].onward])
@@ -667,7 +663,7 @@
             a_ref[forth] = a
             b_ref[forth] = b
             a = a.astype(F32)
-            h = (a * sigmoid(a) * b.astype(F32)).astype(BF16)
+            h = (a * jax.nn.sigmoid(a) * b.astype(F32)).astype(BF16)
             o = dot(h, w2_ref[forth]).astype(BF16)
             acc_ref[...] += column(columns_ref, layer, SLOTS + slot) * dot(one_hot_t(columns_ref, layer, slot, cap), o)
 
@@ -707,7 +703,7 @@
         dh = dot_nt(do, w2_ref[back])
         a = a_ref[back].astype(F32)
         b = b_ref[back].astype(F32)
-        sig = sigmoid(a)
+        sig = jax.nn.sigmoid(a)
         act = a * sig
         h = (act * b).astype(BF16)
         db = (dh * act).astype(BF16)

time: 262 us -> 259 us (0.989)
  Pallas kernels: 262 us -> 258 us
    pallas_call x1, Pallas kernels: 253 us -> 249 us  [step(): pl.pallas_call(functools.partial(kernel, cap), grid=(STEPS,), in_specs=[h...]
where the time goes in v11:
time: 259 us
  Pallas kernels  258 us (100%)
    pallas_call x1, Pallas kernels, step(): pl.pallas_call(functools.partial(kernel, cap), grid=(STEPS,), in_specs=[h...  249 us
    pallas_call x1, Pallas kernels, take(): pl.pallas_call(functools.partial(take_kernel, count), in_specs=[hbm] * co...  8.93 us

profile of v11, /device:TPU:1, one launch (start us, length us, event | category | flops | bytes accessed | tf_op | source)
XLA Modules:
  0.0 258.8 jit_solution(13794014440232399223)
XLA Ops:
  0.6 249.3 %step.1 = (bf16[1024,384]{1,0:T(8,128)(2,1)}, bf16[1024,384]{1,0:T(8,128)(2,1)}, bf16[2,384,384]{2,1,0:T(8,128)(2,1)}, bf16[2,2,384,1024]{3,2,1,0:T(8,128)(2,1)}...) custom-call(bf16[1024,384]{1,0:T(8,128)(2,1)} %x0_ref.1, ...), custom_call_target="tpu_custom_call" | custom-call | tf_op jit(solution)/shard_map/step/pallas_call | solution.py:817
  249.9 8.9 %take.1 = (bf16[1024,384]{1,0:T(8,128)(2,1)}, bf16[1024,384]{1,0:T(8,128)(2,1)}, bf16[2,384,384]{2,1,0:T(8,128)(2,1)}, bf16[2,2,384,1024]{3,2,1,0:T(8,128)(2,1)}...) custom-call(bf16[1024,384]{1,0:T(8,128)(2,1)} %get-tuple-element.12.refs_0_, ...), custom_call_target="tpu_custom_call" | custom-call | tf_op jit(solution)/shard_map/take/pallas_call | solution.py:845

commit v12 on v11

--- a/solution.py
+++ b/solution.py
@@ -53,7 +53,7 @@
 
 class Copies:
     def __init__(self, place, send, recv):
-        self.place, self.send, self.recv, self.made, self.number, self.count, self.over = place, send, recv, {}, {}, 0, set()
+        self.place, self.send, self.recv, self.made, self.number, self.count = place, send, recv, {}, {}, 0
 
     def add(self, key, src, dst, axis, step, like=None):
         if like is None:
@@ -74,10 +74,6 @@
     def sent(self, *keys):
         for key in keys:
             self.made[key].wait_send()
-            self.over.add(key)
-
-    def drain(self):
-        self.sent(*[key for key in self.made if key not in self.over])
 
 
 def greet(place):
@@ -89,29 +85,30 @@
 
 
 class Gather:
-    PASS = {2: 4, 3: 6, 5: 7}
+    SECOND = {int(slot): int(second) for slot, second in ("20", "30", "41", "51", "60", "71")}
+    AHEAD = {"x": {2: 6, 4: 7}, "z": {3: 6, 5: 7}}
 
     def __init__(self, layer, copies, place, own, whole):
         self.layer, self.copies, self.place, self.own, self.whole = layer, copies, place, own, whole
         rows, ff = own[0].shape[2], own[2].shape[2]
-        self.cut = {"x": ((0, 0, rows // SIDE), (2, 0, ff // 2 // SIDE)), "z": ((1, 0, rows // SIDE), (2, ff // 2, ff // 2 // SIDE))}
+        half = ff // 2
+        self.cut = {"x": ((0, 0, rows // SIDE), (2, 0, half // SIDE)), "z": ((1, 0, rows // SIDE), (2, half, half // SIDE))}
         mine = {"x": place.x, "z": place.z}
-        for color in ("x", "z"):
+        for color in mine:
+            back = {after: before for before, after in self.AHEAD[color].items()}
             for part in BUFS:
-                self._add(("y", 2, color, part), color, part, None, 2, mine[color], None, "y", 1)
-                self._add(("y", 3, color, part), color, part, None, 3, mine[color], None, "y", -1)
-                if color == "x":
-                    self._add(("y", 5, color, part), color, part, 2, 5, mine[color], None, "y", 1)
-                else:
-                    self._add(("y", 5, color, part), color, part, 3, 5, mine[color], None, "y", -1)
-                for slot in (2, 3, 5):
+                for slot, second in self.SECOND.items():
+                    way = WAYS[back.get(slot, slot) % 2]
+                    self._add(("y", slot, part), color, part, back.get(slot), second, slot, mine[color], None, "y", way)
                     for step in WAYS:
-                        self._add(("near", slot, color, part, step), color, part, slot, slot, mine[color], None, color, step)
                         behind = (mine[color] - step + SIDE) % SIDE
-                        self._add(("far", slot, color, part, step), color, part, slot, slot, behind, (1 - step) // 2, color, step)
-        for slot, to in self.PASS.items():
-            for array in ARRAYS:
-                copies.add((layer, "pass", slot, array), whole[array].at[layer, slot], whole[array].at[layer, to], "c", 0)
+                        self._add(("near", slot, part, step), color, part, slot, None, slot, mine[color], None, color, step)
+                        self._add(("far", slot, part, step), color, part, slot, None, slot, behind, (1 - step) // 2, color, step)
+            up = whole[self.cut[color][0][0]]
+            down = pl.ds(self.cut[color][1][1], half)
+            for slot in self.SECOND:
+                for n, view in enumerate((up.at[layer, slot], whole[2].at[layer, slot, down])):
+                    self._put(("pass", slot, n), color, view, view, "c", 0)
 
     def _view(self, refs, index, color, part, quarter, half):
         array, base, size = self.cut[color][part]
@@ -121,81 +118,74 @@
             start = start + half * size
         return refs[array].at[self.layer, index, pl.ds(pl.multiple_of(start, 16), size)]
 
-    def _add(self, key, color, part, src_slot, dst_slot, quarter, half, axis, step):
-        src = self._view(self.own, self.place.c, color, part, quarter, half) if src_slot is None else self._view(self.whole, src_slot, color, part, quarter, half)
-        self.copies.add((self.layer,) + key, src, self._view(self.whole, dst_slot, color, part, quarter, half), axis, step)
-
-    def _keys(self, *key, extra=()):
-        return [(self.layer,) + key + (part,) + extra for part in BUFS]
-
-    def lead(self):
-        self.spread(2, "x")
-        self.spread(3, "z")
-
-    def lead_onward(self):
-        self.onward(2, "x")
-        self.onward(3, "z")
-
-    def follow(self):
-        self.spread(2, "z")
-        self.spread(3, "x")
-
-    def follow_onward(self):
-        self.onward(2, "z")
-        self.onward(3, "x")
-
-    def last(self):
-        self.spread(5, "x")
-        self.spread(5, "z")
-
-    def last_onward(self):
-        self.onward(5, "x")
-        self.onward(5, "z")
-
-    def complete_y(self):
-        self.complete(2)
-        self.complete(3)
-
-    def complete_last(self):
-        self.complete(5)
-
-    def passed_left(self):
-        self.passed(2)
-
-    def passed_right(self):
-        self.passed(3)
-
-    def passed_last(self):
-        self.passed(5)
+    def _add(self, key, color, part, src_slot, second, dst_slot, quarter, half, axis, step):
+        src = self._view(self.own, second, color, part, quarter, half) if src_slot is None else self._view(self.whole, src_slot, color, part, quarter, half)
+        self._put(key, color, src, self._view(self.whole, dst_slot, color, part, quarter, half), axis, step)
+
+    def _put(self, key, color, src, dst, axis, step):
+        self.copies.add((self.layer, color) + key, src, dst, axis, step, None if color == "x" else (self.layer, "x") + key)
+
+    def _stage(self, act):
+        for core, color in enumerate("xz"):
+            pl.when(self.place.c == core)(lambda: act(color))
+
+    def _start(self, color, *key):
+        self.copies.start((self.layer, color) + key)
+
+    def _arrive(self, color, *key):
+        self.copies.arrive((self.layer, color) + key)
 
     def begin(self):
-        for slot, color in ((2, "x"), (3, "z"), (2, "z"), (3, "x")):
-            self.copies.start(*self._keys("y", slot, color))
-
-    def spread(self, slot, color):
-        for part in BUFS:
-            self.copies.arrive((self.layer, "y", slot, color, part))
-            self.copies.start(*[(self.layer, "near", slot, color, part, step) for step in WAYS])
-        if (slot, color) in ((2, "x"), (3, "z")):
-            self.copies.start(*self._keys("y", 5, color))
-
-    def onward(self, slot, color):
-        for part in BUFS:
-            for step in WAYS:
-                self.copies.arrive((self.layer, "near", slot, color, part, step))
-                self.copies.start((self.layer, "far", slot, color, part, step))
+        def act(color):
+            for slot in (2, 3, 4, 5):
+                for part in BUFS:
+                    self._start(color, "y", slot, part)
+
+        self._stage(act)
+
+    def spread(self, slot):
+        def act(color):
+            for part in BUFS:
+                self._arrive(color, "y", slot, part)
+                for step in WAYS:
+                    self._start(color, "near", slot, part, step)
+            if slot in self.AHEAD[color]:
+                for part in BUFS:
+                    self._start(color, "y", self.AHEAD[color][slot], part)
+
+        return lambda: self._stage(act)
+
+    def onward(self, slot):
+        def act(color):
+            for part in BUFS:
+                for step in WAYS:
+                    self._arrive(color, "near", slot, part, step)
+                    self._start(color, "far", slot, part, step)
+
+        return lambda: self._stage(act)
 
     def complete(self, slot):
-        for color in ("x", "z"):
-            for step in WAYS:
-                self.copies.arrive(*self._keys("far", slot, color, extra=(step,)))
-        self.copies.start(*[(self.layer, "pass", slot, array) for array in ARRAYS])
+        def act(color):
+            for part in BUFS:
+                for step in WAYS:
+                    self._arrive(color, "far", slot, part, step)
+            for n in BUFS:
+                self._start(color, "pass", slot, n)
+
+        return lambda: self._stage(act)
 
     def passed(self, slot):
-        self.copies.arrive(*[(self.layer, "pass", slot, array) for array in ARRAYS])
-
-
-GATHER_COPIES = 2 * (2 * 2 * (3 + 3 * 4) + 9)
+        def act(color):
+            for n in BUFS:
+                self._arrive("zx"["xz".index(color)], "pass", slot, n)
+
+        return lambda: self._stage(act)
+
+    def drain(self):
+        self._stage(lambda color: self.copies.sent(*[key for key in self.copies.made if key[:2] == (self.layer, color)]))
+
+
+GATHER_COPIES = 144
 
 
 def route(ids_ref, gate_ref, rows_ref, columns_ref, place):
@@ -206,8 +196,8 @@
     for layer in range(layers):
         ids, gates = ids_ref[layer], gate_ref[layer]
         off = ((ids >> 1) - place.y) & (SIDE - 1)
-        odd = (ids + place.c) & 1
-        slot = jnp.where(off == 0, odd, jnp.where(off == SIDE - 1, 2 + 2 * odd, jnp.where(off == 1, 3 + 3 * odd, 5 + 2 * odd)))
+        odd = ids & 1
+        slot = jnp.where(off == 0, odd, jnp.where(off == SIDE - 1, 2 + 2 * odd, jnp.where(off == 1, 3 + 2 * odd, 6 + odd)))
         hits = [slot[n : n + 1] == lead for n in BUFS]
         hit = hits[0] | hits[1]
         weight = jnp.where(hits[0], gates[0:1], 0.0) + jnp.where(hits[1], gates[1:2], 0.0)
@@ -327,6 +317,7 @@
 
 
 OWN_STEPS = {2: 0, 4: 1, 5: 2, 7: 3}
+BACK_SLOTS = [int(slot) for slot in "75643210" + "63725401"]
 REDUCE_COPIES = 120
 WEIGHTS1, INPUTS1, WEIGHTS0, INPUTS0, STEPS = (n * SLOTS for n in range(2, 7))
 
@@ -509,20 +500,24 @@
 
     def weights(layer, slot, arrays, buf, is_given=False):
         for n in arrays:
-            src = given[n].at[layer, (place.c + slot) % 2] if is_given else whole[n].at[layer, slot]
+            src = given[n].at[layer, slot] if is_given else whole[n].at[layer, slot]
             yield copy(src, bufs[n].at[buf], load_sem.at[buf, n])
 
     def saved(layer, slot, buf):
         for n, (src, dst) in enumerate(zip(kept, acts)):
             yield copy(src.at[layer, slot], dst.at[buf], load_sem.at[buf, 3 + n])
 
+    def back_slot(step):
+        at, size = place.c * SLOTS + step % SLOTS, len(BACK_SLOTS)
+        return BACK_SLOTS[0] + sum((BACK_SLOTS[n] - BACK_SLOTS[n - 1]) * ((at + size - n) // size) for n in range(1, size))
+
     def weights_loads(step):
-        layer, slot, buf = layer_of(step), SLOTS - 1 - step % SLOTS, (step + 1) % 2
+        layer, slot, buf = layer_of(step), back_slot(step), (step + 1) % 2
         return [*weights(layer, slot, [2], buf), *saved(layer, slot, buf)]
 
     def inputs_loads(step):
-        layer, slot, buf = layer_of(step), SLOTS - 1 - step % SLOTS, (step + 1) % 2
-        return [*weights(layer, slot, BUFS, buf)] + [copy(deferred[n].at[slot], acts[n + 1].at[buf], load_sem.at[buf, 4 + n]) for n in BUFS]
+        layer, slot, buf = layer_of(step), back_slot(step), (step + 1) % 2
+        return [*weights(layer, slot, BUFS, buf)] + [copy(deferred[n].at[step % SLOTS], acts[n + 1].at[buf], load_sem.at[buf, 4 + n]) for n in BUFS]
 
     def load(step):
         slot = step % SLOTS
@@ -539,7 +534,7 @@
         return [copy(src.at[step % 2], dst.at[step // SLOTS, step % SLOTS], save_sem.at[step % 2, n]) for n, (src, dst) in enumerate(zip(acts, kept))]
 
     def defers(step):
-        return [copy(acts[n + 1].at[2], deferred[n].at[SLOTS - 1 - step % SLOTS], save_sem.at[0, n]) for n in BUFS]
+        return [copy(acts[n + 1].at[2], deferred[n].at[step % SLOTS], save_sem.at[0, n]) for n in BUFS]
 
     def wait(items):
         for item in items:
@@ -581,10 +576,12 @@
 
     on, done = lambda q: lambda: reduce_onward(q), lambda q: lambda: reduce_finish(q)
     now = lambda: load(s)
-    plan(before, 1, [g0.lead], [g0.follow, g0.lead_onward, g1.begin, g0.follow_onward, g0.last, g0.complete_y, now], [g0.passed_left])
-    plan(before, 4, [g0.last_onward, g1.lead], [g0.complete_last, now, g0.passed_right, g1.follow], [], [g0.passed_last, now, g1.lead_onward])
-    plan(before, SLOTS + 1, [g1.follow_onward, g1.last], [g1.complete_y, now], [g1.passed_left], [g1.last_onward], [g1.complete_last, now, g1.passed_right], [g1.passed_last])
-    unready = (1, 4, 6, SLOTS + 1, SLOTS + 4)
+    plan(before, 2, [*(g0.spread(n) for n in (2, 3)), g0.onward(2), g0.spread(4), g0.onward(3), g0.spread(5), g0.complete(2), g0.onward(4), g0.passed(2), now])
+    plan(before, 3, [g1.begin, g0.spread(6), g0.complete(3), g0.onward(5), g0.spread(7), g0.passed(3), now], [g0.complete(4), g0.onward(6), g0.passed(4), now])
+    plan(before, 5, [g0.complete(5), g0.onward(7), g0.passed(5), now], [g0.complete(6), g1.spread(2), g1.spread(3), g0.passed(6), now], [g0.complete(7), g0.passed(7), now])
+    plan(before, SLOTS, [g1.onward(2), g1.spread(4)], [g1.onward(3), g1.spread(5), g1.complete(2)], [g1.onward(4), g1.spread(6), g1.passed(2), now])
+    plan(before, SLOTS + 3, [g1.complete(3), g1.onward(5), g1.spread(7), g1.passed(3), now], [g1.complete(4), g1.passed(4), now], [g1.complete(5), g1.onward(6), g1.passed(5), now])
+    plan(before, SLOTS + 6, [g1.complete(6), g1.onward(7), g1.passed(6), now], [g1.complete(7), g1.passed(7), now])
     late = ("x", "z", "u", "l")
     plan(before, INPUTS1 + 6, [w_finish], [], [inner_onward])
     plan(before, WEIGHTS0, [lambda: copies.start("dense pair")], [], [inner_finish], [lambda: cross_onward("x", "z"), dense_to_x], [lambda: cross_onward("u", "l")], [dense_to_z])
@@ -639,9 +636,8 @@
     def _():
         hooks(before, 0, SLOTS)
         pl.when(s > 1)(lambda: wait(saves(s - 2)))
-        ahead = functools.reduce(jnp.logical_and, [s != step for step in unready], (s > 0) & (s < WEIGHTS1 - 1))
         pl.when((t == 1) | (t == 2))(lambda: wait(keeps(s - 1)))
-        pl.when(ahead)(lambda: load(s + 1))
+        pl.when((s == SLOTS - 1) | (s == SLOTS))(lambda: load(s + 1))
 
         @pl.when(t < 2)
         def _():
@@ -667,11 +663,11 @@
             o = dot(h, w2_ref[forth]).astype(BF16)
             acc_ref[...] += column(columns_ref, layer, SLOTS + slot) * dot(one_hot_t(columns_ref, layer, slot, cap), o)
 
-        is_late = functools.reduce(jnp.logical_or, [s == step + 1 for step in unready])
+        is_late = t > 1
         pl.when(is_late)(lambda: forward_step(False))
         pl.when(jnp.logical_not(is_late))(lambda: forward_step(True))
         pl.when(t < 2)(lambda: start(keeps(s)))
-        pl.when(s < WEIGHTS1 - 1)(lambda: start(saves(s)))
+        start(saves(s))
         @pl.when(t == SLOTS - 1)
         def _():
             pl.when(s == SLOTS - 1)(lambda: leave(x1_ref))
@@ -679,7 +675,7 @@
 
     @pl.when((phase == WEIGHTS1 // SLOTS) | (phase == WEIGHTS0 // SLOTS))
     def _():
-        layer, slot = layer_of(s), SLOTS - 1 - t
+        layer, slot = layer_of(s), back_slot(s)
         hooks(before, WEIGHTS1, WEIGHTS0)
 
         @pl.when(s == WEIGHTS1)
@@ -688,12 +684,15 @@
             moved.start()
             bring(dy_ref, cur_ref).start()
             wait(saves(s - 2))
-            gathers.drain()
+            wait(saves(s - 1))
+            start(weights_loads(s))
+            g0.drain()
+            g1.drain()
             bring(dy_ref, cur_ref).wait()
             moved.wait()
             acc_ref[...] = cur_ref[...].astype(F32)
 
-        pl.when(s > WEIGHTS1)(lambda: wait(weights_loads(s)))
+        wait(weights_loads(s))
         pl.when(t > 0)(lambda: wait(defers(s - 1)))
         pl.when(t < SLOTS - 1)(lambda: start(weights_loads(s + 1)))
         pl.when(t == SLOTS - 1)(lambda: start(inputs_loads(s + 1)))
@@ -756,7 +755,7 @@
 
     @pl.when((phase == INPUTS1 // SLOTS) | (phase == INPUTS0 // SLOTS))
     def _():
-        layer, slot = layer_of(s), SLOTS - 1 - t
+        layer, slot = layer_of(s), back_slot(s)
         hooks(before, INPUTS1, INPUTS0)
         wait(inputs_loads(s))
         pl.when(t == 0)(lambda: wait(defers(s - 1)))

time: 259 us -> 282 us (1.089)
  Pallas kernels: 258 us -> 281 us
    pallas_call x1, Pallas kernels: 249 us -> 272 us  [step(): pl.pallas_call(functools.partial(kernel, cap), grid=(STEPS,), in_specs=[h...]
where the time goes in v12:
time: 282 us
  Pallas kernels  281 us (100%)
    pallas_call x1, Pallas kernels, step(): pl.pallas_call(functools.partial(kernel, cap), grid=(STEPS,), in_specs=[h...  272 us
    pallas_call x1, Pallas kernels, take(): pl.pallas_call(functools.partial(take_kernel, count), in_specs=[hbm] * co...  8.93 us

profile of v12, /device:TPU:1, one launch (start us, length us, event | category | flops | bytes accessed | tf_op | source)
XLA Modules:
  0.0 281.6 jit_solution(10264463711306430296)
XLA Ops:
  0.6 272.0 %step.1 = (bf16[1024,384]{1,0:T(8,128)(2,1)}, bf16[1024,384]{1,0:T(8,128)(2,1)}, bf16[2,384,384]{2,1,0:T(8,128)(2,1)}, bf16[2,2,384,1024]{3,2,1,0:T(8,128)(2,1)}...) custom-call(bf16[1024,384]{1,0:T(8,128)(2,1)} %x0_ref.1, ...), custom_call_target="tpu_custom_call" | custom-call | tf_op jit(solution)/shard_map/step/pallas_call | solution.py:816
  272.7 8.9 %take.1 = (bf16[1024,384]{1,0:T(8,128)(2,1)}, bf16[1024,384]{1,0:T(8,128)(2,1)}, bf16[2,384,384]{2,1,0:T(8,128)(2,1)}, bf16[2,2,384,1024]{3,2,1,0:T(8,128)(2,1)}...) custom-call(bf16[1024,384]{1,0:T(8,128)(2,1)} %get-tuple-element.12.refs_0_, ...), custom_call_target="tpu_custom_call" | custom-call | tf_op jit(solution)/shard_map/take/pallas_call | solution.py:844

commit v13 on v11

--- a/solution.py
+++ b/solution.py
@@ -586,14 +586,16 @@
     plan(before, SLOTS + 1, [g1.follow_onward, g1.last], [g1.complete_y, now], [g1.passed_left], [g1.last_onward], [g1.complete_last, now, g1.passed_right], [g1.passed_last])
     unready = (1, 4, 6, SLOTS + 1, SLOTS + 4)
     late = ("x", "z", "u", "l")
-    plan(before, INPUTS1 + 6, [w_finish], [], [inner_onward])
+    plan(before, INPUTS1 + 7, [w_finish])
+    plan(middle, WEIGHTS0, [inner_onward])
     plan(before, WEIGHTS0, [lambda: copies.start("dense pair")], [], [inner_finish], [lambda: cross_onward("x", "z"), dense_to_x], [lambda: cross_onward("u", "l")], [dense_to_z])
     plan(middle, WEIGHTS0, [dense_sum, y_finish], [], [], [], [], [], [], [dense_to_y])
     plan(before, INPUTS0, [lambda: cross_finish(1, *late)], [], [], [], [], [lambda: final_onward(1, *late)], [], [lambda: dense_pass(1), lambda: final_finish(1, *late)])
     plan(before, INPUTS0 + 5, [w_finish], [], [inner_onward])
     for base in (WEIGHTS1, WEIGHTS0):
         plan(before, base + 3, [on_y["w"].start], [], [], [done(0), y_start, on_y["w"].onward])
-        plan(middle, base + 4, [on(0)], [], [on(1)], [on(2)])
+        plan(before, base + 4, [on(0)])
+        plan(middle, base + 6, [on(1)], [on(2)])
         plan(before, base + SLOTS, [], [done(1)], [done(2), y_onward], [on(3)], [], [], [done(3)])
         for step, q in OWN_STEPS.items():
             plan(after, base + step, [lambda q=q: reduce_start(q)])

time: 259 us -> 258 us (level)
  no operation moved by 1% of the time
where the time goes in v13:
time: 258 us; the launch traced here: 257 us
  Pallas kernels  257 us (100%)
    pallas_call x1, Pallas kernels, step(): pl.pallas_call(functools.partial(kernel, cap), grid=(STEPS,), in_specs=[h...  248 us
    pallas_call x1, Pallas kernels, take(): pl.pallas_call(functools.partial(take_kernel, count), in_specs=[hbm] * co...  8.93 us

profile of v13, /device:TPU:1, one launch (start us, length us, event | category | flops | bytes accessed | tf_op | source)
XLA Modules:
  0.0 257.3 jit_solution(16532767218125790526)
XLA Ops:
  0.6 247.8 %step.1 = (bf16[1024,384]{1,0:T(8,128)(2,1)}, bf16[1024,384]{1,0:T(8,128)(2,1)}, bf16[2,384,384]{2,1,0:T(8,128)(2,1)}, bf16[2,2,384,1024]{3,2,1,0:T(8,128)(2,1)}...) custom-call(bf16[1024,384]{1,0:T(8,128)(2,1)} %x0_ref.1, ...), custom_call_target="tpu_custom_call" | custom-call | tf_op jit(solution)/shard_map/step/pallas_call | solution.py:819
  248.4 8.9 %take.1 = (bf16[1024,384]{1,0:T(8,128)(2,1)}, bf16[1024,384]{1,0:T(8,128)(2,1)}, bf16[2,384,384]{2,1,0:T(8,128)(2,1)}, bf16[2,2,384,1024]{3,2,1,0:T(8,128)(2,1)}...) custom-call(bf16[1024,384]{1,0:T(8,128)(2,1)} %get-tuple-element.12.refs_0_, ...), custom_call_target="tpu_custom_call" | custom-call | tf_op jit(solution)/shard_map/take/pallas_call | solution.py:847
